TPU v7x, 256 devices: a whole 4x4x8 slice. The times are simulated.
256 devices in a mesh: gx: 4 (over z_lo), gy: 8 (over z_hi, x), gz: 8 (over y, core).
Axes of the slice: x: 4, y: 4, z: 8 (z_hi: 2, z_lo: 4; z = z_hi * 4 + z_lo), core: 2. Of those that a mesh axis runs over, the one named last changes fastest.
Arguments:
- volume: bfloat16 [32, 8, 128, 1024], P(None, 'gx', 'gy', 'gz'), may hold values from -6 to 6
- w_first: bfloat16 [3, 3, 3, 32, 32], replicated, may hold values from -0.21875 to 0.21875
- w_second: bfloat16 [3, 3, 3, 32, 32], replicated, may hold values from -0.21875 to 0.21875
- v_first: bfloat16 [3, 3, 3, 32, 32], replicated, may hold values from -0.21875 to 0.21875
- v_second: bfloat16 [3, 3, 3, 32, 32], replicated, may hold values from -0.21875 to 0.21875
Outputs:
- jv: bfloat16 [32, 8, 128, 1024], P(None, 'gx', 'gy', 'gz')
- gv_first: float32 [3, 3, 3, 32, 32], replicated
- gv_second: float32 [3, 3, 3, 32, 32], replicated
All inputs are finite; a program needn't handle non-finite values.
Results may differ from a plain program's by a relative error of at most 0.005.
Values may be sent and summed in bfloat16 or wider, within the bound.
No kernel may reach another device: no remote copies, remote signals or barrier semaphores. Data moves between devices by JAX's collectives and lax.ppermute only.
A program may use at most 64 MiB of HBM per device.

v0:
```python
import math

import jax
import jax.numpy as jnp
from jax import lax
from jax.sharding import PartitionSpec as P


def padded_2(cells, sides, width):
    for axis, dim in sides:
        count = lax.axis_size(axis)
        ends = count - 1
        head = lax.slice_in_dim(cells, 0, width, axis=dim)
        tail = lax.slice_in_dim(cells, cells.shape[dim] - width, cells.shape[dim], axis=dim)
        cells = jnp.concatenate(
            [
                lax.ppermute(tail, axis, [(i, (i + 1) % count) for i in range(ends)]),
                cells,
                lax.ppermute(head, axis, [((i + 1) % count, i) for i in range(ends)]),
            ],
            axis=dim,
        )
    return cells


def gelu_pair(pre):
    inner = 0.7978845608 * (pre + 0.044715 * pre * pre * pre)
    hyper = jnp.tanh(inner)
    hidden = 0.5 * pre * (1.0 + hyper)
    slope = 0.5 * (1.0 + hyper) + 0.5 * pre * (1.0 - hyper * hyper) * 0.7978845608 * (
        1.0 + 0.134145 * pre * pre
    )
    return (hidden, slope)


def stencil(padded, weight):
    depth = padded.shape[1] - 2
    height = padded.shape[2] - 2
    width = padded.shape[3] - 2
    in_chan = weight.shape[3]
    out_chan = weight.shape[4]
    summed = jnp.zeros((out_chan, depth, height, width), jnp.float32)
    for shift_x in range(3):
        for shift_y in range(3):
            stacked = jnp.concatenate(
                [
                    padded[
                        :,
                        shift_x : shift_x + depth,
                        shift_y : shift_y + height,
                        shift_z : shift_z + width,
                    ]
                    for shift_z in range(3)
                ],
                axis=0,
            )
            matrix = weight[shift_x, shift_y].reshape(3 * in_chan, out_chan)
            summed = summed + jnp.einsum(
                "kxyz,ko->oxyz", stacked, matrix, preferred_element_type=jnp.float32
            )
    return summed


def correlate(padded, target):
    depth = target.shape[1]
    height = target.shape[2]
    width = target.shape[3]
    in_chan = padded.shape[0]
    out_chan = target.shape[0]
    planes = []
    for shift_x in range(3):
        rows_y = []
        for shift_y in range(3):
            stacked = jnp.concatenate(
                [
                    padded[
                        :,
                        shift_x : shift_x + depth,
                        shift_y : shift_y + height,
                        shift_z : shift_z + width,
                    ]
                    for shift_z in range(3)
                ],
                axis=0,
            )
            product = jnp.einsum(
                "kxyz,oxyz->ko", stacked, target, preferred_element_type=jnp.float32
            )
            rows_y.append(product.reshape(3, in_chan, out_chan))
        planes.append(jnp.stack(rows_y))
    return jnp.stack(planes)


def body(volume, w_first, w_second, v_first, v_second):
    channels = volume.shape[0]
    depth = volume.shape[1]
    height = volume.shape[2]
    width = volume.shape[3]
    count_all = float(
        depth * height * width * lax.axis_size("gx") * lax.axis_size("gy") * lax.axis_size("gz")
    )
    factor = math.sqrt(27.0 * channels)
    input_pad = padded_2(volume, (("gx", 1), ("gy", 2), ("gz", 3)), 1)
    pre = stencil(input_pad, w_first)
    hidden_f, slope = gelu_pair(pre)
    hidden = hidden_f.astype(jnp.bfloat16)
    tangent = (slope * stencil(input_pad, v_first)).astype(jnp.bfloat16)
    paired = padded_2(jnp.stack([hidden, tangent]), (("gx", 2), ("gy", 3), ("gz", 4)), 1)
    hidden_pad = paired[0]
    tangent_pad = paired[1]
    jv = (stencil(tangent_pad, w_second) + stencil(hidden_pad, v_second)).astype(jnp.bfloat16)
    local_second = correlate(hidden_pad, jv)
    jv_pad = padded_2(jv, (("gx", 1), ("gy", 2), ("gz", 3)), 1)
    flipped = jnp.transpose(jnp.flip(w_second, (0, 1, 2)), (0, 1, 2, 4, 3))
    back = (slope * stencil(jv_pad, flipped)).astype(jnp.bfloat16)
    local_first = correlate(input_pad, back)
    summed_first, summed_second = lax.psum((local_first, local_second), ("gx", "gy", "gz"))
    gv_first = factor * (summed_first / count_all + 0.1 * v_first.astype(jnp.float32))
    gv_second = factor * (summed_second / count_all + 0.1 * v_second.astype(jnp.float32))
    return (jv, gv_first, gv_second)


def solution(mesh):
    in_specs = (P(None, "gx", "gy", "gz"), P(), P(), P(), P())
    out_specs = (P(None, "gx", "gy", "gz"), P(), P())
    return jax.shard_map(body, mesh=mesh, in_specs=in_specs, out_specs=out_specs, check_vma=False)
```

profile of v0, /device:TPU:1, one launch (start us, length us, event | category | flops | bytes accessed | tf_op | source)
XLA Modules:
  0.0 442.0 jit_solution(16340484945520998631)
XLA Ops:
  7.2 1.1 copy.134
  8.4 1.3 collective-permute-start.1
  9.7 5.0 %collective-permute-start = (bf16[32,1,16,128]{3,0,2,1:T(8,128)(2,1)S(1)}, bf16[32,1,16,128]{3,0,2,1:T(8,128)(2,1)S(1)}, u32[]{:S(2)}, u32[]{:S(2)}) collective-permute-start(bf16[32,1,16,128]{3,0,2,1:T(8,128)(2,1)S(1)} %get-tuple-element.141), channel_id=1, source_target_pairs={{0,64},{64,128},{128,192},{1,65},{65,129},{129,193},{2,66},{66,130... | collective-permute-start | bytes 393224 | tf_op jit(solution)/shard_map/ppermute | solution.py:17
  14.7 1.5 fusion.203
  16.8 3.1 collective-permute-start.2
  19.9 1.3 collective-permute-start.3
  21.2 0.7 fusion.204
  21.9 2.7 collective-permute-done.3
  24.9 1.1 copy.137
  26.5 5.1 %collective-permute-start.5 = (bf16[32,4,18,1]{0,1,3,2:T(4,128)(2,1)S(1)}, bf16[32,4,18,1]{0,1,3,2:T(4,128)(2,1)}, u32[]{:S(2)}, u32[]{:S(2)}) collective-permute-start(bf16[32,4,18,1]{0,1,3,2:T(4,128)(2,1)S(1)} %copy.139), channel_id=1, source_target_pairs={{1,0},{2,1},{3,2},{4,3},{5,4},{6,5},{7,6},{9,8},{10,9},{11,10},{12... | collective-permute-start | bytes 13832 | tf_op jit(solution)/shard_map/ppermute | solution.py:19
  31.6 3.1 collective-permute-start.4
  34.9 1.0 collective-permute-done.4
  36.4 1.3 copy.140
  37.6 0.8 maximum_maximum_fusion
  38.5 1.1 fusion.191
  47.4 4.1 collective-permute-start.6
  51.5 1.3 collective-permute-start.7
  52.8 0.7 fusion.202
  53.5 3.8 collective-permute-done.6
  57.3 4.2 collective-permute-done.7
  61.6 3.1 collective-permute-start.8
  64.7 1.3 collective-permute-start.9
  66.0 0.7 fusion.200
  66.7 7.5 %collective-permute-done.9 = bf16[2,32,4,1,128]{4,1,3,2,0:T(8,128)(2,1)S(1)} collective-permute-done((bf16[2,32,4,1,128]{4,1,3,2,0:T(8,128)(2,1)S(1)}, bf16[2,32,4,1,128]{4,1,3,2,0:T(8,128)(2,1)S(1)}, u32[]{:S(2)}, u32[]{:S(2)}) %collective-permute-start.9) | collective-permute-done | bytes 65568 | tf_op jit(solution)/shard_map/ppermute | solution.py:19
  74.3 0.6 copy-done.12
  75.7 1.5 copy.162
  77.3 0.9 copy.163
  78.2 3.5 collective-permute-start.11
  81.6 3.3 collective-permute-start.10
  84.9 1.6 fusion.201
  86.8 0.7 reshape.48
  87.5 0.7 reshape.47
  88.2 0.7 reshape.46
  88.9 0.7 reshape.45
  89.6 0.7 reshape.44
  90.3 0.7 reshape.43
  91.0 0.7 reshape.42
  91.7 1.0 copy.164
  92.7 1.7 copy.165
  94.4 3.8 pad_maximum_fusion
  99.0 1.2 fusion.188
  100.8 1.2 fusion.186
  113.0 2.6 collective-permute-start.12
  115.6 1.3 collective-permute-start.13
  117.4 1.3 collective-permute-done.12
  118.7 4.3 collective-permute-done.13
  123.0 9.6 %collective-permute-start.14 = (bf16[32,4,1,128]{3,0,2,1:T(8,128)(2,1)S(1)}, bf16[32,4,1,128]{3,0,2,1:T(8,128)(2,1)S(1)}, u32[]{:S(2)}, u32[]{:S(2)}) collective-permute-start(bf16[32,4,1,128]{3,0,2,1:T(8,128)(2,1)S(1)} %get-tuple-element.130), channel_id=1, source_target_pairs={{0,8},{8,16},{16,24},{24,32},{32,40},{40,48},{48,56},{1,9},{9,17},... | collective-permute-start | bytes 98312 | tf_op jit(solution)/shard_map/ppermute | solution.py:17
  132.6 1.5 collective-permute-start.15
  134.1 1.0 pad_maximum_fusion.27
  135.1 2.4 collective-permute-done.15
  139.0 3.5 collective-permute-start.17
  142.5 2.8 collective-permute-start.16
  145.5 0.9 fusion.196
  147.5 1.4 maximum_maximum_fusion.1
  149.3 0.7 fusion.185
  153.4 0.8 copy-done.11
  155.6 0.6 copy-done.18
  160.1 0.6 copy-done.34
  165.0 1.0 pad_maximum_fusion.26
  166.4 0.8 copy.199
  167.2 264.3 %all-reduce.3.cloned.1.call-done = (f32[3,3,3,32,32]{3,2,4,1,0:T(4,128)}, f32[3,3,3,32,32]{3,2,4,1,0:T(4,128)}) async-done(((f32[3,3,3,32,32]{3,2,4,1,0:T(4,128)}, f32[3,3,3,32,32]{3,2,4,1,0:T(4,128)}), (f32[3,3,3,32,32]{3,2,4,1,0:T(4,128)}, f32[3,3,3,32,32]{3,2,4,1,0:T(4,128)})) %all-reduce.3.cloned.1.call-update) | async-done | bytes 221200 | tf_op jit(solution)/shard_map/psum | solution.py:117
  431.5 1.4 add_multiply_fusion.1
  433.0 1.0 copy.200
  434.2 1.0 copy.201
  (353 shorter events, 39.6 us)
Async XLA Ops:
  7.2 9.5 %copy-start.2 = (bf16[32,2,16,128]{3,2,1,0:T(8,128)(2,1)S(1)}, bf16[32,2,16,128]{3,2,1,0:T(8,128)(2,1)}, u32[]{:S(2)}) copy-start(bf16[32,2,16,128]{3,2,1,0:T(8,128)(2,1)} %param.5) | copy-start | bytes 786436
  7.2 14.1 %copy-start.6 = (bf16[3,3,3,32,32]{4,3,2,1,0:T(8,128)(2,1)S(1)}, bf16[3,3,3,32,32]{4,3,2,1,0:T(8,128)(2,1)}, u32[]{:S(2)}) copy-start(bf16[3,3,3,32,32]{4,3,2,1,0:T(8,128)(2,1)} %param.8) | copy-start | bytes 165892
  7.2 424.4 %all-reduce.3.cloned.1.call-start = ((), (), s32[]{:S(2)}) async-start(), calls=%async_computation | async-start | bytes 2359296 | tf_op jit(solution)/shard_map/psum | solution.py:117
  8.3 38.1 %copy-start.3 = (bf16[32,2,16,128]{3,0,2,1:T(8,128)(2,1)}, bf16[32,2,16,128]{3,0,2,1:T(8,128)(2,1)S(1)}, u32[]{:S(2)}) copy-start(bf16[32,2,16,128]{3,0,2,1:T(8,128)(2,1)S(1)} %copy.134) | copy-start | bytes 786436
  8.4 8.4 %collective-permute-start.1 = (bf16[32,1,16,128]{3,0,2,1:T(8,128)(2,1)S(1)}, bf16[32,1,16,128]{3,0,2,1:T(8,128)(2,1)S(1)}, u32[]{:S(2)}, u32[]{:S(2)}) collective-permute-start(bf16[32,1,16,128]{3,0,2,1:T(8,128)(2,1)S(1)} %get-tuple-element.140), channel_id=1, source_target_pairs={{64,0},{128,64},{192,128},{65,1},{129,65},{193,129},{66,2},{130,66... | collective-permute-start | bytes 393224 | tf_op jit(solution)/shard_map/ppermute | solution.py:19
  9.7 6.9 %collective-permute-start = (bf16[32,1,16,128]{3,0,2,1:T(8,128)(2,1)S(1)}, bf16[32,1,16,128]{3,0,2,1:T(8,128)(2,1)S(1)}, u32[]{:S(2)}, u32[]{:S(2)}) collective-permute-start(bf16[32,1,16,128]{3,0,2,1:T(8,128)(2,1)S(1)} %get-tuple-element.141), channel_id=1, source_target_pairs={{0,64},{64,128},{128,192},{1,65},{65,129},{129,193},{2,66},{66,130... | collective-permute-start | bytes 393224 | tf_op jit(solution)/shard_map/ppermute | solution.py:17
  16.6 27.4 %copy-start.61 = (bf16[32,1,16,128]{3,0,2,1:T(8,128)(2,1)}, bf16[32,1,16,128]{3,0,2,1:T(8,128)(2,1)S(1)}, u32[]{:S(2)}) copy-start(bf16[32,1,16,128]{3,0,2,1:T(8,128)(2,1)S(1)} %collective-permute-done) | copy-start | bytes 393220
  16.8 29.7 %copy-start.59 = (bf16[32,1,16,128]{3,0,2,1:T(8,128)(2,1)}, bf16[32,1,16,128]{3,0,2,1:T(8,128)(2,1)S(1)}, u32[]{:S(2)}) copy-start(bf16[32,1,16,128]{3,0,2,1:T(8,128)(2,1)S(1)} %collective-permute-done.1) | copy-start | bytes 393220
  16.8 5.1 %collective-permute-start.2 = (bf16[32,4,1,128]{3,0,2,1:T(8,128)(2,1)S(1)}, bf16[32,4,1,128]{3,0,2,1:T(8,128)(2,1)S(1)}, u32[]{:S(2)}, u32[]{:S(2)}) collective-permute-start(bf16[32,4,1,128]{3,0,2,1:T(8,128)(2,1)S(1)} %get-tuple-element.136), channel_id=1, source_target_pairs={{0,8},{8,16},{16,24},{24,32},{32,40},{40,48},{48,56},{1,9},{9,17},... | collective-permute-start | bytes 98312 | tf_op jit(solution)/shard_map/ppermute | solution.py:17
  19.9 4.7 %collective-permute-start.3 = (bf16[32,4,1,128]{3,0,2,1:T(8,128)(2,1)S(1)}, bf16[32,4,1,128]{3,0,2,1:T(8,128)(2,1)S(1)}, u32[]{:S(2)}, u32[]{:S(2)}) collective-permute-start(bf16[32,4,1,128]{3,0,2,1:T(8,128)(2,1)S(1)} %get-tuple-element.137), channel_id=1, source_target_pairs={{8,0},{16,8},{24,16},{32,24},{40,32},{48,40},{56,48},{9,1},{17,9},... | collective-permute-start | bytes 98312 | tf_op jit(solution)/shard_map/ppermute | solution.py:19
  26.5 9.8 %collective-permute-start.5 = (bf16[32,4,18,1]{0,1,3,2:T(4,128)(2,1)S(1)}, bf16[32,4,18,1]{0,1,3,2:T(4,128)(2,1)}, u32[]{:S(2)}, u32[]{:S(2)}) collective-permute-start(bf16[32,4,18,1]{0,1,3,2:T(4,128)(2,1)S(1)} %copy.139), channel_id=1, source_target_pairs={{1,0},{2,1},{3,2},{4,3},{5,4},{6,5},{7,6},{9,8},{10,9},{11,10},{12... | collective-permute-start | bytes 13832 | tf_op jit(solution)/shard_map/ppermute | solution.py:19
  31.6 4.2 collective-permute-start.4
  34.8 8.7 %copy-start.13 = (bf16[32,2,16,128]{3,0,2,1:T(8,128)(2,1)}, bf16[32,2,16,128]{3,0,2,1:T(8,128)(2,1)S(1)}, u32[]{:S(2)}) copy-start(bf16[32,2,16,128]{3,0,2,1:T(8,128)(2,1)S(1)} %get-tuple-element.134) | copy-start | bytes 786436
  34.8 9.5 %copy-start.15 = (bf16[32,2,16,128]{3,0,2,1:T(8,128)(2,1)}, bf16[32,2,16,128]{3,0,2,1:T(8,128)(2,1)S(1)}, u32[]{:S(2)}) copy-start(bf16[32,2,16,128]{3,0,2,1:T(8,128)(2,1)S(1)} %get-tuple-element.125) | copy-start | bytes 786436
  34.8 10.2 %copy-start.17 = (bf16[32,2,16,128]{3,0,2,1:T(8,128)(2,1)}, bf16[32,2,16,128]{3,0,2,1:T(8,128)(2,1)S(1)}, u32[]{:S(2)}) copy-start(bf16[32,2,16,128]{3,0,2,1:T(8,128)(2,1)S(1)} %get-tuple-element.135) | copy-start | bytes 786436
  34.9 10.9 %copy-start.23 = (bf16[32,2,16,128]{3,0,2,1:T(8,128)(2,1)}, bf16[32,2,16,128]{3,0,2,1:T(8,128)(2,1)S(1)}, u32[]{:S(2)}) copy-start(bf16[32,2,16,128]{3,0,2,1:T(8,128)(2,1)S(1)} %get-tuple-element.124) | copy-start | bytes 786436
  38.5 1.3 copy-start.95
  39.6 4.0 copy-start.41
  39.6 4.0 copy-start.43
  39.6 4.5 %copy-start.25 = (bf16[32,2,16,128]{3,0,2,1:T(8,128)(2,1)}, bf16[32,2,16,128]{3,0,2,1:T(8,128)(2,1)S(1)}, u32[]{:S(2)}) copy-start(bf16[32,2,16,128]{3,0,2,1:T(8,128)(2,1)S(1)} %get-tuple-element.97) | copy-start | bytes 786436
  39.6 4.5 %copy-start.27 = (bf16[32,2,16,128]{3,0,2,1:T(8,128)(2,1)}, bf16[32,2,16,128]{3,0,2,1:T(8,128)(2,1)S(1)}, u32[]{:S(2)}) copy-start(bf16[32,2,16,128]{3,0,2,1:T(8,128)(2,1)S(1)} %get-tuple-element.188) | copy-start | bytes 786436
  39.6 4.8 %copy-start.45 = (bf16[32,2,16,128]{3,0,2,1:T(8,128)(2,1)}, bf16[32,2,16,128]{3,0,2,1:T(8,128)(2,1)S(1)}, u32[]{:S(2)}) copy-start(bf16[32,2,16,128]{3,0,2,1:T(8,128)(2,1)S(1)} %get-tuple-element.96) | copy-start | bytes 786436
  39.6 4.8 %copy-start.47 = (bf16[32,2,16,128]{3,0,2,1:T(8,128)(2,1)}, bf16[32,2,16,128]{3,0,2,1:T(8,128)(2,1)S(1)}, u32[]{:S(2)}) copy-start(bf16[32,2,16,128]{3,0,2,1:T(8,128)(2,1)S(1)} %get-tuple-element.189) | copy-start | bytes 786436
  39.6 5.5 %copy-start.49 = (bf16[32,2,16,128]{3,0,2,1:T(8,128)(2,1)}, bf16[32,2,16,128]{3,0,2,1:T(8,128)(2,1)S(1)}, u32[]{:S(2)}) copy-start(bf16[32,2,16,128]{3,0,2,1:T(8,128)(2,1)S(1)} %get-tuple-element.95) | copy-start | bytes 786436
  39.6 5.5 %copy-start.51 = (bf16[32,2,16,128]{3,0,2,1:T(8,128)(2,1)}, bf16[32,2,16,128]{3,0,2,1:T(8,128)(2,1)S(1)}, u32[]{:S(2)}) copy-start(bf16[32,2,16,128]{3,0,2,1:T(8,128)(2,1)S(1)} %get-tuple-element.190) | copy-start | bytes 786436
  39.6 5.8 %copy-start.37 = (bf16[32,2,16,128]{3,0,2,1:T(8,128)(2,1)}, bf16[32,2,16,128]{3,0,2,1:T(8,128)(2,1)S(1)}, u32[]{:S(2)}) copy-start(bf16[32,2,16,128]{3,0,2,1:T(8,128)(2,1)S(1)} %get-tuple-element.94) | copy-start | bytes 786436
  39.6 5.8 %copy-start.39 = (bf16[32,2,16,128]{3,0,2,1:T(8,128)(2,1)}, bf16[32,2,16,128]{3,0,2,1:T(8,128)(2,1)S(1)}, u32[]{:S(2)}) copy-start(bf16[32,2,16,128]{3,0,2,1:T(8,128)(2,1)S(1)} %get-tuple-element.191) | copy-start | bytes 786436
  39.7 6.2 %copy-start.53 = (bf16[32,2,16,128]{3,0,2,1:T(8,128)(2,1)}, bf16[32,2,16,128]{3,0,2,1:T(8,128)(2,1)S(1)}, u32[]{:S(2)}) copy-start(bf16[32,2,16,128]{3,0,2,1:T(8,128)(2,1)S(1)} %get-tuple-element.93) | copy-start | bytes 786436
  39.7 6.2 %copy-start.55 = (bf16[32,2,16,128]{3,0,2,1:T(8,128)(2,1)}, bf16[32,2,16,128]{3,0,2,1:T(8,128)(2,1)S(1)}, u32[]{:S(2)}) copy-start(bf16[32,2,16,128]{3,0,2,1:T(8,128)(2,1)S(1)} %get-tuple-element.192) | copy-start | bytes 786436
  39.7 6.5 %copy-start.33 = (bf16[32,2,16,128]{3,0,2,1:T(8,128)(2,1)}, bf16[32,2,16,128]{3,0,2,1:T(8,128)(2,1)S(1)}, u32[]{:S(2)}) copy-start(bf16[32,2,16,128]{3,0,2,1:T(8,128)(2,1)S(1)} %get-tuple-element.92) | copy-start | bytes 786436
  39.7 6.5 %copy-start.35 = (bf16[32,2,16,128]{3,0,2,1:T(8,128)(2,1)}, bf16[32,2,16,128]{3,0,2,1:T(8,128)(2,1)S(1)}, u32[]{:S(2)}) copy-start(bf16[32,2,16,128]{3,0,2,1:T(8,128)(2,1)S(1)} %get-tuple-element.193) | copy-start | bytes 786436
  39.7 6.8 %copy-start.19 = (bf16[32,2,16,128]{3,0,2,1:T(8,128)(2,1)}, bf16[32,2,16,128]{3,0,2,1:T(8,128)(2,1)S(1)}, u32[]{:S(2)}) copy-start(bf16[32,2,16,128]{3,0,2,1:T(8,128)(2,1)S(1)} %get-tuple-element.91) | copy-start | bytes 786436
  39.7 6.8 %copy-start.21 = (bf16[32,2,16,128]{3,0,2,1:T(8,128)(2,1)}, bf16[32,2,16,128]{3,0,2,1:T(8,128)(2,1)S(1)}, u32[]{:S(2)}) copy-start(bf16[32,2,16,128]{3,0,2,1:T(8,128)(2,1)S(1)} %get-tuple-element.194) | copy-start | bytes 786436
  39.7 7.0 %copy-start.29 = (bf16[32,2,16,128]{3,0,2,1:T(8,128)(2,1)}, bf16[32,2,16,128]{3,0,2,1:T(8,128)(2,1)S(1)}, u32[]{:S(2)}) copy-start(bf16[32,2,16,128]{3,0,2,1:T(8,128)(2,1)S(1)} %get-tuple-element.90) | copy-start | bytes 786436
  39.7 7.0 %copy-start.31 = (bf16[32,2,16,128]{3,0,2,1:T(8,128)(2,1)}, bf16[32,2,16,128]{3,0,2,1:T(8,128)(2,1)S(1)}, u32[]{:S(2)}) copy-start(bf16[32,2,16,128]{3,0,2,1:T(8,128)(2,1)S(1)} %get-tuple-element.195) | copy-start | bytes 786436
  43.3 3.5 copy-start.10
  46.8 6.0 %copy-start.5 = (bf16[3,3,3,32,32]{4,3,2,1,0:T(8,128)(2,1)S(1)}, bf16[3,3,3,32,32]{4,3,2,1,0:T(8,128)(2,1)}, u32[]{:S(2)}) copy-start(bf16[3,3,3,32,32]{4,3,2,1,0:T(8,128)(2,1)} %param.7) | copy-start | bytes 165892
  47.4 9.9 %collective-permute-start.6 = (bf16[2,32,1,16,128]{4,1,3,2,0:T(8,128)(2,1)S(1)}, bf16[2,32,1,16,128]{4,1,3,2,0:T(8,128)(2,1)S(1)}, u32[]{:S(2)}, u32[]{:S(2)}) collective-permute-start(bf16[2,32,1,16,128]{4,1,3,2,0:T(8,128)(2,1)S(1)} %get-tuple-element.132), channel_id=1, source_target_pairs={{0,64},{64,128},{128,192},{1,65},{65,129},{129,193},{2,66},{66,130... | collective-permute-start | bytes 786440 | tf_op jit(solution)/shard_map/ppermute | solution.py:17
  51.5 10.1 %collective-permute-start.7 = (bf16[2,32,1,16,128]{4,1,3,2,0:T(8,128)(2,1)S(1)}, bf16[2,32,1,16,128]{4,1,3,2,0:T(8,128)(2,1)S(1)}, u32[]{:S(2)}, u32[]{:S(2)}) collective-permute-start(bf16[2,32,1,16,128]{4,1,3,2,0:T(8,128)(2,1)S(1)} %get-tuple-element.133), channel_id=1, source_target_pairs={{64,0},{128,64},{192,128},{65,1},{129,65},{193,129},{66,2},{130,66... | collective-permute-start | bytes 786440 | tf_op jit(solution)/shard_map/ppermute | solution.py:19
  57.3 17.0 %copy-start = (bf16[2,32,1,16,128]{4,1,3,2,0:T(8,128)(2,1)}, bf16[2,32,1,16,128]{4,1,3,2,0:T(8,128)(2,1)S(1)}, u32[]{:S(2)}) copy-start(bf16[2,32,1,16,128]{4,1,3,2,0:T(8,128)(2,1)S(1)} %collective-permute-done.6) | copy-start | bytes 786436
  61.5 12.7 %copy-start.1 = (bf16[2,32,1,16,128]{4,1,3,2,0:T(8,128)(2,1)}, bf16[2,32,1,16,128]{4,1,3,2,0:T(8,128)(2,1)S(1)}, u32[]{:S(2)}) copy-start(bf16[2,32,1,16,128]{4,1,3,2,0:T(8,128)(2,1)S(1)} %collective-permute-done.7) | copy-start | bytes 786436
  61.6 5.2 %collective-permute-start.8 = (bf16[2,32,4,1,128]{4,1,3,2,0:T(8,128)(2,1)S(1)}, bf16[2,32,4,1,128]{4,1,3,2,0:T(8,128)(2,1)S(1)}, u32[]{:S(2)}, u32[]{:S(2)}) collective-permute-start(bf16[2,32,4,1,128]{4,1,3,2,0:T(8,128)(2,1)S(1)} %get-tuple-element.108), channel_id=1, source_target_pairs={{0,8},{8,16},{16,24},{24,32},{32,40},{40,48},{48,56},{1,9},{9,17},... | collective-permute-start | bytes 196616 | tf_op jit(solution)/shard_map/ppermute | solution.py:17
  64.7 9.5 %collective-permute-start.9 = (bf16[2,32,4,1,128]{4,1,3,2,0:T(8,128)(2,1)S(1)}, bf16[2,32,4,1,128]{4,1,3,2,0:T(8,128)(2,1)S(1)}, u32[]{:S(2)}, u32[]{:S(2)}) collective-permute-start(bf16[2,32,4,1,128]{4,1,3,2,0:T(8,128)(2,1)S(1)} %get-tuple-element.109), channel_id=1, source_target_pairs={{8,0},{16,8},{24,16},{32,24},{40,32},{48,40},{56,48},{9,1},{17,9},... | collective-permute-start | bytes 196616 | tf_op jit(solution)/shard_map/ppermute | solution.py:19
  77.2 9.3 %copy-start.72 = (bf16[1,1,3,32,32]{3,4,2,1,0:T(8,128)(2,1)S(1)}, bf16[1,1,3,32,32]{3,4,2,1,0:T(8,128)(2,1)}, u32[]{:S(2)}) copy-start(bf16[1,1,3,32,32]{3,4,2,1,0:T(8,128)(2,1)} %get-tuple-element.142) | copy-start | bytes 18436
  77.2 9.4 %copy-start.71 = (bf16[1,1,3,32,32]{3,4,2,1,0:T(8,128)(2,1)S(1)}, bf16[1,1,3,32,32]{3,4,2,1,0:T(8,128)(2,1)}, u32[]{:S(2)}) copy-start(bf16[1,1,3,32,32]{3,4,2,1,0:T(8,128)(2,1)} %get-tuple-element.143) | copy-start | bytes 18436
  77.2 9.6 %copy-start.70 = (bf16[1,1,3,32,32]{3,4,2,1,0:T(8,128)(2,1)S(1)}, bf16[1,1,3,32,32]{3,4,2,1,0:T(8,128)(2,1)}, u32[]{:S(2)}) copy-start(bf16[1,1,3,32,32]{3,4,2,1,0:T(8,128)(2,1)} %get-tuple-element.144) | copy-start | bytes 18436
  77.2 10.3 %copy-start.69 = (bf16[1,1,3,32,32]{3,4,2,1,0:T(8,128)(2,1)S(1)}, bf16[1,1,3,32,32]{3,4,2,1,0:T(8,128)(2,1)}, u32[]{:S(2)}) copy-start(bf16[1,1,3,32,32]{3,4,2,1,0:T(8,128)(2,1)} %get-tuple-element.145) | copy-start | bytes 18436
  77.2 11.0 %copy-start.68 = (bf16[1,1,3,32,32]{3,4,2,1,0:T(8,128)(2,1)S(1)}, bf16[1,1,3,32,32]{3,4,2,1,0:T(8,128)(2,1)}, u32[]{:S(2)}) copy-start(bf16[1,1,3,32,32]{3,4,2,1,0:T(8,128)(2,1)} %get-tuple-element.146) | copy-start | bytes 18436
  77.2 11.7 %copy-start.67 = (bf16[1,1,3,32,32]{3,4,2,1,0:T(8,128)(2,1)S(1)}, bf16[1,1,3,32,32]{3,4,2,1,0:T(8,128)(2,1)}, u32[]{:S(2)}) copy-start(bf16[1,1,3,32,32]{3,4,2,1,0:T(8,128)(2,1)} %get-tuple-element.147) | copy-start | bytes 18436
  77.2 12.4 %copy-start.66 = (bf16[1,1,3,32,32]{3,4,2,1,0:T(8,128)(2,1)S(1)}, bf16[1,1,3,32,32]{3,4,2,1,0:T(8,128)(2,1)}, u32[]{:S(2)}) copy-start(bf16[1,1,3,32,32]{3,4,2,1,0:T(8,128)(2,1)} %get-tuple-element.148) | copy-start | bytes 18436
  77.2 13.1 %copy-start.65 = (bf16[1,1,3,32,32]{3,4,2,1,0:T(8,128)(2,1)S(1)}, bf16[1,1,3,32,32]{3,4,2,1,0:T(8,128)(2,1)}, u32[]{:S(2)}) copy-start(bf16[1,1,3,32,32]{3,4,2,1,0:T(8,128)(2,1)} %get-tuple-element.149) | copy-start | bytes 18436
  77.3 13.8 %copy-start.64 = (bf16[1,1,3,32,32]{3,4,2,1,0:T(8,128)(2,1)S(1)}, bf16[1,1,3,32,32]{3,4,2,1,0:T(8,128)(2,1)}, u32[]{:S(2)}) copy-start(bf16[1,1,3,32,32]{3,4,2,1,0:T(8,128)(2,1)} %get-tuple-element.150) | copy-start | bytes 18436
  78.2 14.5 %collective-permute-start.11 = (bf16[2,32,4,18,1]{1,2,4,3,0:T(4,128)(2,1)S(1)}, bf16[2,32,4,18,1]{1,2,4,3,0:T(4,128)(2,1)}, u32[]{:S(2)}, u32[]{:S(2)}) collective-permute-start(bf16[2,32,4,18,1]{1,2,4,3,0:T(4,128)(2,1)S(1)} %copy.163), channel_id=1, source_target_pairs={{1,0},{2,1},{3,2},{4,3},{5,4},{6,5},{7,6},{9,8},{10,9},{11,10},{12... | collective-permute-start | bytes 27656 | tf_op jit(solution)/shard_map/ppermute | solution.py:19
  81.6 10.1 %collective-permute-start.10 = (bf16[2,32,4,18,1]{1,2,4,3,0:T(4,128)(2,1)}, bf16[2,32,4,18,1]{1,2,4,3,0:T(4,128)(2,1)S(1)}, u32[]{:S(2)}, u32[]{:S(2)}) collective-permute-start(bf16[2,32,4,18,1]{1,2,4,3,0:T(4,128)(2,1)} %copy.162), channel_id=1, source_target_pairs={{0,1},{1,2},{2,3},{3,4},{4,5},{5,6},{6,7},{8,9},{9,10},{10,11},{11... | collective-permute-start | bytes 27656 | tf_op jit(solution)/shard_map/ppermute | solution.py:17
  100.7 1.2 copy-start.89
  113.0 5.7 %collective-permute-start.12 = (bf16[32,1,16,128]{3,0,2,1:T(8,128)(2,1)S(1)}, bf16[32,1,16,128]{3,0,2,1:T(8,128)(2,1)S(1)}, u32[]{:S(2)}, u32[]{:S(2)}) collective-permute-start(bf16[32,1,16,128]{3,0,2,1:T(8,128)(2,1)S(1)} %get-tuple-element.138), channel_id=1, source_target_pairs={{0,64},{64,128},{128,192},{1,65},{65,129},{129,193},{2,66},{66,130... | collective-permute-start | bytes 393224 | tf_op jit(solution)/shard_map/ppermute | solution.py:17
  115.6 7.3 %collective-permute-start.13 = (bf16[32,1,16,128]{3,0,2,1:T(8,128)(2,1)S(1)}, bf16[32,1,16,128]{3,0,2,1:T(8,128)(2,1)S(1)}, u32[]{:S(2)}, u32[]{:S(2)}) collective-permute-start(bf16[32,1,16,128]{3,0,2,1:T(8,128)(2,1)S(1)} %get-tuple-element.139), channel_id=1, source_target_pairs={{64,0},{128,64},{192,128},{65,1},{129,65},{193,129},{66,2},{130,66... | collective-permute-start | bytes 393224 | tf_op jit(solution)/shard_map/ppermute | solution.py:19
  123.0 12.2 %collective-permute-start.14 = (bf16[32,4,1,128]{3,0,2,1:T(8,128)(2,1)S(1)}, bf16[32,4,1,128]{3,0,2,1:T(8,128)(2,1)S(1)}, u32[]{:S(2)}, u32[]{:S(2)}) collective-permute-start(bf16[32,4,1,128]{3,0,2,1:T(8,128)(2,1)S(1)} %get-tuple-element.130), channel_id=1, source_target_pairs={{0,8},{8,16},{16,24},{24,32},{32,40},{40,48},{48,56},{1,9},{9,17},... | collective-permute-start | bytes 98312 | tf_op jit(solution)/shard_map/ppermute | solution.py:17
  132.6 5.0 %collective-permute-start.15 = (bf16[32,4,1,128]{3,0,2,1:T(8,128)(2,1)S(1)}, bf16[32,4,1,128]{3,0,2,1:T(8,128)(2,1)S(1)}, u32[]{:S(2)}, u32[]{:S(2)}) collective-permute-start(bf16[32,4,1,128]{3,0,2,1:T(8,128)(2,1)S(1)} %get-tuple-element.131), channel_id=1, source_target_pairs={{8,0},{16,8},{24,16},{32,24},{40,32},{48,40},{56,48},{9,1},{17,9},... | collective-permute-start | bytes 98312 | tf_op jit(solution)/shard_map/ppermute | solution.py:19
  139.0 8.0 %collective-permute-start.17 = (bf16[32,4,18,1]{0,1,3,2:T(4,128)(2,1)S(1)}, bf16[32,4,18,1]{0,1,3,2:T(4,128)(2,1)S(1)}, u32[]{:S(2)}, u32[]{:S(2)}) collective-permute-start(bf16[32,4,18,1]{0,1,3,2:T(4,128)(2,1)S(1)} %copy.186), channel_id=1, source_target_pairs={{1,0},{2,1},{3,2},{4,3},{5,4},{6,5},{7,6},{9,8},{10,9},{11,10},{12... | collective-permute-start | bytes 13832 | tf_op jit(solution)/shard_map/ppermute | solution.py:19
  142.5 3.9 collective-permute-start.16
  164.8 1.1 copy-start.7
  164.9 1.3 copy-start.8
  431.5 2.4 copy-start.9
  (62 other events, 54.3 us)
Sparse Core Ops, SparseCore 0:
  166.1 265.4 all-reduce.2
where the time goes:
time: 446 us; the launch traced here: 442 us
  waiting for transfers between devices  292 us (65%)
  starting transfers between devices  56.9 us (13%)
  local copies, waits for them, and re-layouts  47.2 us (11%)
  matrix products  19.3 us (4%)
  between operations  15.7 us (4%)
  other arithmetic  10.9 us (2%)
    psum x1, waiting for transfers between devices, body(): lax.psum((local_first, local_second), ('gx', 'gy', 'gz'))  264 us
    ppermute x9, starting transfers between devices, padded_2(): lax.ppermute(tail, axis, [(i, (i + 1) % count) for i in range(ends)])  36.8 us
    ppermute x9, waiting for transfers between devices, padded_2(): lax.ppermute(head, axis, [((i + 1) % count, i) for i in range(ends)])  21.2 us
    ppermute x9, starting transfers between devices, padded_2(): lax.ppermute(head, axis, [((i + 1) % count, i) for i in range(ends)])  20 us
    unnamed x222, local copies, waits for them, and re-layouts  16.6 us
    dot_general x45, matrix products, stencil(): jnp.einsum('kxyz,ko->oxyz', stacked, matrix, preferred_element_type=jnp.f...  12.7 us
  transfers between devices with their start and end apart: 19, of which 10 were waited for; matrix products, arithmetic and copies ran while one was open for 4% of the time, Pallas kernels for 0%

commit v1 on v0

v1 whole, which is shorter than its diff:
```python
import math

import jax
import jax.numpy as jnp
from jax import lax
from jax.experimental import pallas as pl
from jax.experimental.pallas import tpu as pltpu
from jax.sharding import PartitionSpec as P

PITCH = 136
LA = 1408
LH = 1152
LJ = 896
LB = 640
F32 = jnp.float32
BF16 = jnp.bfloat16
AXES = ("gx", "gy", "gz")


def lanes_of(shape):
    return lax.broadcasted_iota(jnp.int32, shape, len(shape) - 1)


def assemble(planes, main_ref, up_ref, down_ref, field_ref, strip_ref):
    lane = lanes_of((32, 128))

    def plane(x, carry):
        rolled = []
        for row in range(10):
            if row < 3:
                tile = up_ref[x, row]
            elif row < 7:
                tile = main_ref[x, row - 3]
            else:
                tile = down_ref[x, row - 7]
            rolled.append(pltpu.roll(tile.astype(F32), 8 * row + 3, 1))
        strip = jnp.zeros((32, 128), F32)
        for row in range(10):
            strip = jnp.where((lane >= 8 * row) & (lane < 8 * row + 6), rolled[row], strip)
        strip_ref[x] = strip.astype(BF16)
        for tile in range(11):
            value = jnp.zeros((32, 128), F32)
            if tile < 10:
                value = jnp.where(lane >= 8 * tile + 3, rolled[tile], value)
            if tile > 0:
                value = jnp.where(lane < 8 * tile - 5, rolled[tile - 1], value)
            field_ref[x, :, 128 * tile : 128 * tile + 128] = value.astype(BF16)
        return carry

    lax.fori_loop(0, planes, plane, 0)


def gelu_pair(pre):
    inner = 0.7978845608 * (pre + 0.044715 * pre * pre * pre)
    hyper = jnp.tanh(inner)
    hidden = 0.5 * pre * (1.0 + hyper)
    slope = 0.5 * (1.0 + hyper) + 0.5 * pre * (1.0 - hyper * hyper) * 0.7978845608 * (
        1.0 + 0.134145 * pre * pre
    )
    return hidden, slope


def back_by(value, shift):
    if shift == 0:
        return value
    return pltpu.roll(value, value.shape[1] - shift, 1)


def fold(product):
    return product[0:32] + back_by(product[32:64], 1) + back_by(product[64:96], 2)


def spread(ref, x, value, width):
    for shift in range(3):
        ref[pl.ds(pl.multiple_of((x + 1) * 96 + 32 * shift, 32), 32), :] = back_by(
            value, PITCH * shift
        )[:, :width].astype(BF16)


def layers(
    planes,
    field_ref,
    left_ref,
    right_ref,
    weight_ref,
    mask_ref,
    jv_ref,
    sums_ref,
    p_vol,
    p_hid,
    p_tan,
    p_jv,
    slopes,
):
    for ref, width in ((p_vol, LH), (p_hid, LJ), (p_tan, LJ), (p_jv, LB)):
        blank = jnp.zeros((96, width), BF16)
        ref[0:96, :] = blank
        ref[96 * (planes + 1) : 96 * (planes + 2), :] = blank
    sums_ref[...] = jnp.zeros_like(sums_ref)
    lane = lanes_of((32, 128))

    def window(x):
        return pl.ds(pl.multiple_of(x * 96, 32), 288)

    def fill(x, carry):
        left = left_ref[x].astype(F32)
        right = right_ref[x].astype(F32)
        tiles = []
        for tile in range(11):
            value = field_ref[x, :, 128 * tile : 128 * tile + 128].astype(F32)
            if tile < 10:
                value = jnp.where((lane >= 8 * tile) & (lane < 8 * tile + 3), left, value)
            if tile > 0:
                value = jnp.where((lane >= 8 * tile - 5) & (lane < 8 * tile - 2), right, value)
            tiles.append(value)
        spread(p_vol, x, jnp.concatenate(tiles, axis=1), LH)
        return carry

    lax.fori_loop(0, planes, fill, 0)

    def first(x, carry):
        product = jnp.dot(weight_ref[0:192, :], p_vol[window(x), :], preferred_element_type=F32)
        inside = mask_ref[0:1, :LH] > 0.0
        hidden, slope = gelu_pair(fold(product[0:96]))
        tangent = slope * fold(product[96:192])
        slopes[x] = back_by(slope, 2 * PITCH + 2)[:, :LB]
        spread(p_hid, x, jnp.where(inside, hidden, 0.0), LJ)
        spread(p_tan, x, jnp.where(inside, tangent, 0.0), LJ)
        return carry

    lax.fori_loop(0, planes, first, 0)

    def second(x, carry):
        near = p_hid[window(x), :]
        product = jnp.dot(weight_ref[192:288, :], p_tan[window(x), :], preferred_element_type=F32)
        product = product + jnp.dot(weight_ref[288:384, :], near, preferred_element_type=F32)
        jv = fold(product).astype(BF16).astype(F32)
        jv = jnp.where(mask_ref[1:2, :LJ] > 0.0, jv, 0.0)
        spread(p_jv, x, jv, LB)
        for row in range(4):
            pair = jv[:, 128 * (row + 1) : 128 * (row + 3)]
            jv_ref[x, row] = back_by(pair, 8 * row + 9)[:, :128].astype(BF16)
        own = jnp.where(mask_ref[2:3, :LJ] > 0.0, jv, 0.0)
        moved = jnp.concatenate([own, pltpu.roll(own, 1, 1), pltpu.roll(own, 2, 1)], axis=0)
        sums_ref[0] += lax.dot_general(
            near[:, 128:768],
            moved[:, 128:768].astype(BF16),
            (((1,), (1,)), ((), ())),
            preferred_element_type=F32,
        )
        return carry

    lax.fori_loop(0, planes, second, 0)

    def third(x, carry):
        product = jnp.dot(weight_ref[384:480, :], p_jv[window(x), :], preferred_element_type=F32)
        back = slopes[x] * fold(product)
        back = jnp.where(mask_ref[3:4, :LB] > 0.0, back, 0.0).astype(BF16).astype(F32)
        moved = jnp.concatenate([pltpu.roll(back, 18 + k, 1) for k in range(3)], axis=0)
        sums_ref[1] += lax.dot_general(
            p_vol[window(x), 256:896],
            moved.astype(BF16),
            (((1,), (1,)), ((), ())),
            preferred_element_type=F32,
        )
        return carry

    lax.fori_loop(0, planes, third, 0)


def cell_masks(row0, col0, height, width):
    q = jnp.arange(LH, dtype=jnp.int32)
    row, col = q // PITCH, q % PITCH

    def inside(rows, cols, margin):
        y = row0 + row - margin
        z = col0 + col - margin
        return (row < rows) & (col < cols) & (y >= 0) & (y < height) & (z >= 0) & (z < width)

    own_jv = (row >= 1) & (row < 5) & (col >= 1) & (col < 129)
    own_back = (row < 4) & (col < 128)
    none = jnp.zeros_like(own_jv)
    rows = [inside(8, 132, 2), inside(6, 130, 1), own_jv, own_back, none, none, none, none]
    return jnp.stack(rows).astype(F32)


def filters(w_first, v_first, w_second, v_second):
    flipped = jnp.transpose(jnp.flip(w_second, (0, 1, 2)), (0, 1, 2, 4, 3))
    stacked = jnp.stack([w_first, v_first, w_second, v_second, flipped])
    return jnp.transpose(stacked, (0, 3, 5, 1, 2, 4)).reshape(480, 288)


def total(sums):
    count = lax.axis_size(AXES)
    parts = sums.reshape(count, -1)
    mine = jnp.sum(lax.all_to_all(parts, AXES, 0, 0), axis=0).astype(BF16)
    every = jnp.broadcast_to(mine[None], (count, mine.shape[0]))
    return lax.all_to_all(every, AXES, 0, 0).astype(F32).reshape(sums.shape)


def body(volume, w_first, w_second, v_first, v_second):
    channels, depth, height, width = volume.shape
    n_gx, n_gy, n_gz = lax.axis_size("gx"), lax.axis_size("gy"), lax.axis_size("gz")
    planes = depth * n_gx
    rows = height // n_gx
    count_all = float(planes * height * n_gy * width * n_gz)
    factor = math.sqrt(27.0 * channels)

    split = jnp.transpose(volume.reshape(channels, depth, n_gx, rows, width), (2, 1, 3, 0, 4))
    main = lax.all_to_all(split, "gx", 0, 0).reshape(planes, rows, channels, width)

    def device(block):
        return (block % n_gx) * n_gy + block // n_gx

    blocks = n_gx * n_gy
    onward = [(device(i), device(i + 1)) for i in range(blocks - 1)]
    backward = [(b, a) for a, b in onward]
    up = lax.ppermute(main[:, 1:], ("gx", "gy"), onward)
    down = lax.ppermute(main[:, :3], ("gx", "gy"), backward)

    vmem = pl.BlockSpec(memory_space=pltpu.VMEM)
    field, strip = pl.pallas_call(
        lambda *refs: assemble(planes, *refs),
        out_shape=(
            jax.ShapeDtypeStruct((planes, channels, LA), BF16),
            jax.ShapeDtypeStruct((planes, channels, 128), BF16),
        ),
        in_specs=[vmem] * 3,
        out_specs=(vmem, vmem),
        name="assemble",
    )(main, up, down)

    ends = [(i, i + 1) for i in range(n_gz - 1)]
    left = lax.ppermute(strip, "gz", ends)
    right = lax.ppermute(strip, "gz", [(b, a) for a, b in ends])

    row0 = (lax.axis_index("gy") * n_gx + lax.axis_index("gx")) * rows
    col0 = lax.axis_index("gz") * width
    masks = cell_masks(row0, col0, height * n_gy, width * n_gz)
    weights = filters(w_first, v_first, w_second, v_second)

    jv, sums = pl.pallas_call(
        lambda *refs: layers(planes, *refs),
        out_shape=(
            jax.ShapeDtypeStruct((planes, rows, channels, width), BF16),
            jax.ShapeDtypeStruct((2, 288, 96), F32),
        ),
        in_specs=[vmem] * 5,
        out_specs=(vmem, vmem),
        scratch_shapes=[
            pltpu.VMEM((96 * (planes + 2), LH), BF16),
            pltpu.VMEM((96 * (planes + 2), LJ), BF16),
            pltpu.VMEM((96 * (planes + 2), LJ), BF16),
            pltpu.VMEM((96 * (planes + 2), LB), BF16),
            pltpu.VMEM((planes, channels, LB), F32),
        ],
        name="layers",
    )(field, left, right, weights, masks)

    home = lax.all_to_all(jv.reshape(n_gx, depth, rows, channels, width), "gx", 0, 0)
    out = jnp.transpose(home, (3, 1, 0, 2, 4)).reshape(channels, depth, height, width)

    summed = total(sums).reshape(2, 3, 3, channels, 3, channels)
    summed_second, summed_first = jnp.transpose(summed, (0, 1, 2, 4, 3, 5))
    gv_first = factor * (summed_first / count_all + 0.1 * v_first.astype(F32))
    gv_second = factor * (summed_second / count_all + 0.1 * v_second.astype(F32))
    return (out, gv_first, gv_second)


def solution(mesh):
    in_specs = (P(None, "gx", "gy", "gz"), P(), P(), P(), P())
    out_specs = (P(None, "gx", "gy", "gz"), P(), P())
    return jax.shard_map(body, mesh=mesh, in_specs=in_specs, out_specs=out_specs, check_vma=False)
```

time: 446 us -> 135 us (0.30)
  waiting for transfers between devices: 292 us -> 40.5 us
  local copies, waits for them, and re-layouts: 47.2 us -> 12 us
  starting transfers between devices: 56.9 us -> 27 us
  blocking collectives: 0 us -> 28 us
  Pallas kernels: 0 us -> 23.5 us
  matrix products: 19.3 us -> 0 us
  between operations: 15.7 us -> 0.84 us
  other arithmetic: 10.9 us -> 2.41 us
    psum x1 -> x0, waiting for transfers between devices: 264 us -> none  [body(): lax.psum((local_first, local_second), ('gx', 'gy', 'gz'))]
    ppermute x18 -> x4, starting transfers between devices: 56.9 us -> 9.5 us  [the longest x1 4.34 us: body(): left = lax.ppermute(strip, 'gz', ends)]
    all_to_all x0 -> x3, waiting for transfers between devices: none -> 29.3 us  [the longest x1 15.2 us: total(): return lax.all_to_all(every, AXES, 0, 0).astype(F32).reshape(sums.shape)]
    all_to_all x0 -> x1, blocking collectives: none -> 28 us  [total(): mine = jnp.sum(lax.all_to_all(parts, AXES, 0, 0), axis=0).astype(BF16)]
    pallas_call x0 -> x2, Pallas kernels: none -> 23.5 us  [the longest x1 20.6 us: body(): pl.pallas_call(lambda *refs: layers(planes, *refs), out_shape=(jax.ShapeD...]
    dot_general x63 -> x0, matrix products: 19.3 us -> none  [the longest x45 12.7 us: stencil(): jnp.einsum('kxyz,ko->oxyz', stacked, matrix, preferred_element_type=jnp.f...]
    slice x35 -> x1, local copies, waits for them, and re-layouts: 18.1 us -> 0.04 us  [body(): down = lax.ppermute(main[:, :3], ('gx', 'gy'), backward)]
    all_to_all x0 -> x3, starting transfers between devices: none -> 17.5 us  [the longest x1 7.56 us: total(): return lax.all_to_all(every, AXES, 0, 0).astype(F32).reshape(sums.shape)]
  transfers between devices with their start and end apart: 19 -> 7, of which waited for: 10 -> 6; matrix products, arithmetic and copies ran while one was open for 4% -> 4% of each run, Pallas kernels for 0% -> 0%
where the time goes in v1:
time: 135 us; the launch traced here: 134 us
  waiting for transfers between devices  40.5 us (30%)
  blocking collectives  28 us (21%)
  starting transfers between devices  27 us (20%)
  Pallas kernels  23.5 us (17%)
  local copies, waits for them, and re-layouts  12 us (9%)
  other arithmetic  2.41 us (2%)
    all_to_all x1, blocking collectives, total(): mine = jnp.sum(lax.all_to_all(parts, AXES, 0, 0), axis=0).astype(BF16)  28 us
    pallas_call x1, Pallas kernels, body(): pl.pallas_call(lambda *refs: layers(planes, *refs), out_shape=(jax.ShapeD...  20.6 us
    all_to_all x1, waiting for transfers between devices, total(): return lax.all_to_all(every, AXES, 0, 0).astype(F32).reshape(sums.shape)  15.2 us
    ppermute x1, waiting for transfers between devices, body(): down = lax.ppermute(main[:, :3], ('gx', 'gy'), backward)  9.57 us
    all_to_all x1, starting transfers between devices, total(): return lax.all_to_all(every, AXES, 0, 0).astype(F32).reshape(sums.shape)  7.56 us
    all_to_all x1, waiting for transfers between devices, body(): lax.all_to_all(split, 'gx', 0, 0).reshape(planes, rows, channels, width)  7.18 us
    all_to_all x1, waiting for transfers between devices, body(): lax.all_to_all(jv.reshape(n_gx, depth, rows, channels, width), 'gx', 0, 0)  6.97 us
    all_to_all x1, starting transfers between devices, body(): lax.all_to_all(split, 'gx', 0, 0).reshape(planes, rows, channels, width)  6.56 us
  transfers between devices with their start and end apart: 7, of which 6 were waited for; matrix products, arithmetic and copies ran while one was open for 4% of the time, Pallas kernels for 0%

profile of v1, /device:TPU:1, one launch (start us, length us, event | category | flops | bytes accessed | tf_op | source)
XLA Modules:
  0.0 134.3 jit_solution(17356383057239631780)
XLA Ops:
  0.6 0.0 copy-start.4
  0.6 0.0 copy-start.1
  0.7 0.0 copy-start.2
  0.7 1.8 %copy.36 = bf16[32,2,4,4,128]{4,0,3,1,2:T(8,128)(2,1)} copy(bf16[32,2,4,4,128]{4,3,2,1,0:T(4,128)(2,1)} %bitcast.39) | data formatting | bytes 524288 | tf_op jit(solution)/shard_map/reshape | solution.py:209
  2.5 0.0 copy-start.3
  2.5 6.6 %all-to-all-start = ((bf16[4,2,4,32,128]{4,3,2,1,0:T(8,128)(2,1)}), bf16[4,2,4,32,128]{4,3,2,1,0:T(8,128)(2,1)S(1)}, u32[]{:S(2)}, u32[]{:S(2)}) async-start(bf16[4,2,4,32,128]{4,3,2,1,0:T(8,128)(2,1)} %bitcast.33), calls=%async_computation | async-start | bytes 524288 | tf_op jit(solution)/shard_map/all_to_all | solution.py:210
  9.0 0.0 copy-done.4
  9.1 0.0 copy-done.1
  9.1 0.2 copy.22
  9.2 0.0 copy-done.2
  9.4 0.0 copy-done.3
  9.4 7.2 %all-to-all-done = bf16[4,2,4,32,128]{4,3,2,1,0:T(8,128)(2,1)S(1)} async-done(((bf16[4,2,4,32,128]{4,3,2,1,0:T(8,128)(2,1)}), bf16[4,2,4,32,128]{4,3,2,1,0:T(8,128)(2,1)S(1)}, u32[]{:S(2)}, u32[]{:S(2)}) %all-to-all-start) | async-done | bytes 262176 | tf_op jit(solution)/shard_map/all_to_all | solution.py:210
  16.6 0.0 copy-start
  16.7 1.9 %collective-permute-start = (bf16[8,3,32,128]{3,2,1,0:T(8,128)(2,1)S(1)}, bf16[8,3,32,128]{3,2,1,0:T(8,128)(2,1)S(1)}, u32[]{:S(2)}, u32[]{:S(2)}) collective-permute-start(bf16[8,3,32,128]{3,2,1,0:T(8,128)(2,1)S(1)} %get-tuple-element.20), channel_id=1, source_target_pairs={{0,64},{64,128},{128,192},{192,8},{8,72},{72,136},{136,200},{200,1... | collective-permute-start | bytes 589832 | tf_op jit(solution)/shard_map/ppermute | solution.py:218
  18.6 1.3 collective-permute-start.1
  19.9 0.1 compare_and_fusion.2
  20.0 1.2 collective-permute-done.refs_1_
  21.2 0.0 copy-start.5
  21.2 9.6 %collective-permute-done.1.refs_2_ = bf16[8,3,32,128]{3,2,1,0:T(8,128)(2,1)S(1)} collective-permute-done((bf16[8,3,32,128]{3,2,1,0:T(8,128)(2,1)S(1)}, bf16[8,3,32,128]{3,2,1,0:T(8,128)(2,1)S(1)}, u32[]{:S(2)}, u32[]{:S(2)}) %collective-permute-start.1) | collective-permute-done | bytes 196640 | tf_op jit(solution)/shard_map/ppermute | solution.py:219
  30.8 0.0 copy-done
  30.8 0.0 copy-done.5
  30.8 0.0 copy-start.6
  30.8 0.7 copy-done.6
  31.5 2.8 %assemble.1 = (bf16[8,32,1408]{2,1,0:T(8,128)(2,1)}, bf16[8,32,128]{2,1,0:T(8,128)(2,1)}) custom-call(bf16[8,4,32,128]{3,2,1,0:T(8,128)(2,1)} %bitcast.36, bf16[8,3,32,128]{3,2,1,0:T(8,128)(2,1)} %copy-done.5, bf16[8,3,32,128]{3,2,1,0:T(8,128)(2,1)} %copy-done.6), custom_call_target="tpu_custom_call" | custom-call | tf_op jit(solution)/shard_map/assemble/pallas_call | solution.py:222
  34.3 4.3 %collective-permute-start.2 = (bf16[8,32,128]{2,1,0:T(8,128)(2,1)}, bf16[8,32,128]{2,1,0:T(8,128)(2,1)S(1)}, u32[]{:S(2)}, u32[]{:S(2)}) collective-permute-start(bf16[8,32,128]{2,1,0:T(8,128)(2,1)} %get-tuple-element.8), channel_id=1, source_target_pairs={{0,1},{1,2},{2,3},{3,4},{4,5},{5,6},{6,7},{8,9},{9,10},{10,11},{11... | collective-permute-start | bytes 196616 | tf_op jit(solution)/shard_map/ppermute | solution.py:234
  38.7 1.9 %collective-permute-start.3 = (bf16[8,32,128]{2,1,0:T(8,128)(2,1)}, bf16[8,32,128]{2,1,0:T(8,128)(2,1)S(1)}, u32[]{:S(2)}, u32[]{:S(2)}) collective-permute-start(bf16[8,32,128]{2,1,0:T(8,128)(2,1)} %get-tuple-element.8), channel_id=1, source_target_pairs={{1,0},{2,1},{3,2},{4,3},{5,4},{6,5},{7,6},{9,8},{10,9},{11,10},{12... | collective-permute-start | bytes 196616 | tf_op jit(solution)/shard_map/ppermute | solution.py:235
  40.6 0.9 copy.31
  41.5 1.8 %reshape.210.refs_3_ = bf16[480,288]{1,0:T(8,128)(2,1)} reshape(bf16[5,3,32,3,3,32]{5,4,3,2,1,0:T(4,128)(2,1)S(1)} %copy.31) | data formatting | bytes 552960 | tf_op jit(solution)/shard_map/reshape | solution.py:190
  43.4 0.1 stack.35
  43.4 0.6 convert_element_type.21.refs_4_
  44.0 0.0 collective-permute-done.2.refs_1_
  44.0 0.0 copy-start.7
  44.1 0.4 collective-permute-done.3.refs_2_
  44.4 0.0 copy-start.8
  44.4 0.2 copy-done.7
  44.7 0.4 copy-done.8
  45.1 20.6 %layers.1 = (bf16[8,4,32,128]{3,2,1,0:T(8,128)(2,1)}, f32[2,288,96]{2,1,0:T(8,128)}) custom-call(bf16[8,32,1408]{2,1,0:T(8,128)(2,1)} %get-tuple-element.7.refs_0_, bf16[8,32,128]{2,1,0:T(8,128)(2,1)} %copy-done.7, bf16[8,32,128]{2,1,0:T(8,128)(2,1)} %copy-done.8, bf16[480,288]{1,0:T(8,128)(2,1)} %reshape.210.refs_3_, f32[8,1152]{1,0:T(8,128)} %convert_element_type.21.refs_4_), custom_call_target="tpu_custom_call" | custom-call | tf_op jit(solution)/shard_map/layers/pallas_call | solution.py:242
  65.7 1.7 %all_to_all.21 = f32[256,1,216]{2,1,0:T(1,128)S(1)} reshape(f32[2,288,96]{2,1,0:T(8,128)} %get-tuple-element.10) | data formatting | bytes 442368 | tf_op jit(solution)/shard_map/all_to_all | solution.py:196
  67.4 28.0 %all_to_all.26 = f32[256,1,216]{2,1,0:T(1,128)S(1)} all-to-all(f32[256,1,216]{2,1,0:T(1,128)S(1)} %all_to_all.21), channel_id=1, replica_groups=mesh['gx'=4,'gy'=8,'gz'=8] {'gx','gy','gz'}, dimensions={0} | all-to-all | bytes 442368 | tf_op jit(solution)/shard_map/all_to_all | solution.py:196
  95.5 3.4 %all-to-all-start.1 = ((bf16[4,2,4,32,128]{4,3,2,1,0:T(8,128)(2,1)}), bf16[4,2,4,32,128]{4,3,2,1,0:T(8,128)(2,1)S(1)}, u32[]{:S(2)}, u32[]{:S(2)}) async-start(bf16[4,2,4,32,128]{4,3,2,1,0:T(8,128)(2,1)} %bitcast.41), calls=%async_computation.1 | async-start | bytes 524288 | tf_op jit(solution)/shard_map/all_to_all | solution.py:260
  98.9 0.3 reduce_sum.9
  99.2 7.0 %all-to-all-done.1 = bf16[4,2,4,32,128]{4,3,2,1,0:T(8,128)(2,1)S(1)} async-done(((bf16[4,2,4,32,128]{4,3,2,1,0:T(8,128)(2,1)}), bf16[4,2,4,32,128]{4,3,2,1,0:T(8,128)(2,1)S(1)}, u32[]{:S(2)}, u32[]{:S(2)}) %all-to-all-start.1) | async-done | bytes 262176 | tf_op jit(solution)/shard_map/all_to_all | solution.py:260
  106.2 0.8 broadcast_in_dim.2
  107.0 7.6 %all-to-all-start.3 = ((bf16[256,1,216]{2,1,0:T(2,128)(2,1)}), bf16[256,1,216]{2,1,0:T(2,128)(2,1)S(1)}, u32[]{:S(2)}, u32[]{:S(2)}) async-start(bf16[256,1,216]{2,1,0:T(2,128)(2,1)} %broadcast_in_dim.2), calls=%async_computation.3 | async-start | bytes 524288 | tf_op jit(solution)/shard_map/all_to_all | solution.py:198
  114.6 0.8 copy.25
  115.4 15.2 %all-to-all-done.3 = bf16[256,1,216]{2,1,0:T(2,128)(2,1)S(1)} async-done(((bf16[256,1,216]{2,1,0:T(2,128)(2,1)}), bf16[256,1,216]{2,1,0:T(2,128)(2,1)S(1)}, u32[]{:S(2)}, u32[]{:S(2)}) %all-to-all-start.3) | async-done | bytes 110624 | tf_op jit(solution)/shard_map/all_to_all | solution.py:198
  130.6 0.7 convert_reduce_fusion
  131.3 0.7 reshape.209
  132.0 0.7 fusion.2
  132.7 0.8 copy.29
  133.5 0.8 copy.30
  (8 shorter events, 0.2 us)
Async XLA Ops:
  0.6 8.4 %copy-start.4 = (bf16[3,3,3,32,32]{4,3,2,1,0:T(8,128)(2,1)S(1)}, bf16[3,3,3,32,32]{4,3,2,1,0:T(8,128)(2,1)}, u32[]{:S(2)}) copy-start(bf16[3,3,3,32,32]{4,3,2,1,0:T(8,128)(2,1)} %param.6) | copy-start | bytes 165892
  0.6 8.4 %copy-start.1 = (bf16[3,3,3,32,32]{4,3,2,1,0:T(8,128)(2,1)S(1)}, bf16[3,3,3,32,32]{4,3,2,1,0:T(8,128)(2,1)}, u32[]{:S(2)}) copy-start(bf16[3,3,3,32,32]{4,3,2,1,0:T(8,128)(2,1)} %param.7) | copy-start | bytes 165892
  0.7 8.6 %copy-start.2 = (bf16[3,3,3,32,32]{4,3,2,1,0:T(8,128)(2,1)S(1)}, bf16[3,3,3,32,32]{4,3,2,1,0:T(8,128)(2,1)}, u32[]{:S(2)}) copy-start(bf16[3,3,3,32,32]{4,3,2,1,0:T(8,128)(2,1)} %param.8) | copy-start | bytes 165892
  2.5 6.9 %copy-start.3 = (bf16[3,3,3,32,32]{4,3,2,1,0:T(8,128)(2,1)S(1)}, bf16[3,3,3,32,32]{4,3,2,1,0:T(8,128)(2,1)}, u32[]{:S(2)}) copy-start(bf16[3,3,3,32,32]{4,3,2,1,0:T(8,128)(2,1)} %param.9) | copy-start | bytes 165892
  2.5 14.1 %all-to-all-start = ((bf16[4,2,4,32,128]{4,3,2,1,0:T(8,128)(2,1)}), bf16[4,2,4,32,128]{4,3,2,1,0:T(8,128)(2,1)S(1)}, u32[]{:S(2)}, u32[]{:S(2)}) async-start(bf16[4,2,4,32,128]{4,3,2,1,0:T(8,128)(2,1)} %bitcast.33), calls=%async_computation | async-start | bytes 524288 | tf_op jit(solution)/shard_map/all_to_all | solution.py:210
  16.6 14.2 %copy-start = (bf16[4,2,4,32,128]{4,3,2,1,0:T(8,128)(2,1)}, bf16[4,2,4,32,128]{4,3,2,1,0:T(8,128)(2,1)S(1)}, u32[]{:S(2)}) copy-start(bf16[4,2,4,32,128]{4,3,2,1,0:T(8,128)(2,1)S(1)} %all-to-all-done) | copy-start | bytes 786436
  16.7 4.5 %collective-permute-start = (bf16[8,3,32,128]{3,2,1,0:T(8,128)(2,1)S(1)}, bf16[8,3,32,128]{3,2,1,0:T(8,128)(2,1)S(1)}, u32[]{:S(2)}, u32[]{:S(2)}) collective-permute-start(bf16[8,3,32,128]{3,2,1,0:T(8,128)(2,1)S(1)} %get-tuple-element.20), channel_id=1, source_target_pairs={{0,64},{64,128},{128,192},{192,8},{8,72},{72,136},{136,200},{200,1... | collective-permute-start | bytes 589832 | tf_op jit(solution)/shard_map/ppermute | solution.py:218
  18.6 12.2 %collective-permute-start.1 = (bf16[8,3,32,128]{3,2,1,0:T(8,128)(2,1)S(1)}, bf16[8,3,32,128]{3,2,1,0:T(8,128)(2,1)S(1)}, u32[]{:S(2)}, u32[]{:S(2)}) collective-permute-start(bf16[8,3,32,128]{3,2,1,0:T(8,128)(2,1)S(1)} %get-tuple-element.19), channel_id=1, source_target_pairs={{64,0},{128,64},{192,128},{8,192},{72,8},{136,72},{200,136},{16,20... | collective-permute-start | bytes 589832 | tf_op jit(solution)/shard_map/ppermute | solution.py:219
  21.2 9.6 %copy-start.5 = (bf16[8,3,32,128]{3,2,1,0:T(8,128)(2,1)}, bf16[8,3,32,128]{3,2,1,0:T(8,128)(2,1)S(1)}, u32[]{:S(2)}) copy-start(bf16[8,3,32,128]{3,2,1,0:T(8,128)(2,1)S(1)} %collective-permute-done.refs_1_) | copy-start | bytes 589828
  30.8 0.7 copy-start.6
  34.3 9.7 %collective-permute-start.2 = (bf16[8,32,128]{2,1,0:T(8,128)(2,1)}, bf16[8,32,128]{2,1,0:T(8,128)(2,1)S(1)}, u32[]{:S(2)}, u32[]{:S(2)}) collective-permute-start(bf16[8,32,128]{2,1,0:T(8,128)(2,1)} %get-tuple-element.8), channel_id=1, source_target_pairs={{0,1},{1,2},{2,3},{3,4},{4,5},{5,6},{6,7},{8,9},{9,10},{10,11},{11... | collective-permute-start | bytes 196616 | tf_op jit(solution)/shard_map/ppermute | solution.py:234
  38.7 5.8 %collective-permute-start.3 = (bf16[8,32,128]{2,1,0:T(8,128)(2,1)}, bf16[8,32,128]{2,1,0:T(8,128)(2,1)S(1)}, u32[]{:S(2)}, u32[]{:S(2)}) collective-permute-start(bf16[8,32,128]{2,1,0:T(8,128)(2,1)} %get-tuple-element.8), channel_id=1, source_target_pairs={{1,0},{2,1},{3,2},{4,3},{5,4},{6,5},{7,6},{9,8},{10,9},{11,10},{12... | collective-permute-start | bytes 196616 | tf_op jit(solution)/shard_map/ppermute | solution.py:235
  44.0 0.6 copy-start.7
  44.4 0.6 copy-start.8
  95.5 10.7 %all-to-all-start.1 = ((bf16[4,2,4,32,128]{4,3,2,1,0:T(8,128)(2,1)}), bf16[4,2,4,32,128]{4,3,2,1,0:T(8,128)(2,1)S(1)}, u32[]{:S(2)}, u32[]{:S(2)}) async-start(bf16[4,2,4,32,128]{4,3,2,1,0:T(8,128)(2,1)} %bitcast.41), calls=%async_computation.1 | async-start | bytes 524288 | tf_op jit(solution)/shard_map/all_to_all | solution.py:260
  107.0 23.6 %all-to-all-start.3 = ((bf16[256,1,216]{2,1,0:T(2,128)(2,1)}), bf16[256,1,216]{2,1,0:T(2,128)(2,1)S(1)}, u32[]{:S(2)}, u32[]{:S(2)}) async-start(bf16[256,1,216]{2,1,0:T(2,128)(2,1)} %broadcast_in_dim.2), calls=%async_computation.3 | async-start | bytes 524288 | tf_op jit(solution)/shard_map/all_to_all | solution.py:198

commit v2 on v1

--- a/solution.py
+++ b/solution.py
@@ -77,7 +77,17 @@
         )[:, :width].astype(BF16)
 
 
-def layers(
+def window(x):
+    return pl.ds(pl.multiple_of(x * 96, 32), 288)
+
+
+def correlate(rows, moved):
+    return lax.dot_general(
+        rows, moved.astype(BF16), (((1,), (1,)), ((), ())), preferred_element_type=F32
+    )
+
+
+def outward(
     planes,
     field_ref,
     left_ref,
@@ -87,10 +97,10 @@
     jv_ref,
     sums_ref,
     p_vol,
+    p_jv,
+    slopes,
     p_hid,
     p_tan,
-    p_jv,
-    slopes,
 ):
     for ref, width in ((p_vol, LH), (p_hid, LJ), (p_tan, LJ), (p_jv, LB)):
         blank = jnp.zeros((96, width), BF16)
@@ -98,9 +108,6 @@
         ref[96 * (planes + 1) : 96 * (planes + 2), :] = blank
     sums_ref[...] = jnp.zeros_like(sums_ref)
     lane = lanes_of((32, 128))
-
-    def window(x):
-        return pl.ds(pl.multiple_of(x * 96, 32), 288)
 
     def fill(x, carry):
         left = left_ref[x].astype(F32)
@@ -141,31 +148,64 @@
             pair = jv[:, 128 * (row + 1) : 128 * (row + 3)]
             jv_ref[x, row] = back_by(pair, 8 * row + 9)[:, :128].astype(BF16)
         own = jnp.where(mask_ref[2:3, :LJ] > 0.0, jv, 0.0)
-        moved = jnp.concatenate([own, pltpu.roll(own, 1, 1), pltpu.roll(own, 2, 1)], axis=0)
-        sums_ref[0] += lax.dot_general(
-            near[:, 128:768],
-            moved[:, 128:768].astype(BF16),
-            (((1,), (1,)), ((), ())),
-            preferred_element_type=F32,
+        moved = jnp.concatenate(
+            [own, pltpu.roll(own, 1, 1), pltpu.roll(own, 2, 1), jnp.zeros_like(own)], axis=0
         )
+        sums_ref[...] += correlate(near[:, 128:768], moved[:, 128:768])
         return carry
 
     lax.fori_loop(0, planes, second, 0)
+
+
+def inward(planes, weight_ref, mask_ref, second_ref, p_vol, p_jv, slopes, packed_ref, sums):
+    sums[...] = jnp.zeros_like(sums)
 
     def third(x, carry):
         product = jnp.dot(weight_ref[384:480, :], p_jv[window(x), :], preferred_element_type=F32)
         back = slopes[x] * fold(product)
         back = jnp.where(mask_ref[3:4, :LB] > 0.0, back, 0.0).astype(BF16).astype(F32)
-        moved = jnp.concatenate([pltpu.roll(back, 18 + k, 1) for k in range(3)], axis=0)
-        sums_ref[1] += lax.dot_general(
-            p_vol[window(x), 256:896],
-            moved.astype(BF16),
-            (((1,), (1,)), ((), ())),
-            preferred_element_type=F32,
+        moved = jnp.concatenate(
+            [
+                pltpu.roll(back, 19, 1),
+                pltpu.roll(back, 20, 1),
+                jnp.zeros_like(back),
+                pltpu.roll(back, 18, 1),
+            ],
+            axis=0,
         )
+        sums[...] += correlate(p_vol[window(x), 256:896], moved)
         return carry
 
     lax.fori_loop(0, planes, third, 0)
+    packed_ref[0:288, :] = jnp.where(lanes_of((288, 128)) < 96, second_ref[...], sums[...])
+    packed_ref[288:432, :] = jnp.where(
+        lanes_of((144, 128)) < 64, sums[0:144, :], pltpu.roll(sums[144:288, :], 64, 1)
+    )
+    packed_ref[432:512, :] = jnp.zeros((80, 128), F32)
+
+
+def combine(parts_ref, out_ref):
+    total = jnp.sum(parts_ref[...].reshape(64, 8, 128), axis=0)
+    total = total + pltpu.roll(total, 4, 0)
+    total = total + pltpu.roll(total, 2, 0)
+    out_ref[...] = jnp.broadcast_to(total[None], (64, 8, 128)).reshape(512, 128).astype(BF16)
+
+
+def finish(factor, count_all, packed_ref, v_first_ref, v_second_ref, first_ref, second_ref):
+    def damped(summed, direction):
+        return factor * (summed / count_all + 0.1 * direction.astype(F32))
+
+    high = packed_ref[288:432, :].astype(F32)
+    high = jnp.concatenate([high, pltpu.roll(high, 64, 1)], axis=0)
+    for k in range(9):
+        low = packed_ref[32 * k : 32 * k + 32, :].astype(F32)
+        far = high[32 * k : 32 * k + 32]
+        for offset in range(3):
+            at = 3 * k + offset
+            second_ref[at] = damped(low[:, 32 * offset : 32 * offset + 32], v_second_ref[at])
+        first_ref[3 * k] = damped(low[:, 96:128], v_first_ref[3 * k])
+        first_ref[3 * k + 1] = damped(far[:, 0:32], v_first_ref[3 * k + 1])
+        first_ref[3 * k + 2] = damped(far[:, 32:64], v_first_ref[3 * k + 2])
 
 
 def cell_masks(row0, col0, height, width):
@@ -188,14 +228,6 @@
     flipped = jnp.transpose(jnp.flip(w_second, (0, 1, 2)), (0, 1, 2, 4, 3))
     stacked = jnp.stack([w_first, v_first, w_second, v_second, flipped])
     return jnp.transpose(stacked, (0, 3, 5, 1, 2, 4)).reshape(480, 288)
-
-
-def total(sums):
-    count = lax.axis_size(AXES)
-    parts = sums.reshape(count, -1)
-    mine = jnp.sum(lax.all_to_all(parts, AXES, 0, 0), axis=0).astype(BF16)
-    every = jnp.broadcast_to(mine[None], (count, mine.shape[0]))
-    return lax.all_to_all(every, AXES, 0, 0).astype(F32).reshape(sums.shape)
 
 
 def body(volume, w_first, w_second, v_first, v_second):
@@ -215,56 +247,82 @@
     blocks = n_gx * n_gy
     onward = [(device(i), device(i + 1)) for i in range(blocks - 1)]
     backward = [(b, a) for a, b in onward]
-    up = lax.ppermute(main[:, 1:], ("gx", "gy"), onward)
-    down = lax.ppermute(main[:, :3], ("gx", "gy"), backward)
-
-    vmem = pl.BlockSpec(memory_space=pltpu.VMEM)
-    field, strip = pl.pallas_call(
-        lambda *refs: assemble(planes, *refs),
-        out_shape=(
-            jax.ShapeDtypeStruct((planes, channels, LA), BF16),
-            jax.ShapeDtypeStruct((planes, channels, 128), BF16),
-        ),
-        in_specs=[vmem] * 3,
-        out_specs=(vmem, vmem),
-        name="assemble",
-    )(main, up, down)
-
-    ends = [(i, i + 1) for i in range(n_gz - 1)]
-    left = lax.ppermute(strip, "gz", ends)
-    right = lax.ppermute(strip, "gz", [(b, a) for a, b in ends])
-
     row0 = (lax.axis_index("gy") * n_gx + lax.axis_index("gx")) * rows
     col0 = lax.axis_index("gz") * width
     masks = cell_masks(row0, col0, height * n_gy, width * n_gz)
     weights = filters(w_first, v_first, w_second, v_second)
-
-    jv, sums = pl.pallas_call(
-        lambda *refs: layers(planes, *refs),
-        out_shape=(
-            jax.ShapeDtypeStruct((planes, rows, channels, width), BF16),
-            jax.ShapeDtypeStruct((2, 288, 96), F32),
-        ),
-        in_specs=[vmem] * 5,
-        out_specs=(vmem, vmem),
-        scratch_shapes=[
-            pltpu.VMEM((96 * (planes + 2), LH), BF16),
-            pltpu.VMEM((96 * (planes + 2), LJ), BF16),
-            pltpu.VMEM((96 * (planes + 2), LJ), BF16),
-            pltpu.VMEM((96 * (planes + 2), LB), BF16),
-            pltpu.VMEM((planes, channels, LB), F32),
+    main, masks, weights = lax.optimization_barrier((main, masks, weights))
+
+    up = lax.ppermute(main[:, 1:], ("gx", "gy"), onward)
+    down = lax.ppermute(main[:, :3], ("gx", "gy"), backward)
+
+    vmem = pl.BlockSpec(memory_space=pltpu.VMEM)
+
+    def call(kernel, operands, outputs, scratch, name, limit):
+        return pl.pallas_call(
+            kernel,
+            out_shape=tuple(jax.ShapeDtypeStruct(shape, dtype) for shape, dtype in outputs),
+            in_specs=[vmem] * len(operands),
+            out_specs=(vmem,) * len(outputs),
+            scratch_shapes=[pltpu.VMEM(shape, dtype) for shape, dtype in scratch],
+            compiler_params=pltpu.CompilerParams(vmem_limit_bytes=limit << 20),
+            name=name,
+        )(*operands)
+
+    field, strip = call(
+        lambda *refs: assemble(planes, *refs),
+        (main, up, down),
+        [((planes, channels, LA), BF16), ((planes, channels, 128), BF16)],
+        [],
+        "assemble",
+        8,
+    )
+
+    ends = [(i, i + 1) for i in range(n_gz - 1)]
+    left = lax.ppermute(strip, "gz", ends)
+    right = lax.ppermute(strip, "gz", [(b, a) for a, b in ends])
+
+    stack = 96 * (planes + 2)
+    jv, second, p_vol, p_jv, slopes = call(
+        lambda *refs: outward(planes, *refs),
+        (field, left, right, weights, masks),
+        [
+            ((planes, rows, channels, width), BF16),
+            ((288, 128), F32),
+            ((stack, LH), BF16),
+            ((stack, LB), BF16),
+            ((planes, channels, LB), F32),
         ],
-        name="layers",
-    )(field, left, right, weights, masks)
+        [((stack, LJ), BF16), ((stack, LJ), BF16)],
+        "outward",
+        24,
+    )
 
     home = lax.all_to_all(jv.reshape(n_gx, depth, rows, channels, width), "gx", 0, 0)
     out = jnp.transpose(home, (3, 1, 0, 2, 4)).reshape(channels, depth, height, width)
 
-    summed = total(sums).reshape(2, 3, 3, channels, 3, channels)
-    summed_second, summed_first = jnp.transpose(summed, (0, 1, 2, 4, 3, 5))
-    gv_first = factor * (summed_first / count_all + 0.1 * v_first.astype(F32))
-    gv_second = factor * (summed_second / count_all + 0.1 * v_second.astype(F32))
-    return (out, gv_first, gv_second)
+    (packed,) = call(
+        lambda *refs: inward(planes, *refs),
+        (weights, masks, second, p_vol, p_jv, slopes),
+        [((512, 128), F32)],
+        [((288, 128), F32)],
+        "inward",
+        24,
+    )
+
+    count = lax.axis_size(AXES)
+    parts = lax.all_to_all(packed.reshape(count, 2, 128), AXES, 0, 0).reshape(512, 128)
+    (every,) = call(combine, (parts,), [((512, 128), BF16)], [], "combine", 4)
+    every = lax.all_to_all(every.reshape(count, 2, 128), AXES, 0, 0).reshape(512, 128)
+    gv_first, gv_second = call(
+        lambda *refs: finish(factor, count_all, *refs),
+        (every, v_first.reshape(27, channels, channels), v_second.reshape(27, channels, channels)),
+        [((27, channels, channels), F32)] * 2,
+        [],
+        "finish",
+        8,
+    )
+    return (out, gv_first.reshape(v_first.shape), gv_second.reshape(v_first.shape))
 
 
 def solution(mesh):

time: 135 us -> 122 us (0.904)
  waiting for transfers between devices: 40.5 us -> 27.9 us
  local copies, waits for them, and re-layouts: 12 us -> 4.92 us
  blocking collectives: 28 us -> 33.3 us
  starting transfers between devices: 27 us -> 31.2 us
  other arithmetic: 2.41 us -> 0.11 us
    ppermute x1, waiting for transfers between devices: 9.57 us -> 1.11 us  [body(): down = lax.ppermute(main[:, :3], ('gx', 'gy'), backward)]
    all_to_all x1, blocking collectives: 28 us -> 33.3 us  [body(): lax.all_to_all(packed.reshape(count, 2, 128), AXES, 0, 0).reshape(512, 128)]
    ppermute x1, starting transfers between devices: 1.92 us -> 5.34 us  [body(): right = lax.ppermute(strip, 'gz', [(b, a) for a, b in ends])]
    unnamed x25 -> x13, local copies, waits for them, and re-layouts: 3.21 us -> 0.28 us
    all_to_all x1, waiting for transfers between devices: 15.2 us -> 12.4 us  [body(): lax.all_to_all(every.reshape(count, 2, 128), AXES, 0, 0).reshape(512, 128)]
    ppermute x1, starting transfers between devices: 1.95 us -> 4 us  [body(): up = lax.ppermute(main[:, 1:], ('gx', 'gy'), onward)]
    reshape x2 -> x1, local copies, waits for them, and re-layouts: 2.75 us -> 0.84 us  [filters(): return jnp.transpose(stacked, (0, 3, 5, 1, 2, 4)).reshape(480, 288)]
    all_to_all x1, waiting for transfers between devices: 7.18 us -> 5.36 us  [body(): lax.all_to_all(split, 'gx', 0, 0).reshape(planes, rows, channels, width)]
  transfers between devices with their start and end apart: 7 -> 7, of which waited for: 6 -> 6; matrix products, arithmetic and copies ran while one was open for 4% -> 3% of each run, Pallas kernels for 0% -> 1%
where the time goes in v2:
time: 122 us
  blocking collectives  33.3 us (27%)
  starting transfers between devices  31.2 us (26%)
  waiting for transfers between devices  27.9 us (23%)
  Pallas kernels  23.6 us (19%)
  local copies, waits for them, and re-layouts  4.92 us (4%)
    all_to_all x1, blocking collectives, body(): lax.all_to_all(packed.reshape(count, 2, 128), AXES, 0, 0).reshape(512, 128)  33.3 us
    pallas_call x5, Pallas kernels, call(): pl.pallas_call(kernel, out_shape=tuple((jax.ShapeDtypeStruct(shape, dtype...  23.6 us
    all_to_all x1, waiting for transfers between devices, body(): lax.all_to_all(every.reshape(count, 2, 128), AXES, 0, 0).reshape(512, 128)  12.4 us
    all_to_all x1, starting transfers between devices, body(): lax.all_to_all(every.reshape(count, 2, 128), AXES, 0, 0).reshape(512, 128)  7.53 us
    all_to_all x1, starting transfers between devices, body(): lax.all_to_all(split, 'gx', 0, 0).reshape(planes, rows, channels, width)  6.56 us
    all_to_all x1, waiting for transfers between devices, body(): lax.all_to_all(jv.reshape(n_gx, depth, rows, channels, width), 'gx', 0, 0)  6.53 us
    all_to_all x1, waiting for transfers between devices, body(): lax.all_to_all(split, 'gx', 0, 0).reshape(planes, rows, channels, width)  5.36 us
    ppermute x1, starting transfers between devices, body(): right = lax.ppermute(strip, 'gz', [(b, a) for a, b in ends])  5.34 us
  transfers between devices with their start and end apart: 7, of which 6 were waited for; matrix products, arithmetic and copies ran while one was open for 3% of the time, Pallas kernels for 1%

profile of v2, /device:TPU:1, one launch (start us, length us, event | category | flops | bytes accessed | tf_op | source)
XLA Modules:
  0.0 122.0 jit_solution(9276475097079838543)
XLA Ops:
  0.6 0.0 copy-start.3
  0.6 0.0 copy-start
  0.7 0.0 copy-start.2
  0.7 1.8 %copy.19 = bf16[32,2,4,4,128]{4,0,3,1,2:T(8,128)(2,1)} copy(bf16[32,2,4,4,128]{4,3,2,1,0:T(4,128)(2,1)} %bitcast.40) | data formatting | bytes 524288 | tf_op jit(solution)/shard_map/reshape | solution.py:241
  2.5 0.0 copy-start.1
  2.5 6.6 %all-to-all-start = ((bf16[4,2,4,32,128]{4,3,2,1,0:T(8,128)(2,1)}), bf16[4,2,4,32,128]{4,3,2,1,0:T(8,128)(2,1)S(1)}, u32[]{:S(2)}, u32[]{:S(2)}) async-start(bf16[4,2,4,32,128]{4,3,2,1,0:T(8,128)(2,1)} %bitcast.30), calls=%async_computation | async-start | bytes 524288 | tf_op jit(solution)/shard_map/all_to_all | solution.py:242
  9.1 0.0 copy-done.3
  9.1 0.0 copy-done
  9.2 0.0 copy-done.2
  9.2 0.1 compare_and_fusion.2
  9.3 0.2 copy.13
  9.5 0.1 stack.29
  9.6 0.0 copy-done.1
  9.6 0.8 copy.14
  10.4 0.8 reshape.210
  11.3 5.4 %all-to-all-done = bf16[4,2,4,32,128]{4,3,2,1,0:T(8,128)(2,1)S(1)} async-done(((bf16[4,2,4,32,128]{4,3,2,1,0:T(8,128)(2,1)}), bf16[4,2,4,32,128]{4,3,2,1,0:T(8,128)(2,1)S(1)}, u32[]{:S(2)}, u32[]{:S(2)}) %all-to-all-start) | async-done | bytes 262176 | tf_op jit(solution)/shard_map/all_to_all | solution.py:242
  16.7 1.3 %collective-permute-start.1 = (bf16[8,3,32,128]{3,2,1,0:T(8,128)(2,1)S(1)}, bf16[8,3,32,128]{3,2,1,0:T(8,128)(2,1)S(1)}, u32[]{:S(2)}, u32[]{:S(2)}) collective-permute-start(bf16[8,3,32,128]{3,2,1,0:T(8,128)(2,1)S(1)} %get-tuple-element.27), channel_id=1, source_target_pairs={{64,0},{128,64},{192,128},{8,192},{72,8},{136,72},{200,136},{16,20... | collective-permute-start | bytes 589832 | tf_op jit(solution)/shard_map/ppermute | solution.py:257
  18.0 4.0 %collective-permute-start = (bf16[8,3,32,128]{3,2,1,0:T(8,128)(2,1)S(1)}, bf16[8,3,32,128]{3,2,1,0:T(8,128)(2,1)S(1)}, u32[]{:S(2)}, u32[]{:S(2)}) collective-permute-start(bf16[8,3,32,128]{3,2,1,0:T(8,128)(2,1)S(1)} %get-tuple-element.28), channel_id=1, source_target_pairs={{0,64},{64,128},{128,192},{192,8},{8,72},{72,136},{136,200},{200,1... | collective-permute-start | bytes 589832 | tf_op jit(solution)/shard_map/ppermute | solution.py:256
  22.0 1.1 collective-permute-done.1.refs_2_
  23.1 1.5 %collective-permute-done.refs_1_ = bf16[8,3,32,128]{3,2,1,0:T(8,128)(2,1)S(1)} collective-permute-done((bf16[8,3,32,128]{3,2,1,0:T(8,128)(2,1)S(1)}, bf16[8,3,32,128]{3,2,1,0:T(8,128)(2,1)S(1)}, u32[]{:S(2)}, u32[]{:S(2)}) %collective-permute-start) | collective-permute-done | bytes 196640 | tf_op jit(solution)/shard_map/ppermute | solution.py:256
  24.6 0.8 assemble.1
  25.4 5.3 %collective-permute-start.3 = (bf16[8,32,128]{2,1,0:T(8,128)(2,1)S(1)}, bf16[8,32,128]{2,1,0:T(8,128)(2,1)S(1)}, u32[]{:S(2)}, u32[]{:S(2)}) collective-permute-start(bf16[8,32,128]{2,1,0:T(8,128)(2,1)S(1)} %get-tuple-element.17), channel_id=1, source_target_pairs={{1,0},{2,1},{3,2},{4,3},{5,4},{6,5},{7,6},{9,8},{10,9},{11,10},{12... | collective-permute-start | bytes 196616 | tf_op jit(solution)/shard_map/ppermute | solution.py:283
  30.7 3.1 %collective-permute-start.2 = (bf16[8,32,128]{2,1,0:T(8,128)(2,1)S(1)}, bf16[8,32,128]{2,1,0:T(8,128)(2,1)S(1)}, u32[]{:S(2)}, u32[]{:S(2)}) collective-permute-start(bf16[8,32,128]{2,1,0:T(8,128)(2,1)S(1)} %get-tuple-element.17), channel_id=1, source_target_pairs={{0,1},{1,2},{2,3},{3,4},{4,5},{5,6},{6,7},{8,9},{9,10},{10,11},{11... | collective-permute-start | bytes 196616 | tf_op jit(solution)/shard_map/ppermute | solution.py:282
  33.9 0.2 copy.15.refs_3_.refs_0_
  34.1 0.0 collective-permute-done.3.refs_2_
  34.1 1.1 collective-permute-done.2.refs_1_
  35.2 13.5 %outward.1 = (bf16[8,4,32,128]{3,2,1,0:T(8,128)(2,1)}, f32[288,128]{1,0:T(8,128)S(1)}, bf16[960,1152]{1,0:T(8,128)(2,1)S(1)}, bf16[960,640]{1,0:T(8,128)(2,1)S(1)}, f32[8,32,640]{2,1,0:T(8,128)S(1)}) custom-call(bf16[8,32,1408]{2,1,0:T(8,128)(2,1)S(1)} %get-tuple-element.16.refs_0_, bf16[8,32,128]{2,1,0:T(8,128)(2,1)S(1)} %collective-permute-done.2.refs_1_, ...), custom_call_target="tpu_custom_call" | custom-call | tf_op jit(solution)/shard_map/outward/pallas_call | solution.py:262
  48.7 5.9 %inward.1 = f32[512,128]{1,0:T(8,128)S(1)} custom-call(bf16[480,288]{1,0:T(8,128)(2,1)S(1)} %copy.15.refs_3_.refs_0_, f32[8,1152]{1,0:T(8,128)S(1)} %convert_element_type.3.refs_4_.refs_1_, f32[288,128]{1,0:T(8,128)S(1)} %get-tuple-element.21.refs_2_, bf16[960,1152]{1,0:T(8,128)(2,1)S(1)} %get-tuple-element.22.refs_3_, ...), custom_call_target="tpu_custom_call" | custom-call | tf_op jit(solution)/shard_map/inward/pallas_call | solution.py:262
  54.6 33.3 %all_to_all.20 = f32[256,2,128]{2,1,0:T(2,128)S(1)} all-to-all(f32[256,2,128]{2,1,0:T(2,128)S(1)} %bitcast.33), channel_id=1, replica_groups=mesh['gx'=4,'gy'=8,'gz'=8] {'gx','gy','gz'}, dimensions={0} | all-to-all | bytes 524288 | tf_op jit(solution)/shard_map/all_to_all | solution.py:314
  87.9 3.4 %all-to-all-start.1 = ((bf16[4,2,4,32,128]{4,3,2,1,0:T(8,128)(2,1)}), bf16[4,2,4,32,128]{4,3,2,1,0:T(8,128)(2,1)S(1)}, u32[]{:S(2)}, u32[]{:S(2)}) async-start(bf16[4,2,4,32,128]{4,3,2,1,0:T(8,128)(2,1)} %bitcast.10), calls=%async_computation.1 | async-start | bytes 524288 | tf_op jit(solution)/shard_map/all_to_all | solution.py:301
  91.3 0.7 combine.1
  92.0 6.5 %all-to-all-done.1 = bf16[4,2,4,32,128]{4,3,2,1,0:T(8,128)(2,1)S(1)} async-done(((bf16[4,2,4,32,128]{4,3,2,1,0:T(8,128)(2,1)}), bf16[4,2,4,32,128]{4,3,2,1,0:T(8,128)(2,1)S(1)}, u32[]{:S(2)}, u32[]{:S(2)}) %all-to-all-start.1) | async-done | bytes 262176 | tf_op jit(solution)/shard_map/all_to_all | solution.py:301
  98.6 7.5 %all-to-all-start.3 = ((bf16[256,2,128]{2,1,0:T(2,128)(2,1)}), bf16[256,2,128]{2,1,0:T(2,128)(2,1)S(1)}, u32[]{:S(2)}, u32[]{:S(2)}) async-start(bf16[256,2,128]{2,1,0:T(2,128)(2,1)} %bitcast.15), calls=%async_computation.3 | async-start | bytes 262144 | tf_op jit(solution)/shard_map/all_to_all | solution.py:316
  106.1 0.8 copy.16
  106.9 12.4 %all-to-all-done.3 = bf16[256,2,128]{2,1,0:T(2,128)(2,1)S(1)} async-done(((bf16[256,2,128]{2,1,0:T(2,128)(2,1)}), bf16[256,2,128]{2,1,0:T(2,128)(2,1)S(1)}, u32[]{:S(2)}, u32[]{:S(2)}) %all-to-all-start.3) | async-done | bytes 131104 | tf_op jit(solution)/shard_map/all_to_all | solution.py:316
  119.3 2.7 %finish.1 = (f32[27,32,32]{2,1,0:T(8,128)}, f32[27,32,32]{2,1,0:T(8,128)}) custom-call(bf16[512,128]{1,0:T(8,128)(2,1)S(1)} %bitcast.37, bf16[27,32,32]{2,1,0:T(8,128)(2,1)S(1)} %bitcast.35, bf16[27,32,32]{2,1,0:T(8,128)(2,1)S(1)} %bitcast.36), custom_call_target="tpu_custom_call" | custom-call | tf_op jit(solution)/shard_map/finish/pallas_call | solution.py:262
  (9 shorter events, 0.2 us)
Async XLA Ops:
  0.6 8.5 %copy-start.3 = (bf16[3,3,3,32,32]{4,3,2,1,0:T(8,128)(2,1)S(1)}, bf16[3,3,3,32,32]{4,3,2,1,0:T(8,128)(2,1)}, u32[]{:S(2)}) copy-start(bf16[3,3,3,32,32]{4,3,2,1,0:T(8,128)(2,1)} %param.6) | copy-start | bytes 165892
  0.6 8.5 %copy-start = (bf16[3,3,3,32,32]{4,3,2,1,0:T(8,128)(2,1)S(1)}, bf16[3,3,3,32,32]{4,3,2,1,0:T(8,128)(2,1)}, u32[]{:S(2)}) copy-start(bf16[3,3,3,32,32]{4,3,2,1,0:T(8,128)(2,1)} %param.8) | copy-start | bytes 165892
  0.7 8.5 %copy-start.2 = (bf16[3,3,3,32,32]{4,3,2,1,0:T(8,128)(2,1)S(1)}, bf16[3,3,3,32,32]{4,3,2,1,0:T(8,128)(2,1)}, u32[]{:S(2)}) copy-start(bf16[3,3,3,32,32]{4,3,2,1,0:T(8,128)(2,1)} %param.7) | copy-start | bytes 165892
  2.5 7.1 %copy-start.1 = (bf16[3,3,3,32,32]{4,3,2,1,0:T(8,128)(2,1)S(1)}, bf16[3,3,3,32,32]{4,3,2,1,0:T(8,128)(2,1)}, u32[]{:S(2)}) copy-start(bf16[3,3,3,32,32]{4,3,2,1,0:T(8,128)(2,1)} %param.9) | copy-start | bytes 165892
  2.5 14.1 %all-to-all-start = ((bf16[4,2,4,32,128]{4,3,2,1,0:T(8,128)(2,1)}), bf16[4,2,4,32,128]{4,3,2,1,0:T(8,128)(2,1)S(1)}, u32[]{:S(2)}, u32[]{:S(2)}) async-start(bf16[4,2,4,32,128]{4,3,2,1,0:T(8,128)(2,1)} %bitcast.30), calls=%async_computation | async-start | bytes 524288 | tf_op jit(solution)/shard_map/all_to_all | solution.py:242
  16.7 6.4 %collective-permute-start.1 = (bf16[8,3,32,128]{3,2,1,0:T(8,128)(2,1)S(1)}, bf16[8,3,32,128]{3,2,1,0:T(8,128)(2,1)S(1)}, u32[]{:S(2)}, u32[]{:S(2)}) collective-permute-start(bf16[8,3,32,128]{3,2,1,0:T(8,128)(2,1)S(1)} %get-tuple-element.27), channel_id=1, source_target_pairs={{64,0},{128,64},{192,128},{8,192},{72,8},{136,72},{200,136},{16,20... | collective-permute-start | bytes 589832 | tf_op jit(solution)/shard_map/ppermute | solution.py:257
  18.0 6.6 %collective-permute-start = (bf16[8,3,32,128]{3,2,1,0:T(8,128)(2,1)S(1)}, bf16[8,3,32,128]{3,2,1,0:T(8,128)(2,1)S(1)}, u32[]{:S(2)}, u32[]{:S(2)}) collective-permute-start(bf16[8,3,32,128]{3,2,1,0:T(8,128)(2,1)S(1)} %get-tuple-element.28), channel_id=1, source_target_pairs={{0,64},{64,128},{128,192},{192,8},{8,72},{72,136},{136,200},{200,1... | collective-permute-start | bytes 589832 | tf_op jit(solution)/shard_map/ppermute | solution.py:256
  25.4 8.7 %collective-permute-start.3 = (bf16[8,32,128]{2,1,0:T(8,128)(2,1)S(1)}, bf16[8,32,128]{2,1,0:T(8,128)(2,1)S(1)}, u32[]{:S(2)}, u32[]{:S(2)}) collective-permute-start(bf16[8,32,128]{2,1,0:T(8,128)(2,1)S(1)} %get-tuple-element.17), channel_id=1, source_target_pairs={{1,0},{2,1},{3,2},{4,3},{5,4},{6,5},{7,6},{9,8},{10,9},{11,10},{12... | collective-permute-start | bytes 196616 | tf_op jit(solution)/shard_map/ppermute | solution.py:283
  30.7 4.4 %collective-permute-start.2 = (bf16[8,32,128]{2,1,0:T(8,128)(2,1)S(1)}, bf16[8,32,128]{2,1,0:T(8,128)(2,1)S(1)}, u32[]{:S(2)}, u32[]{:S(2)}) collective-permute-start(bf16[8,32,128]{2,1,0:T(8,128)(2,1)S(1)} %get-tuple-element.17), channel_id=1, source_target_pairs={{0,1},{1,2},{2,3},{3,4},{4,5},{5,6},{6,7},{8,9},{9,10},{10,11},{11... | collective-permute-start | bytes 196616 | tf_op jit(solution)/shard_map/ppermute | solution.py:282
  87.9 10.7 %all-to-all-start.1 = ((bf16[4,2,4,32,128]{4,3,2,1,0:T(8,128)(2,1)}), bf16[4,2,4,32,128]{4,3,2,1,0:T(8,128)(2,1)S(1)}, u32[]{:S(2)}, u32[]{:S(2)}) async-start(bf16[4,2,4,32,128]{4,3,2,1,0:T(8,128)(2,1)} %bitcast.10), calls=%async_computation.1 | async-start | bytes 524288 | tf_op jit(solution)/shard_map/all_to_all | solution.py:301
  98.6 20.8 %all-to-all-start.3 = ((bf16[256,2,128]{2,1,0:T(2,128)(2,1)}), bf16[256,2,128]{2,1,0:T(2,128)(2,1)S(1)}, u32[]{:S(2)}, u32[]{:S(2)}) async-start(bf16[256,2,128]{2,1,0:T(2,128)(2,1)} %bitcast.15), calls=%async_computation.3 | async-start | bytes 262144 | tf_op jit(solution)/shard_map/all_to_all | solution.py:316

commit v3 on v2

--- a/solution.py
+++ b/solution.py
@@ -12,6 +12,7 @@
 LH = 1152
 LJ = 896
 LB = 640
+LV = 1024
 F32 = jnp.float32
 BF16 = jnp.bfloat16
 AXES = ("gx", "gy", "gz")
@@ -77,6 +78,12 @@
         )[:, :width].astype(BF16)
 
 
+def blank_ends(ref, planes):
+    blank = jnp.zeros((96, ref.shape[1]), BF16)
+    ref[0:96, :] = blank
+    ref[96 * (planes + 1) : 96 * (planes + 2), :] = blank
+
+
 def window(x):
     return pl.ds(pl.multiple_of(x * 96, 32), 288)
 
@@ -95,18 +102,16 @@
     weight_ref,
     mask_ref,
     jv_ref,
-    sums_ref,
+    volume_all,
+    hidden_all,
+    jv_all,
+    slopes,
     p_vol,
-    p_jv,
-    slopes,
     p_hid,
     p_tan,
 ):
-    for ref, width in ((p_vol, LH), (p_hid, LJ), (p_tan, LJ), (p_jv, LB)):
-        blank = jnp.zeros((96, width), BF16)
-        ref[0:96, :] = blank
-        ref[96 * (planes + 1) : 96 * (planes + 2), :] = blank
-    sums_ref[...] = jnp.zeros_like(sums_ref)
+    for ref in (p_vol, p_hid, p_tan):
+        blank_ends(ref, planes)
     lane = lanes_of((32, 128))
 
     def fill(x, carry):
@@ -120,7 +125,9 @@
             if tile > 0:
                 value = jnp.where((lane >= 8 * tile - 5) & (lane < 8 * tile - 2), right, value)
             tiles.append(value)
-        spread(p_vol, x, jnp.concatenate(tiles, axis=1), LH)
+        value = jnp.concatenate(tiles, axis=1)
+        spread(p_vol, x, value, LH)
+        volume_all[x] = value[:, 256 : 256 + LV].astype(BF16)
         return carry
 
     lax.fori_loop(0, planes, fill, 0)
@@ -131,7 +138,9 @@
         hidden, slope = gelu_pair(fold(product[0:96]))
         tangent = slope * fold(product[96:192])
         slopes[x] = back_by(slope, 2 * PITCH + 2)[:, :LB]
-        spread(p_hid, x, jnp.where(inside, hidden, 0.0), LJ)
+        hidden = jnp.where(inside, hidden, 0.0)
+        hidden_all[x] = hidden[:, 128:].astype(BF16)
+        spread(p_hid, x, hidden, LJ)
         spread(p_tan, x, jnp.where(inside, tangent, 0.0), LJ)
         return carry
 
@@ -143,43 +152,66 @@
         product = product + jnp.dot(weight_ref[288:384, :], near, preferred_element_type=F32)
         jv = fold(product).astype(BF16).astype(F32)
         jv = jnp.where(mask_ref[1:2, :LJ] > 0.0, jv, 0.0)
-        spread(p_jv, x, jv, LB)
+        jv_all[x] = jv.astype(BF16)
         for row in range(4):
             pair = jv[:, 128 * (row + 1) : 128 * (row + 3)]
             jv_ref[x, row] = back_by(pair, 8 * row + 9)[:, :128].astype(BF16)
-        own = jnp.where(mask_ref[2:3, :LJ] > 0.0, jv, 0.0)
-        moved = jnp.concatenate(
-            [own, pltpu.roll(own, 1, 1), pltpu.roll(own, 2, 1), jnp.zeros_like(own)], axis=0
-        )
-        sums_ref[...] += correlate(near[:, 128:768], moved[:, 128:768])
         return carry
 
     lax.fori_loop(0, planes, second, 0)
 
 
-def inward(planes, weight_ref, mask_ref, second_ref, p_vol, p_jv, slopes, packed_ref, sums):
-    sums[...] = jnp.zeros_like(sums)
-
-    def third(x, carry):
+def inward(
+    planes,
+    weight_ref,
+    mask_ref,
+    volume_all,
+    hidden_all,
+    jv_all,
+    slopes,
+    packed_ref,
+    sums_first,
+    sums_second,
+    p_vol,
+    p_hid,
+    p_jv,
+):
+    for ref in (p_vol, p_hid, p_jv):
+        blank_ends(ref, planes)
+    sums_first[...] = jnp.zeros_like(sums_first)
+    sums_second[...] = jnp.zeros_like(sums_second)
+
+    def fill(x, carry):
+        spread(p_vol, x, volume_all[x].astype(F32), LB)
+        spread(p_hid, x, hidden_all[x].astype(F32), LB)
+        spread(p_jv, x, jv_all[x].astype(F32), LB)
+        return carry
+
+    lax.fori_loop(0, planes, fill, 0)
+
+    def sums(x, carry):
+        own = jnp.where(mask_ref[2:3, :LJ] > 0.0, jv_all[x].astype(F32), 0.0)[:, 128:768]
+        moved = [own, pltpu.roll(own, 1, 1), pltpu.roll(own, 2, 1), jnp.zeros_like(own)]
+        sums_second[...] += correlate(p_hid[window(x), :], jnp.concatenate(moved, axis=0))
+
         product = jnp.dot(weight_ref[384:480, :], p_jv[window(x), :], preferred_element_type=F32)
         back = slopes[x] * fold(product)
         back = jnp.where(mask_ref[3:4, :LB] > 0.0, back, 0.0).astype(BF16).astype(F32)
-        moved = jnp.concatenate(
-            [
-                pltpu.roll(back, 19, 1),
-                pltpu.roll(back, 20, 1),
-                jnp.zeros_like(back),
-                pltpu.roll(back, 18, 1),
-            ],
-            axis=0,
-        )
-        sums[...] += correlate(p_vol[window(x), 256:896], moved)
-        return carry
-
-    lax.fori_loop(0, planes, third, 0)
-    packed_ref[0:288, :] = jnp.where(lanes_of((288, 128)) < 96, second_ref[...], sums[...])
+        moved = [
+            pltpu.roll(back, 19, 1),
+            pltpu.roll(back, 20, 1),
+            jnp.zeros_like(back),
+            pltpu.roll(back, 18, 1),
+        ]
+        sums_first[...] += correlate(p_vol[window(x), :], jnp.concatenate(moved, axis=0))
+        return carry
+
+    lax.fori_loop(0, planes, sums, 0)
+    packed_ref[0:288, :] = jnp.where(
+        lanes_of((288, 128)) < 96, sums_second[...], sums_first[...]
+    )
     packed_ref[288:432, :] = jnp.where(
-        lanes_of((144, 128)) < 64, sums[0:144, :], pltpu.roll(sums[144:288, :], 64, 1)
+        lanes_of((144, 128)) < 64, sums_first[0:144, :], pltpu.roll(sums_first[144:288, :], 64, 1)
     )
     packed_ref[432:512, :] = jnp.zeros((80, 128), F32)
 
@@ -258,7 +290,7 @@
 
     vmem = pl.BlockSpec(memory_space=pltpu.VMEM)
 
-    def call(kernel, operands, outputs, scratch, name, limit):
+    def call(kernel, operands, outputs, scratch, name, limit, flops):
         return pl.pallas_call(
             kernel,
             out_shape=tuple(jax.ShapeDtypeStruct(shape, dtype) for shape, dtype in outputs),
@@ -266,6 +298,7 @@
             out_specs=(vmem,) * len(outputs),
             scratch_shapes=[pltpu.VMEM(shape, dtype) for shape, dtype in scratch],
             compiler_params=pltpu.CompilerParams(vmem_limit_bytes=limit << 20),
+            cost_estimate=pl.CostEstimate(flops=flops, bytes_accessed=1 << 20, transcendentals=0),
             name=name,
         )(*operands)
 
@@ -276,6 +309,7 @@
         [],
         "assemble",
         8,
+        10**8,
     )
 
     ends = [(i, i + 1) for i in range(n_gz - 1)]
@@ -283,36 +317,41 @@
     right = lax.ppermute(strip, "gz", [(b, a) for a, b in ends])
 
     stack = 96 * (planes + 2)
-    jv, second, p_vol, p_jv, slopes = call(
+    jv, volume_all, hidden_all, jv_all, slopes = call(
         lambda *refs: outward(planes, *refs),
         (field, left, right, weights, masks),
         [
             ((planes, rows, channels, width), BF16),
-            ((288, 128), F32),
-            ((stack, LH), BF16),
-            ((stack, LB), BF16),
+            ((planes, channels, LV), BF16),
+            ((planes, channels, LV), BF16),
+            ((planes, channels, LJ), BF16),
             ((planes, channels, LB), F32),
         ],
-        [((stack, LJ), BF16), ((stack, LJ), BF16)],
+        [((stack, LH), BF16), ((stack, LJ), BF16), ((stack, LJ), BF16)],
         "outward",
         24,
+        6 * 10**9,
     )
 
     home = lax.all_to_all(jv.reshape(n_gx, depth, rows, channels, width), "gx", 0, 0)
-    out = jnp.transpose(home, (3, 1, 0, 2, 4)).reshape(channels, depth, height, width)
 
     (packed,) = call(
         lambda *refs: inward(planes, *refs),
-        (weights, masks, second, p_vol, p_jv, slopes),
+        (weights, masks, volume_all, hidden_all, jv_all, slopes),
         [((512, 128), F32)],
-        [((288, 128), F32)],
+        [((288, 128), F32)] * 2 + [((stack, LB), BF16)] * 3,
         "inward",
         24,
-    )
+        3 * 10**9,
+    )
+
+    packed, home = lax.optimization_barrier((packed, home))
+
+    out = jnp.transpose(home, (3, 1, 0, 2, 4)).reshape(channels, depth, height, width)
 
     count = lax.axis_size(AXES)
     parts = lax.all_to_all(packed.reshape(count, 2, 128), AXES, 0, 0).reshape(512, 128)
-    (every,) = call(combine, (parts,), [((512, 128), BF16)], [], "combine", 4)
+    (every,) = call(combine, (parts,), [((512, 128), BF16)], [], "combine", 4, 10**8)
     every = lax.all_to_all(every.reshape(count, 2, 128), AXES, 0, 0).reshape(512, 128)
     gv_first, gv_second = call(
         lambda *refs: finish(factor, count_all, *refs),
@@ -321,6 +360,7 @@
         [],
         "finish",
         8,
+        10**8,
     )
     return (out, gv_first.reshape(v_first.shape), gv_second.reshape(v_first.shape))
 

time: 122 us -> 116 us (0.951)
  waiting for transfers between devices: 27.9 us -> 21.4 us
  blocking collectives: 33.3 us -> 31.5 us
  local copies, waits for them, and re-layouts: 4.92 us -> 6.71 us
    all_to_all x1, waiting for transfers between devices: 6.53 us -> 0.01 us  [body(): lax.all_to_all(jv.reshape(n_gx, depth, rows, channels, width), 'gx', 0, 0)]
    all_to_all x1, starting transfers between devices: 3.41 us -> 5.78 us  [body(): lax.all_to_all(jv.reshape(n_gx, depth, rows, channels, width), 'gx', 0, 0)]
    all_to_all x1, starting transfers between devices: 7.53 us -> 5.49 us  [body(): lax.all_to_all(every.reshape(count, 2, 128), AXES, 0, 0).reshape(512, 128)]
    all_to_all x1, blocking collectives: 33.3 us -> 31.5 us  [body(): lax.all_to_all(packed.reshape(count, 2, 128), AXES, 0, 0).reshape(512, 128)]
    unnamed x13 -> x17, local copies, waits for them, and re-layouts: 0.28 us -> 2.07 us
  transfers between devices with their start and end apart: 7 -> 7, of which waited for: 6 -> 5; matrix products, arithmetic and copies ran while one was open for 3% -> 3% of each run, Pallas kernels for 1% -> 7%
where the time goes in v3:
time: 116 us; the launch traced here: 115 us
  starting transfers between devices  31.6 us (27%)
  blocking collectives  31.5 us (27%)
  Pallas kernels  23 us (20%)
  waiting for transfers between devices  21.4 us (18%)
  local copies, waits for them, and re-layouts  6.71 us (6%)
    all_to_all x1, blocking collectives, body(): lax.all_to_all(packed.reshape(count, 2, 128), AXES, 0, 0).reshape(512, 128)  31.5 us
    pallas_call x5, Pallas kernels, call(): pl.pallas_call(kernel, out_shape=tuple((jax.ShapeDtypeStruct(shape, dtype...  23 us
    all_to_all x1, waiting for transfers between devices, body(): lax.all_to_all(every.reshape(count, 2, 128), AXES, 0, 0).reshape(512, 128)  12.4 us
    all_to_all x1, starting transfers between devices, body(): lax.all_to_all(split, 'gx', 0, 0).reshape(planes, rows, channels, width)  6.56 us
    all_to_all x1, starting transfers between devices, body(): lax.all_to_all(jv.reshape(n_gx, depth, rows, channels, width), 'gx', 0, 0)  5.78 us
    all_to_all x1, starting transfers between devices, body(): lax.all_to_all(every.reshape(count, 2, 128), AXES, 0, 0).reshape(512, 128)  5.49 us
    all_to_all x1, waiting for transfers between devices, body(): lax.all_to_all(split, 'gx', 0, 0).reshape(planes, rows, channels, width)  5.36 us
    ppermute x1, starting transfers between devices, body(): right = lax.ppermute(strip, 'gz', [(b, a) for a, b in ends])  5.34 us
  transfers between devices with their start and end apart: 7, of which 5 were waited for; matrix products, arithmetic and copies ran while one was open for 3% of the time, Pallas kernels for 7%

profile of v3, /device:TPU:1, one launch (start us, length us, event | category | flops | bytes accessed | tf_op | source)
XLA Modules:
  0.0 115.1 jit_solution(15393636669888541843)
XLA Ops:
  0.6 0.0 copy-start.5
  0.6 0.0 copy-start
  0.7 0.0 copy-start.4
  0.7 1.8 %copy.19 = bf16[32,2,4,4,128]{4,0,3,1,2:T(8,128)(2,1)} copy(bf16[32,2,4,4,128]{4,3,2,1,0:T(4,128)(2,1)} %bitcast.40) | data formatting | bytes 524288 | tf_op jit(solution)/shard_map/reshape | solution.py:273
  2.5 0.0 copy-start.1
  2.5 6.6 %all-to-all-start = ((bf16[4,2,4,32,128]{4,3,2,1,0:T(8,128)(2,1)}), bf16[4,2,4,32,128]{4,3,2,1,0:T(8,128)(2,1)S(1)}, u32[]{:S(2)}, u32[]{:S(2)}) async-start(bf16[4,2,4,32,128]{4,3,2,1,0:T(8,128)(2,1)} %bitcast.30), calls=%async_computation | async-start | bytes 524288 | tf_op jit(solution)/shard_map/all_to_all | solution.py:274
  9.1 0.0 copy-done.5
  9.1 0.0 copy-done
  9.2 0.0 copy-done.4
  9.2 0.1 compare_and_fusion.2
  9.3 0.2 copy.13
  9.5 0.1 stack.29
  9.6 0.0 copy-done.1
  9.6 0.8 copy.14
  10.4 0.8 reshape.210
  11.3 5.4 %all-to-all-done = bf16[4,2,4,32,128]{4,3,2,1,0:T(8,128)(2,1)S(1)} async-done(((bf16[4,2,4,32,128]{4,3,2,1,0:T(8,128)(2,1)}), bf16[4,2,4,32,128]{4,3,2,1,0:T(8,128)(2,1)S(1)}, u32[]{:S(2)}, u32[]{:S(2)}) %all-to-all-start) | async-done | bytes 262176 | tf_op jit(solution)/shard_map/all_to_all | solution.py:274
  16.7 1.3 %collective-permute-start.1 = (bf16[8,3,32,128]{3,2,1,0:T(8,128)(2,1)S(1)}, bf16[8,3,32,128]{3,2,1,0:T(8,128)(2,1)S(1)}, u32[]{:S(2)}, u32[]{:S(2)}) collective-permute-start(bf16[8,3,32,128]{3,2,1,0:T(8,128)(2,1)S(1)} %get-tuple-element.31), channel_id=1, source_target_pairs={{64,0},{128,64},{192,128},{8,192},{72,8},{136,72},{200,136},{16,20... | collective-permute-start | bytes 589832 | tf_op jit(solution)/shard_map/ppermute | solution.py:289
  18.0 4.0 %collective-permute-start = (bf16[8,3,32,128]{3,2,1,0:T(8,128)(2,1)S(1)}, bf16[8,3,32,128]{3,2,1,0:T(8,128)(2,1)S(1)}, u32[]{:S(2)}, u32[]{:S(2)}) collective-permute-start(bf16[8,3,32,128]{3,2,1,0:T(8,128)(2,1)S(1)} %get-tuple-element.32), channel_id=1, source_target_pairs={{0,64},{64,128},{128,192},{192,8},{8,72},{72,136},{136,200},{200,1... | collective-permute-start | bytes 589832 | tf_op jit(solution)/shard_map/ppermute | solution.py:288
  22.0 1.1 collective-permute-done.1.refs_2_
  23.1 1.5 %collective-permute-done.refs_1_ = bf16[8,3,32,128]{3,2,1,0:T(8,128)(2,1)S(1)} collective-permute-done((bf16[8,3,32,128]{3,2,1,0:T(8,128)(2,1)S(1)}, bf16[8,3,32,128]{3,2,1,0:T(8,128)(2,1)S(1)}, u32[]{:S(2)}, u32[]{:S(2)}) %collective-permute-start) | collective-permute-done | bytes 196640 | tf_op jit(solution)/shard_map/ppermute | solution.py:288
  24.6 0.8 assemble.1
  25.4 5.3 %collective-permute-start.3 = (bf16[8,32,128]{2,1,0:T(8,128)(2,1)S(1)}, bf16[8,32,128]{2,1,0:T(8,128)(2,1)S(1)}, u32[]{:S(2)}, u32[]{:S(2)}) collective-permute-start(bf16[8,32,128]{2,1,0:T(8,128)(2,1)S(1)} %get-tuple-element.21), channel_id=1, source_target_pairs={{1,0},{2,1},{3,2},{4,3},{5,4},{6,5},{7,6},{9,8},{10,9},{11,10},{12... | collective-permute-start | bytes 196616 | tf_op jit(solution)/shard_map/ppermute | solution.py:317
  30.7 3.1 %collective-permute-start.2 = (bf16[8,32,128]{2,1,0:T(8,128)(2,1)S(1)}, bf16[8,32,128]{2,1,0:T(8,128)(2,1)S(1)}, u32[]{:S(2)}, u32[]{:S(2)}) collective-permute-start(bf16[8,32,128]{2,1,0:T(8,128)(2,1)S(1)} %get-tuple-element.21), channel_id=1, source_target_pairs={{0,1},{1,2},{2,3},{3,4},{4,5},{5,6},{6,7},{8,9},{9,10},{10,11},{11... | collective-permute-start | bytes 196616 | tf_op jit(solution)/shard_map/ppermute | solution.py:316
  33.9 0.2 copy.16.refs_3_.refs_0_
  34.1 0.0 collective-permute-done.3.refs_2_
  34.1 1.1 collective-permute-done.2.refs_1_
  35.2 11.0 %outward.1 = (bf16[8,4,32,128]{3,2,1,0:T(8,128)(2,1)}, bf16[8,32,1024]{2,1,0:T(8,128)(2,1)S(1)}, bf16[8,32,1024]{2,1,0:T(8,128)(2,1)S(1)}, bf16[8,32,896]{2,1,0:T(8,128)(2,1)S(1)}, f32[8,32,640]{2,1,0:T(8,128)S(1)}) custom-call(bf16[8,32,1408]{2,1,0:T(8,128)(2,1)S(1)} %get-tuple-element.20.refs_0_, bf16[8,32,128]{2,1,0:T(8,128)(2,1)S(1)} %collective-permute-done.2.refs_1_, ...), custom_call_target="tpu_custom_call" | custom-call | flops 6000000000 | bytes 1048576 | tf_op jit(solution)/shard_map/outward/pallas_call | solution.py:294
  46.2 0.0 copy-start.2
  46.2 0.8 copy-done.2
  46.9 5.8 %all-to-all-start.1 = ((bf16[4,2,4,32,128]{4,3,2,1,0:T(8,128)(2,1)}), bf16[4,2,4,32,128]{4,3,2,1,0:T(8,128)(2,1)S(1)}, u32[]{:S(2)}, u32[]{:S(2)}) async-start(bf16[4,2,4,32,128]{4,3,2,1,0:T(8,128)(2,1)} %bitcast.10), calls=%async_computation.1 | async-start | bytes 524288 | tf_op jit(solution)/shard_map/all_to_all | solution.py:336
  52.7 0.0 copy-start.3
  52.7 1.0 copy-done.3
  53.7 7.8 %inward.1 = f32[512,128]{1,0:T(8,128)S(1)} custom-call(bf16[480,288]{1,0:T(8,128)(2,1)S(1)} %copy.16.refs_3_.refs_0_, f32[8,1152]{1,0:T(8,128)S(1)} %convert_element_type.3.refs_4_.refs_1_, bf16[8,32,1024]{2,1,0:T(8,128)(2,1)S(1)} %get-tuple-element.22.refs_2_, bf16[8,32,1024]{2,1,0:T(8,128)(2,1)S(1)} %get-tuple-element.23.refs_3_, ...), custom_call_target="tpu_custom_call" | custom-call | flops 3000000000 | bytes 1048576 | tf_op jit(solution)/shard_map/inward/pallas_call | solution.py:294
  61.5 0.0 all-to-all-done.1
  61.5 31.5 %all_to_all.20 = f32[256,2,128]{2,1,0:T(2,128)S(1)} all-to-all(f32[256,2,128]{2,1,0:T(2,128)S(1)} %bitcast.37), channel_id=1, replica_groups=mesh['gx'=4,'gy'=8,'gz'=8] {'gx','gy','gz'}, dimensions={0} | all-to-all | bytes 524288 | tf_op jit(solution)/shard_map/all_to_all | solution.py:353
  93.0 0.7 combine.1
  93.7 5.5 %all-to-all-start.3 = ((bf16[256,2,128]{2,1,0:T(2,128)(2,1)}), bf16[256,2,128]{2,1,0:T(2,128)(2,1)S(1)}, u32[]{:S(2)}, u32[]{:S(2)}) async-start(bf16[256,2,128]{2,1,0:T(2,128)(2,1)} %bitcast.15), calls=%async_computation.3 | async-start | bytes 262144 | tf_op jit(solution)/shard_map/all_to_all | solution.py:355
  99.2 0.8 copy.17
  100.1 12.4 %all-to-all-done.3 = bf16[256,2,128]{2,1,0:T(2,128)(2,1)S(1)} async-done(((bf16[256,2,128]{2,1,0:T(2,128)(2,1)}), bf16[256,2,128]{2,1,0:T(2,128)(2,1)S(1)}, u32[]{:S(2)}, u32[]{:S(2)}) %all-to-all-start.3) | async-done | bytes 131104 | tf_op jit(solution)/shard_map/all_to_all | solution.py:355
  112.5 2.7 %finish.1 = (f32[27,32,32]{2,1,0:T(8,128)}, f32[27,32,32]{2,1,0:T(8,128)}) custom-call(bf16[512,128]{1,0:T(8,128)(2,1)S(1)} %bitcast.36, bf16[27,32,32]{2,1,0:T(8,128)(2,1)S(1)} %bitcast.34, bf16[27,32,32]{2,1,0:T(8,128)(2,1)S(1)} %bitcast.35), custom_call_target="tpu_custom_call" | custom-call | flops 100000000 | bytes 1048576 | tf_op jit(solution)/shard_map/finish/pallas_call | solution.py:294
  (9 shorter events, 0.2 us)
Async XLA Ops:
  0.6 8.5 %copy-start.5 = (bf16[3,3,3,32,32]{4,3,2,1,0:T(8,128)(2,1)S(1)}, bf16[3,3,3,32,32]{4,3,2,1,0:T(8,128)(2,1)}, u32[]{:S(2)}) copy-start(bf16[3,3,3,32,32]{4,3,2,1,0:T(8,128)(2,1)} %param.6) | copy-start | bytes 165892
  0.6 8.5 %copy-start = (bf16[3,3,3,32,32]{4,3,2,1,0:T(8,128)(2,1)S(1)}, bf16[3,3,3,32,32]{4,3,2,1,0:T(8,128)(2,1)}, u32[]{:S(2)}) copy-start(bf16[3,3,3,32,32]{4,3,2,1,0:T(8,128)(2,1)} %param.8) | copy-start | bytes 165892
  0.7 8.5 %copy-start.4 = (bf16[3,3,3,32,32]{4,3,2,1,0:T(8,128)(2,1)S(1)}, bf16[3,3,3,32,32]{4,3,2,1,0:T(8,128)(2,1)}, u32[]{:S(2)}) copy-start(bf16[3,3,3,32,32]{4,3,2,1,0:T(8,128)(2,1)} %param.7) | copy-start | bytes 165892
  2.5 7.1 %copy-start.1 = (bf16[3,3,3,32,32]{4,3,2,1,0:T(8,128)(2,1)S(1)}, bf16[3,3,3,32,32]{4,3,2,1,0:T(8,128)(2,1)}, u32[]{:S(2)}) copy-start(bf16[3,3,3,32,32]{4,3,2,1,0:T(8,128)(2,1)} %param.9) | copy-start | bytes 165892
  2.5 14.1 %all-to-all-start = ((bf16[4,2,4,32,128]{4,3,2,1,0:T(8,128)(2,1)}), bf16[4,2,4,32,128]{4,3,2,1,0:T(8,128)(2,1)S(1)}, u32[]{:S(2)}, u32[]{:S(2)}) async-start(bf16[4,2,4,32,128]{4,3,2,1,0:T(8,128)(2,1)} %bitcast.30), calls=%async_computation | async-start | bytes 524288 | tf_op jit(solution)/shard_map/all_to_all | solution.py:274
  16.7 6.4 %collective-permute-start.1 = (bf16[8,3,32,128]{3,2,1,0:T(8,128)(2,1)S(1)}, bf16[8,3,32,128]{3,2,1,0:T(8,128)(2,1)S(1)}, u32[]{:S(2)}, u32[]{:S(2)}) collective-permute-start(bf16[8,3,32,128]{3,2,1,0:T(8,128)(2,1)S(1)} %get-tuple-element.31), channel_id=1, source_target_pairs={{64,0},{128,64},{192,128},{8,192},{72,8},{136,72},{200,136},{16,20... | collective-permute-start | bytes 589832 | tf_op jit(solution)/shard_map/ppermute | solution.py:289
  18.0 6.6 %collective-permute-start = (bf16[8,3,32,128]{3,2,1,0:T(8,128)(2,1)S(1)}, bf16[8,3,32,128]{3,2,1,0:T(8,128)(2,1)S(1)}, u32[]{:S(2)}, u32[]{:S(2)}) collective-permute-start(bf16[8,3,32,128]{3,2,1,0:T(8,128)(2,1)S(1)} %get-tuple-element.32), channel_id=1, source_target_pairs={{0,64},{64,128},{128,192},{192,8},{8,72},{72,136},{136,200},{200,1... | collective-permute-start | bytes 589832 | tf_op jit(solution)/shard_map/ppermute | solution.py:288
  25.4 8.7 %collective-permute-start.3 = (bf16[8,32,128]{2,1,0:T(8,128)(2,1)S(1)}, bf16[8,32,128]{2,1,0:T(8,128)(2,1)S(1)}, u32[]{:S(2)}, u32[]{:S(2)}) collective-permute-start(bf16[8,32,128]{2,1,0:T(8,128)(2,1)S(1)} %get-tuple-element.21), channel_id=1, source_target_pairs={{1,0},{2,1},{3,2},{4,3},{5,4},{6,5},{7,6},{9,8},{10,9},{11,10},{12... | collective-permute-start | bytes 196616 | tf_op jit(solution)/shard_map/ppermute | solution.py:317
  30.7 4.4 %collective-permute-start.2 = (bf16[8,32,128]{2,1,0:T(8,128)(2,1)S(1)}, bf16[8,32,128]{2,1,0:T(8,128)(2,1)S(1)}, u32[]{:S(2)}, u32[]{:S(2)}) collective-permute-start(bf16[8,32,128]{2,1,0:T(8,128)(2,1)S(1)} %get-tuple-element.21), channel_id=1, source_target_pairs={{0,1},{1,2},{2,3},{3,4},{4,5},{5,6},{6,7},{8,9},{9,10},{10,11},{11... | collective-permute-start | bytes 196616 | tf_op jit(solution)/shard_map/ppermute | solution.py:316
  46.2 0.8 copy-start.2
  46.9 14.6 %all-to-all-start.1 = ((bf16[4,2,4,32,128]{4,3,2,1,0:T(8,128)(2,1)}), bf16[4,2,4,32,128]{4,3,2,1,0:T(8,128)(2,1)S(1)}, u32[]{:S(2)}, u32[]{:S(2)}) async-start(bf16[4,2,4,32,128]{4,3,2,1,0:T(8,128)(2,1)} %bitcast.10), calls=%async_computation.1 | async-start | bytes 524288 | tf_op jit(solution)/shard_map/all_to_all | solution.py:336
  52.7 1.0 copy-start.3
  93.7 18.7 %all-to-all-start.3 = ((bf16[256,2,128]{2,1,0:T(2,128)(2,1)}), bf16[256,2,128]{2,1,0:T(2,128)(2,1)S(1)}, u32[]{:S(2)}, u32[]{:S(2)}) async-start(bf16[256,2,128]{2,1,0:T(2,128)(2,1)} %bitcast.15), calls=%async_computation.3 | async-start | bytes 262144 | tf_op jit(solution)/shard_map/all_to_all | solution.py:355

commit v4 on v0

v4 whole, which is shorter than its diff:
```python
import math

import jax
import jax.numpy as jnp
from jax import lax
from jax.experimental import pallas as pl
from jax.experimental.pallas import tpu as pltpu
from jax.sharding import PartitionSpec as P

F32 = jnp.float32
BF16 = jnp.bfloat16
AXES = ("gx", "gy", "gz")
GROUP = ("gx", "gy")
PLANES = 8
OWN = 4
MEMBERS = 32


def lanes_of(shape):
    return lax.broadcasted_iota(jnp.int32, shape, len(shape) - 1)


def exchange(tiles, bits):
    tiles = list(tiles)
    lane = lanes_of(tiles[0].shape)
    for place, bit in enumerate(bits):
        step = 1 << bit
        clear = (lane & step) == 0
        for low in range(len(tiles)):
            if low & (1 << place):
                continue
            high = low | (1 << place)
            a, b = tiles[low], tiles[high]
            tiles[low] = jnp.where(clear, a, pltpu.roll(b, step, 1))
            tiles[high] = jnp.where(clear, pltpu.roll(a, 128 - step, 1), b)
    return tiles


def permutation(inverse):
    source = lax.broadcasted_iota(jnp.int32, (128, 128), 0)
    target = lax.broadcasted_iota(jnp.int32, (128, 128), 1)
    if inverse:
        source, target = target, source
    hit = source == 4 * (target & 31) + (target >> 5)
    return jnp.where(hit, 1.0, 0.0).astype(BF16)


def pack(cells_ref, out_ref, sorted_ref):
    moved = jnp.dot(cells_ref[...].reshape(1024, 128), permutation(False), preferred_element_type=F32)
    sorted_ref[...] = moved.reshape(32, 32, 128)
    for part in range(2):
        at = slice(16 * part, 16 * part + 16)
        tiles = exchange([sorted_ref[i, at] for i in range(32)], (0, 1, 2, 3, 4))
        for member in range(MEMBERS):
            out_ref[member, at] = tiles[member].astype(BF16)


def arrange(parts_ref, own_ref):
    for g in range(4):
        tiles = exchange([parts_ref[8 * g + j].astype(F32) for j in range(8)], (4, 5, 6))
        for i in range(8):
            plane = 2 * g + i % 2
            own_ref[i // 2, 32 * plane : 32 * plane + 32] = tiles[i].astype(BF16)


def unpack(parts_ref, out_ref, mixed_ref):
    for part in range(2):
        at = slice(16 * part, 16 * part + 16)
        tiles = exchange([parts_ref[i, at].astype(F32) for i in range(MEMBERS)], (0, 1, 2, 3, 4))
        for i in range(32):
            mixed_ref[i, at] = tiles[i].astype(BF16)
    moved = jnp.dot(mixed_ref[...].reshape(1024, 128), permutation(True), preferred_element_type=F32)
    out_ref[...] = moved.astype(BF16).reshape(2, 16, 32, 128)


def gelu_pair(pre):
    inner = 0.7978845608 * (pre + 0.044715 * pre * pre * pre)
    hyper = jnp.tanh(inner)
    hidden = 0.5 * pre * (1.0 + hyper)
    slope = 0.5 * (1.0 + hyper) + 0.5 * pre * (1.0 - hyper * hyper) * 0.7978845608 * (
        1.0 + 0.134145 * pre * pre
    )
    return hidden, slope


def before(value):
    return jnp.where(lanes_of(value.shape) > 0, pltpu.roll(value, 1, 1), 0.0)


def after(value):
    return jnp.where(lanes_of(value.shape) < 127, pltpu.roll(value, 127, 1), 0.0)


def fold(product):
    return before(product[0:32]) + product[32:64] + after(product[64:96])


def near(ref, z, x):
    return jnp.concatenate(
        [
            jnp.concatenate([ref[z + at + offset, 32 * x : 32 * x + 96] for offset in range(3)], axis=0)
            for at in range(2)
        ],
        axis=1,
    )


def tile_of(x):
    return slice(32 * x + 32, 32 * x + 64)


def correlate(ref, z, targets):
    rows = jnp.concatenate([near(ref, z, x) for x in range(PLANES)], axis=1)
    return lax.dot_general(
        rows,
        jnp.concatenate(targets, axis=1),
        (((1,), (1,)), ((), ())),
        preferred_element_type=F32,
    )


def layers(
    own_ref,
    left_ref,
    right_ref,
    weight_ref,
    mask_ref,
    out_ref,
    p_vol,
    p_hid,
    p_tan,
    p_jv,
    slopes,
    sums_first,
    sums_second,
    packed,
):
    blank = jnp.zeros((32, 128), BF16)
    for ref, count in ((p_vol, 10), (p_hid, 8), (p_tan, 8), (p_jv, 6)):
        for z in range(count):
            ref[z, 0:32] = blank
            ref[z, 288:320] = blank
    for z in range(3):
        p_vol[z, 32:288] = left_ref[z]
        p_vol[7 + z, 32:288] = right_ref[z]
    for z in range(OWN):
        p_vol[3 + z, 32:288] = own_ref[z]
    sums_first[...] = jnp.zeros_like(sums_first)
    sums_second[...] = jnp.zeros_like(sums_second)

    def first(step, carry):
        z = 2 * step
        for x in range(PLANES):
            product = jnp.dot(weight_ref[0:192, :], near(p_vol, z, x), preferred_element_type=F32)
            for at in range(2):
                part = product[:, 128 * at : 128 * at + 128]
                inside = mask_ref[z + at] > 0.0
                hidden, slope = gelu_pair(fold(part[0:96]))
                tangent = slope * fold(part[96:192])
                p_hid[z + at, tile_of(x)] = jnp.where(inside, hidden, 0.0).astype(BF16)
                p_tan[z + at, tile_of(x)] = jnp.where(inside, tangent, 0.0).astype(BF16)
                slopes[z + at, x] = slope
        return carry

    lax.fori_loop(0, 4, first, 0)

    def second(step, carry):
        z = 2 * step
        for x in range(PLANES):
            product = jnp.dot(weight_ref[192:288, :], near(p_tan, z, x), preferred_element_type=F32)
            product = product + jnp.dot(
                weight_ref[288:384, :], near(p_hid, z, x), preferred_element_type=F32
            )
            for at in range(2):
                jv = fold(product[:, 128 * at : 128 * at + 128])
                jv = jnp.where(mask_ref[8 + z + at] > 0.0, jv, 0.0)
                p_jv[z + at, tile_of(x)] = jv.astype(BF16)
        return carry

    lax.fori_loop(0, 3, second, 0)

    def spread(tiles):
        both = [
            jnp.concatenate(
                [after(tile), tile, before(tile), jnp.zeros_like(tile)], axis=0
            )
            for tile in tiles
        ]
        return jnp.concatenate(both, axis=1).astype(BF16)

    def third(step, carry):
        z = 2 * step
        targets = [
            spread([p_jv[z + at + 1, tile_of(x)].astype(F32) for at in range(2)])
            for x in range(PLANES)
        ]
        sums_second[...] += correlate(p_hid.at[pl.ds(1, 6)], z, targets)
        targets = []
        for x in range(PLANES):
            product = jnp.dot(weight_ref[384:480, :], near(p_jv, z, x), preferred_element_type=F32)
            tiles = []
            for at in range(2):
                back = slopes[z + at + 2, x] * fold(product[:, 128 * at : 128 * at + 128])
                tiles.append(back.astype(BF16).astype(F32))
            targets.append(spread(tiles))
        sums_first[...] += correlate(p_vol.at[pl.ds(2, 6)], z, targets)
        return carry

    lax.fori_loop(0, 2, third, 0)

    for g in range(4):
        tiles = [p_jv[1 + i // 2, tile_of(2 * g + i % 2)].astype(F32) for i in range(8)]
        tiles = exchange(tiles, (4, 5, 6))
        for j in range(8):
            out_ref[8 * g + j, 0:32] = tiles[j].astype(BF16)

    low = jnp.where(
        lanes_of((288, 128)) < 96, sums_second[...], pltpu.roll(sums_first[...], 96, 1)
    )
    rest = pltpu.roll(sums_first[...], 96, 1)
    packed[0:288] = low
    packed[288:432] = jnp.where(
        lanes_of((144, 128)) < 64, rest[0:144], pltpu.roll(rest[144:288], 64, 1)
    )
    packed[432:512] = jnp.zeros((80, 128), F32)
    for member in range(MEMBERS):
        rows = packed[16 * member : 16 * member + 16]
        high = rows.astype(BF16)
        out_ref[member, 32:48] = high
        out_ref[member, 48:64] = (rows - high.astype(F32)).astype(BF16)


def gather_sums(parts_ref, out_ref):
    total = jnp.sum(
        parts_ref[:, 32:48].astype(F32) + parts_ref[:, 48:64].astype(F32), axis=0
    )
    for member in range(8):
        out_ref[member] = total


def combine(parts_ref, out_ref):
    total = jnp.sum(parts_ref[...], axis=0).astype(BF16)
    for member in range(MEMBERS):
        out_ref[member] = total


def finish(factor, count_all, packed_ref, v_first_ref, v_second_ref, first_ref, second_ref):
    def damped(summed, direction):
        return factor * (summed / count_all + 0.1 * direction.astype(F32))

    rest = packed_ref[288:432, :].astype(F32)
    rest = jnp.concatenate([rest, pltpu.roll(rest, 64, 1)], axis=0)
    for block in range(9):
        low = packed_ref[32 * block : 32 * block + 32, :].astype(F32)
        far = rest[32 * block : 32 * block + 32]
        at = [9 * (block % 3) + 3 * row + block // 3 for row in range(3)]
        for row in range(3):
            second_ref[at[row]] = damped(low[:, 32 * row : 32 * row + 32], v_second_ref[at[row]])
        first_ref[at[0]] = damped(low[:, 96:128], v_first_ref[at[0]])
        first_ref[at[1]] = damped(far[:, 0:32], v_first_ref[at[1]])
        first_ref[at[2]] = damped(far[:, 32:64], v_first_ref[at[2]])


def cell_masks(column, width):
    at = jnp.concatenate([jnp.arange(8) - 2, jnp.arange(8) - 1]).astype(jnp.int32) + column
    inside = (at >= 0) & (at < width)
    return jnp.broadcast_to(inside[:, None, None], (16, 32, 128)).astype(F32)


def filters(w_first, v_first, w_second, v_second):
    flipped = jnp.transpose(jnp.flip(w_second, (0, 1, 2)), (0, 1, 2, 4, 3))
    stacked = jnp.stack([w_first, v_first, w_second, v_second, flipped])
    return jnp.transpose(stacked, (0, 2, 5, 3, 1, 4)).reshape(480, 288)


def call(kernel, operands, outputs, scratch, name, limit, flops):
    vmem = pl.BlockSpec(memory_space=pltpu.VMEM)
    return pl.pallas_call(
        kernel,
        out_shape=tuple(jax.ShapeDtypeStruct(shape, dtype) for shape, dtype in outputs),
        in_specs=[vmem] * len(operands),
        out_specs=(vmem,) * len(outputs),
        scratch_shapes=[pltpu.VMEM(shape, dtype) for shape, dtype in scratch],
        compiler_params=pltpu.CompilerParams(vmem_limit_bytes=limit << 20),
        cost_estimate=pl.CostEstimate(flops=flops, bytes_accessed=1 << 20, transcendentals=0),
        name=name,
    )(*operands)


def body(volume, w_first, w_second, v_first, v_second):
    channels, depth, height, width = volume.shape
    n_gx, n_gy, n_gz = (lax.axis_size(axis) for axis in AXES)
    members = n_gx * n_gy
    count_all = float(depth * n_gx * height * n_gy * width * n_gz)
    factor = math.sqrt(27.0 * channels)
    small = (channels, 128)

    cells = jnp.transpose(volume, (1, 2, 0, 3))
    (sent,) = call(pack, (cells,), [((members,) + small, BF16)], [((32,) + small, F32)], "pack", 8, 10**8)
    parts = lax.all_to_all(sent, GROUP, 0, 0)

    block = lax.axis_index("gz") * members + lax.axis_index("gx") * n_gy + lax.axis_index("gy")
    masks = cell_masks(OWN * block, width * n_gz)
    weights = filters(w_first, v_first, w_second, v_second)
    parts, masks, weights = lax.optimization_barrier((parts, masks, weights))

    (own,) = call(arrange, (parts,), [((OWN, 256, 128), BF16)], [], "arrange", 8, 10**8)

    def device(at):
        return (at % members) * n_gz + at // members

    onward = [(device(i), device(i + 1)) for i in range(members * n_gz - 1)]
    left = lax.ppermute(own[1:], AXES, onward)
    right = lax.ppermute(own[:3], AXES, [(b, a) for a, b in onward])

    (leaving,) = call(
        layers,
        (own, left, right, weights, masks),
        [((members, 64, 128), BF16)],
        [
            ((10, 320, 128), BF16),
            ((8, 320, 128), BF16),
            ((8, 320, 128), BF16),
            ((6, 320, 128), BF16),
            ((8, PLANES) + small, F32),
            ((288, 128), F32),
            ((288, 128), F32),
            ((512, 128), F32),
        ],
        "layers",
        24,
        8 * 10**9,
    )

    parts = lax.all_to_all(leaving, GROUP, 0, 0)
    (sums,) = call(gather_sums, (parts,), [((n_gz, 16, 128), F32)], [], "gather_sums", 8, 10**8)
    sums = lax.all_to_all(sums, "gz", 0, 0)
    (every,) = call(combine, (sums,), [((members, 16, 128), BF16)], [], "combine", 8, 10**8)
    every = lax.all_to_all(every, GROUP, 0, 0).reshape(512, 128)
    (home,) = call(
        unpack,
        (parts,),
        [((depth, height) + small, BF16)],
        [((32,) + small, BF16)],
        "unpack",
        8,
        10**9,
    )
    out = jnp.transpose(home, (2, 0, 1, 3))
    gv_first, gv_second = call(
        lambda *refs: finish(factor, count_all, *refs),
        (every, v_first.reshape(27, channels, channels), v_second.reshape(27, channels, channels)),
        [((27, channels, channels), F32)] * 2,
        [],
        "finish",
        8,
        10**8,
    )
    return (out, gv_first.reshape(v_first.shape), gv_second.reshape(v_first.shape))


def solution(mesh):
    in_specs = (P(None, "gx", "gy", "gz"), P(), P(), P(), P())
    out_specs = (P(None, "gx", "gy", "gz"), P(), P())
    return jax.shard_map(body, mesh=mesh, in_specs=in_specs, out_specs=out_specs, check_vma=False)
```

time: 446 us -> 113 us (0.25)
  waiting for transfers between devices: 292 us -> 19.9 us
  blocking collectives: 0 us -> 48.1 us
  local copies, waits for them, and re-layouts: 47.2 us -> 4.21 us
  starting transfers between devices: 56.9 us -> 24.7 us
  matrix products: 19.3 us -> 0 us
  between operations: 15.7 us -> 0.85 us
  Pallas kernels: 0 us -> 14.5 us
  other arithmetic: 10.9 us -> 0.09 us
    psum x1 -> x0, waiting for transfers between devices: 264 us -> none  [body(): lax.psum((local_first, local_second), ('gx', 'gy', 'gz'))]
    all_to_all x0 -> x2, blocking collectives: none -> 48.1 us  [the longest x1 36.8 us: body(): parts = lax.all_to_all(leaving, GROUP, 0, 0)]
    ppermute x18 -> x2, starting transfers between devices: 56.9 us -> 8.88 us  [the longest x1 6.96 us: body(): right = lax.ppermute(own[:3], AXES, [(b, a) for a, b in onward])]
    ppermute x18 -> x2, waiting for transfers between devices: 27.6 us -> 2.35 us  [the longest x1 1.18 us: body(): right = lax.ppermute(own[:3], AXES, [(b, a) for a, b in onward])]
    dot_general x63 -> x0, matrix products: 19.3 us -> none  [the longest x45 12.7 us: stencil(): jnp.einsum('kxyz,ko->oxyz', stacked, matrix, preferred_element_type=jnp.f...]
    slice x35 -> x1, local copies, waits for them, and re-layouts: 18.1 us -> 0.05 us  [body(): right = lax.ppermute(own[:3], AXES, [(b, a) for a, b in onward])]
    all_to_all x0 -> x2, waiting for transfers between devices: none -> 17.6 us  [the longest x1 9.55 us: body(): parts = lax.all_to_all(sent, GROUP, 0, 0)]
    all_to_all x0 -> x2, starting transfers between devices: none -> 15.8 us  [the longest x1 12 us: body(): parts = lax.all_to_all(sent, GROUP, 0, 0)]
  transfers between devices with their start and end apart: 19 -> 4, of which waited for: 10 -> 4; matrix products, arithmetic and copies ran while one was open for 4% -> 3% of each run, Pallas kernels for 0% -> 1%
where the time goes in v4:
time: 113 us; the launch traced here: 112 us
  blocking collectives  48.1 us (43%)
  starting transfers between devices  24.7 us (22%)
  waiting for transfers between devices  19.9 us (18%)
  Pallas kernels  14.5 us (13%)
  local copies, waits for them, and re-layouts  4.21 us (4%)
    all_to_all x1, blocking collectives, body(): parts = lax.all_to_all(leaving, GROUP, 0, 0)  36.8 us
    pallas_call x7, Pallas kernels, call(): pl.pallas_call(kernel, out_shape=tuple((jax.ShapeDtypeStruct(shape, dtype...  14.5 us
    all_to_all x1, starting transfers between devices, body(): parts = lax.all_to_all(sent, GROUP, 0, 0)  12 us
    all_to_all x1, blocking collectives, body(): sums = lax.all_to_all(sums, 'gz', 0, 0)  11.3 us
    all_to_all x1, waiting for transfers between devices, body(): parts = lax.all_to_all(sent, GROUP, 0, 0)  9.55 us
    all_to_all x1, waiting for transfers between devices, body(): every = lax.all_to_all(every, GROUP, 0, 0).reshape(512, 128)  8.02 us
    ppermute x1, starting transfers between devices, body(): right = lax.ppermute(own[:3], AXES, [(b, a) for a, b in onward])  6.96 us
    all_to_all x1, starting transfers between devices, body(): every = lax.all_to_all(every, GROUP, 0, 0).reshape(512, 128)  3.86 us
  transfers between devices with their start and end apart: 4, of which 4 were waited for; matrix products, arithmetic and copies ran while one was open for 3% of the time, Pallas kernels for 1%

profile of v4, /device:TPU:1, one launch (start us, length us, event | category | flops | bytes accessed | tf_op | source)
XLA Modules:
  0.0 112.4 jit_solution(17341981439628442901)
XLA Ops:
  0.6 0.0 copy-start.3
  0.6 0.0 copy-start.2
  0.7 1.1 copy.18
  1.8 0.0 copy-start
  1.8 1.3 %pack.1 = bf16[32,32,128]{2,1,0:T(8,128)(2,1)} custom-call(bf16[2,16,32,128]{3,2,1,0:T(8,128)(2,1)S(1)} %bitcast.24), custom_call_target="tpu_custom_call" | custom-call | flops 100000000 | bytes 1048576 | tf_op jit(solution)/shard_map/pack/pallas_call | solution.py:278
  3.1 0.0 copy-start.1
  3.1 12.0 %all-to-all-start = ((bf16[32,32,128]{2,1,0:T(8,128)(2,1)}), bf16[32,32,128]{2,1,0:T(8,128)(2,1)S(1)}, u32[]{:S(2)}, u32[]{:S(2)}) async-start(bf16[32,32,128]{2,1,0:T(8,128)(2,1)} %pack.1), calls=%async_computation | async-start | bytes 524288 | tf_op jit(solution)/shard_map/all_to_all | solution.py:300
  15.1 0.0 copy-done.3
  15.1 0.0 copy-done.2
  15.1 0.2 copy.13
  15.3 0.0 copy-done
  15.4 0.0 copy-done.1
  15.5 0.8 copy.14
  16.2 0.8 reshape.40
  17.1 0.1 and_convert_fusion
  17.2 9.6 %all-to-all-done.parts_ref = bf16[32,32,128]{2,1,0:T(8,128)(2,1)S(1)} async-done(((bf16[32,32,128]{2,1,0:T(8,128)(2,1)}), bf16[32,32,128]{2,1,0:T(8,128)(2,1)S(1)}, u32[]{:S(2)}, u32[]{:S(2)}) %all-to-all-start) | async-done | bytes 262176 | tf_op jit(solution)/shard_map/all_to_all | solution.py:300
  26.8 0.1 broadcast_in_dim.2.mask_ref
  26.8 0.5 arrange.1.own_ref
  27.4 1.9 %collective-permute-start = (bf16[3,256,128]{2,1,0:T(8,128)(2,1)S(1)}, bf16[3,256,128]{2,1,0:T(8,128)(2,1)S(1)}, u32[]{:S(2)}, u32[]{:S(2)}) collective-permute-start(bf16[3,256,128]{2,1,0:T(8,128)(2,1)S(1)} %get-tuple-element.20), channel_id=1, source_target_pairs={{0,8},{8,16},{16,24},{24,32},{32,40},{40,48},{48,56},{56,64},{64,7... | collective-permute-start | bytes 589832 | tf_op jit(solution)/shard_map/ppermute | solution.py:313
  29.3 7.0 %collective-permute-start.1 = (bf16[3,256,128]{2,1,0:T(8,128)(2,1)S(1)}, bf16[3,256,128]{2,1,0:T(8,128)(2,1)S(1)}, u32[]{:S(2)}, u32[]{:S(2)}) collective-permute-start(bf16[3,256,128]{2,1,0:T(8,128)(2,1)S(1)} %get-tuple-element.19), channel_id=1, source_target_pairs={{8,0},{16,8},{24,16},{32,24},{40,32},{48,40},{56,48},{64,56},{72,6... | collective-permute-start | bytes 589832 | tf_op jit(solution)/shard_map/ppermute | solution.py:314
  36.3 0.2 copy.15.weight_ref
  36.6 1.2 %collective-permute-done.left_ref = bf16[3,256,128]{2,1,0:T(8,128)(2,1)S(1)} collective-permute-done((bf16[3,256,128]{2,1,0:T(8,128)(2,1)S(1)}, bf16[3,256,128]{2,1,0:T(8,128)(2,1)S(1)}, u32[]{:S(2)}, u32[]{:S(2)}) %collective-permute-start) | collective-permute-done | bytes 196640 | tf_op jit(solution)/shard_map/ppermute | solution.py:313
  37.7 1.2 %collective-permute-done.1.right_ref = bf16[3,256,128]{2,1,0:T(8,128)(2,1)S(1)} collective-permute-done((bf16[3,256,128]{2,1,0:T(8,128)(2,1)S(1)}, bf16[3,256,128]{2,1,0:T(8,128)(2,1)S(1)}, u32[]{:S(2)}, u32[]{:S(2)}) %collective-permute-start.1) | collective-permute-done | bytes 196640 | tf_op jit(solution)/shard_map/ppermute | solution.py:314
  38.9 8.6 %layers.1 = bf16[32,64,128]{2,1,0:T(8,128)(2,1)S(1)} custom-call(bf16[4,256,128]{2,1,0:T(8,128)(2,1)S(1)} %arrange.1.own_ref, bf16[3,256,128]{2,1,0:T(8,128)(2,1)S(1)} %collective-permute-done.left_ref, bf16[3,256,128]{2,1,0:T(8,128)(2,1)S(1)} %collective-permute-done.1.right_ref, bf16[480,288]{1,0:T(8,128)(2,1)S(1)} %copy.15.weight_ref, ...), custom_call_target="tpu_custom_call" | custom-call | flops 8000000000 | bytes 1048576 | tf_op jit(solution)/shard_map/layers/pallas_call | solution.py:278
  47.5 36.8 %all_to_all.20.parts_ref = bf16[32,64,128]{2,1,0:T(8,128)(2,1)S(1)} all-to-all(bf16[32,64,128]{2,1,0:T(8,128)(2,1)S(1)} %layers.1), channel_id=1, replica_groups=mesh['gx'=4,'gy'=8,'gz'=8] {'gx','gy'}, dimensions={0} | all-to-all | bytes 1048576 | tf_op jit(solution)/shard_map/all_to_all | solution.py:335
  84.3 11.3 %all_to_all.21.parts_ref = f32[8,16,128]{2,1,0:T(8,128)S(1)} all-to-all(f32[8,16,128]{2,1,0:T(8,128)S(1)} %gather_sums.1), channel_id=1, replica_groups=mesh['gx'=4,'gy'=8,'gz'=8] {'gz'}, dimensions={0} | all-to-all | bytes 131072 | tf_op jit(solution)/shard_map/all_to_all | solution.py:337
  95.6 0.7 combine.1
  96.3 3.9 %all-to-all-start.3 = ((bf16[32,16,128]{2,1,0:T(8,128)(2,1)}), bf16[32,16,128]{2,1,0:T(8,128)(2,1)S(1)}, u32[]{:S(2)}, u32[]{:S(2)}) async-start(bf16[32,16,128]{2,1,0:T(8,128)(2,1)} %combine.1), calls=%async_computation.3 | async-start | bytes 262144 | tf_op jit(solution)/shard_map/all_to_all | solution.py:339
  100.2 0.7 unpack.1
  100.9 0.8 copy.16
  101.7 8.0 %all-to-all-done.3 = bf16[32,16,128]{2,1,0:T(8,128)(2,1)S(1)} async-done(((bf16[32,16,128]{2,1,0:T(8,128)(2,1)}), bf16[32,16,128]{2,1,0:T(8,128)(2,1)S(1)}, u32[]{:S(2)}, u32[]{:S(2)}) %all-to-all-start.3) | async-done | bytes 131104 | tf_op jit(solution)/shard_map/all_to_all | solution.py:339
  109.8 2.7 %finish.1 = (f32[27,32,32]{2,1,0:T(8,128)}, f32[27,32,32]{2,1,0:T(8,128)}) custom-call(bf16[512,128]{1,0:T(8,128)(2,1)S(1)} %bitcast.27, bf16[27,32,32]{2,1,0:T(8,128)(2,1)S(1)} %bitcast.25, bf16[27,32,32]{2,1,0:T(8,128)(2,1)S(1)} %bitcast.26), custom_call_target="tpu_custom_call" | custom-call | flops 100000000 | bytes 1048576 | tf_op jit(solution)/shard_map/finish/pallas_call | solution.py:278
  (8 shorter events, 0.2 us)
Async XLA Ops:
  0.6 14.5 %copy-start.3 = (bf16[3,3,3,32,32]{4,3,2,1,0:T(8,128)(2,1)S(1)}, bf16[3,3,3,32,32]{4,3,2,1,0:T(8,128)(2,1)}, u32[]{:S(2)}) copy-start(bf16[3,3,3,32,32]{4,3,2,1,0:T(8,128)(2,1)} %param.6) | copy-start | bytes 165892
  0.6 14.5 %copy-start.2 = (bf16[3,3,3,32,32]{4,3,2,1,0:T(8,128)(2,1)S(1)}, bf16[3,3,3,32,32]{4,3,2,1,0:T(8,128)(2,1)}, u32[]{:S(2)}) copy-start(bf16[3,3,3,32,32]{4,3,2,1,0:T(8,128)(2,1)} %param.7) | copy-start | bytes 165892
  1.8 13.5 %copy-start = (bf16[3,3,3,32,32]{4,3,2,1,0:T(8,128)(2,1)S(1)}, bf16[3,3,3,32,32]{4,3,2,1,0:T(8,128)(2,1)}, u32[]{:S(2)}) copy-start(bf16[3,3,3,32,32]{4,3,2,1,0:T(8,128)(2,1)} %param.8) | copy-start | bytes 165892
  3.1 12.3 %copy-start.1 = (bf16[3,3,3,32,32]{4,3,2,1,0:T(8,128)(2,1)S(1)}, bf16[3,3,3,32,32]{4,3,2,1,0:T(8,128)(2,1)}, u32[]{:S(2)}) copy-start(bf16[3,3,3,32,32]{4,3,2,1,0:T(8,128)(2,1)} %param.9) | copy-start | bytes 165892
  3.1 23.7 %all-to-all-start = ((bf16[32,32,128]{2,1,0:T(8,128)(2,1)}), bf16[32,32,128]{2,1,0:T(8,128)(2,1)S(1)}, u32[]{:S(2)}, u32[]{:S(2)}) async-start(bf16[32,32,128]{2,1,0:T(8,128)(2,1)} %pack.1), calls=%async_computation | async-start | bytes 524288 | tf_op jit(solution)/shard_map/all_to_all | solution.py:300
  27.4 10.3 %collective-permute-start = (bf16[3,256,128]{2,1,0:T(8,128)(2,1)S(1)}, bf16[3,256,128]{2,1,0:T(8,128)(2,1)S(1)}, u32[]{:S(2)}, u32[]{:S(2)}) collective-permute-start(bf16[3,256,128]{2,1,0:T(8,128)(2,1)S(1)} %get-tuple-element.20), channel_id=1, source_target_pairs={{0,8},{8,16},{16,24},{24,32},{32,40},{40,48},{48,56},{56,64},{64,7... | collective-permute-start | bytes 589832 | tf_op jit(solution)/shard_map/ppermute | solution.py:313
  29.3 9.6 %collective-permute-start.1 = (bf16[3,256,128]{2,1,0:T(8,128)(2,1)S(1)}, bf16[3,256,128]{2,1,0:T(8,128)(2,1)S(1)}, u32[]{:S(2)}, u32[]{:S(2)}) collective-permute-start(bf16[3,256,128]{2,1,0:T(8,128)(2,1)S(1)} %get-tuple-element.19), channel_id=1, source_target_pairs={{8,0},{16,8},{24,16},{32,24},{40,32},{48,40},{56,48},{64,56},{72,6... | collective-permute-start | bytes 589832 | tf_op jit(solution)/shard_map/ppermute | solution.py:314
  96.3 13.5 %all-to-all-start.3 = ((bf16[32,16,128]{2,1,0:T(8,128)(2,1)}), bf16[32,16,128]{2,1,0:T(8,128)(2,1)S(1)}, u32[]{:S(2)}, u32[]{:S(2)}) async-start(bf16[32,16,128]{2,1,0:T(8,128)(2,1)} %combine.1), calls=%async_computation.3 | async-start | bytes 262144 | tf_op jit(solution)/shard_map/all_to_all | solution.py:339

commit v5 on v4

--- a/solution.py
+++ b/solution.py
@@ -14,6 +14,19 @@
 PLANES = 8
 OWN = 4
 MEMBERS = 32
+
+
+def closed_line():
+    def member(z, x):
+        return (z % 4) * 8 + (z // 4) * 4 + x
+
+    line = []
+    for z in range(8):
+        line += [member(z, x) for x in ((1, 2, 3) if z % 2 == 0 else (3, 2, 1))]
+    return tuple(line + [member(z, 0) for z in reversed(range(8))])
+
+
+LINE = closed_line()
 
 
 def lanes_of(shape):
@@ -46,13 +59,15 @@
 
 
 def pack(cells_ref, out_ref, sorted_ref):
-    moved = jnp.dot(cells_ref[...].reshape(1024, 128), permutation(False), preferred_element_type=F32)
-    sorted_ref[...] = moved.reshape(32, 32, 128)
+    sorted_ref[...] = jnp.dot(
+        cells_ref[...].reshape(1024, 128), permutation(False), preferred_element_type=F32
+    )
     for part in range(2):
         at = slice(16 * part, 16 * part + 16)
-        tiles = exchange([sorted_ref[i, at] for i in range(32)], (0, 1, 2, 3, 4))
-        for member in range(MEMBERS):
-            out_ref[member, at] = tiles[member].astype(BF16)
+        tiles = [sorted_ref[pl.ds(512 * part + i, 16, stride=32)] for i in range(32)]
+        tiles = exchange(tiles, (0, 1, 2, 3, 4))
+        for i in range(MEMBERS):
+            out_ref[LINE[i], at] = tiles[i].astype(BF16)
 
 
 def arrange(parts_ref, own_ref):
@@ -66,11 +81,12 @@
 def unpack(parts_ref, out_ref, mixed_ref):
     for part in range(2):
         at = slice(16 * part, 16 * part + 16)
-        tiles = exchange([parts_ref[i, at].astype(F32) for i in range(MEMBERS)], (0, 1, 2, 3, 4))
+        tiles = [parts_ref[LINE[i], at].astype(F32) for i in range(MEMBERS)]
+        tiles = exchange(tiles, (0, 1, 2, 3, 4))
         for i in range(32):
-            mixed_ref[i, at] = tiles[i].astype(BF16)
-    moved = jnp.dot(mixed_ref[...].reshape(1024, 128), permutation(True), preferred_element_type=F32)
-    out_ref[...] = moved.astype(BF16).reshape(2, 16, 32, 128)
+            mixed_ref[pl.ds(512 * part + i, 16, stride=32)] = tiles[i]
+    moved = jnp.dot(mixed_ref[...].astype(BF16), permutation(True), preferred_element_type=F32)
+    out_ref[...] = moved.astype(BF16).reshape(32, 2, 16, 128)
 
 
 def gelu_pair(pre):
@@ -244,9 +260,9 @@
         out_ref[member] = total
 
 
-def finish(factor, count_all, packed_ref, v_first_ref, v_second_ref, first_ref, second_ref):
-    def damped(summed, direction):
-        return factor * (summed / count_all + 0.1 * direction.astype(F32))
+def finish(scale, packed_ref, d_first_ref, d_second_ref, first_ref, second_ref):
+    def damped(summed, damping):
+        return scale * summed + damping
 
     rest = packed_ref[288:432, :].astype(F32)
     rest = jnp.concatenate([rest, pltpu.roll(rest, 64, 1)], axis=0)
@@ -255,10 +271,10 @@
         far = rest[32 * block : 32 * block + 32]
         at = [9 * (block % 3) + 3 * row + block // 3 for row in range(3)]
         for row in range(3):
-            second_ref[at[row]] = damped(low[:, 32 * row : 32 * row + 32], v_second_ref[at[row]])
-        first_ref[at[0]] = damped(low[:, 96:128], v_first_ref[at[0]])
-        first_ref[at[1]] = damped(far[:, 0:32], v_first_ref[at[1]])
-        first_ref[at[2]] = damped(far[:, 32:64], v_first_ref[at[2]])
+            second_ref[at[row]] = damped(low[:, 32 * row : 32 * row + 32], d_second_ref[at[row]])
+        first_ref[at[0]] = damped(low[:, 96:128], d_first_ref[at[0]])
+        first_ref[at[1]] = damped(far[:, 0:32], d_first_ref[at[1]])
+        first_ref[at[2]] = damped(far[:, 32:64], d_first_ref[at[2]])
 
 
 def cell_masks(column, width):
@@ -295,19 +311,22 @@
     factor = math.sqrt(27.0 * channels)
     small = (channels, 128)
 
-    cells = jnp.transpose(volume, (1, 2, 0, 3))
-    (sent,) = call(pack, (cells,), [((members,) + small, BF16)], [((32,) + small, F32)], "pack", 8, 10**8)
+    (sent,) = call(pack, (volume,), [((members,) + small, BF16)], [((1024, 128), F32)], "pack", 8, 10**8)
     parts = lax.all_to_all(sent, GROUP, 0, 0)
 
-    block = lax.axis_index("gz") * members + lax.axis_index("gx") * n_gy + lax.axis_index("gy")
-    masks = cell_masks(OWN * block, width * n_gz)
+    member = lax.axis_index("gx") * n_gy + lax.axis_index("gy")
+    place = jnp.sum(jnp.where(jnp.array(LINE) == member, jnp.arange(members), 0)).astype(jnp.int32)
+    masks = cell_masks(OWN * (lax.axis_index("gz") * members + place), width * n_gz)
     weights = filters(w_first, v_first, w_second, v_second)
-    parts, masks, weights = lax.optimization_barrier((parts, masks, weights))
+    damping = tuple(
+        factor * 0.1 * v.astype(F32).reshape(27, channels, channels) for v in (v_first, v_second)
+    )
+    parts, masks, weights, damping = lax.optimization_barrier((parts, masks, weights, damping))
 
     (own,) = call(arrange, (parts,), [((OWN, 256, 128), BF16)], [], "arrange", 8, 10**8)
 
     def device(at):
-        return (at % members) * n_gz + at // members
+        return LINE[at % members] * n_gz + at // members
 
     onward = [(device(i), device(i + 1)) for i in range(members * n_gz - 1)]
     left = lax.ppermute(own[1:], AXES, onward)
@@ -337,19 +356,18 @@
     sums = lax.all_to_all(sums, "gz", 0, 0)
     (every,) = call(combine, (sums,), [((members, 16, 128), BF16)], [], "combine", 8, 10**8)
     every = lax.all_to_all(every, GROUP, 0, 0).reshape(512, 128)
-    (home,) = call(
+    (out,) = call(
         unpack,
         (parts,),
-        [((depth, height) + small, BF16)],
-        [((32,) + small, BF16)],
+        [(volume.shape, BF16)],
+        [((1024, 128), F32)],
         "unpack",
         8,
         10**9,
     )
-    out = jnp.transpose(home, (2, 0, 1, 3))
     gv_first, gv_second = call(
-        lambda *refs: finish(factor, count_all, *refs),
-        (every, v_first.reshape(27, channels, channels), v_second.reshape(27, channels, channels)),
+        lambda *refs: finish(factor / count_all, *refs),
+        (every,) + damping,
         [((27, channels, channels), F32)] * 2,
         [],
         "finish",

time: 113 us -> 98.3 us (0.87)
  blocking collectives: 48.1 us -> 31.1 us
  waiting for transfers between devices: 19.9 us -> 22.6 us
  starting transfers between devices: 24.7 us -> 22.9 us
  Pallas kernels: 14.5 us -> 15.8 us
    all_to_all x1, blocking collectives: 36.8 us -> 18.9 us  [body(): parts = lax.all_to_all(leaving, GROUP, 0, 0)]
    ppermute x1, starting transfers between devices: 6.96 us -> 1.92 us  [body(): right = lax.ppermute(own[:3], AXES, [(b, a) for a, b in onward])]
    ppermute x1, waiting for transfers between devices: 1.18 us -> 4.54 us  [body(): right = lax.ppermute(own[:3], AXES, [(b, a) for a, b in onward])]
    ppermute x1, starting transfers between devices: 1.92 us -> 5.11 us  [body(): left = lax.ppermute(own[1:], AXES, onward)]
    all_to_all x1, waiting for transfers between devices: 9.55 us -> 8.16 us  [body(): parts = lax.all_to_all(sent, GROUP, 0, 0)]
    pallas_call x7, Pallas kernels: 14.5 us -> 15.8 us  [call(): pl.pallas_call(kernel, out_shape=tuple((jax.ShapeDtypeStruct(shape, dtype...]
  transfers between devices with their start and end apart: 4 -> 4, of which waited for: 4 -> 4; matrix products, arithmetic and copies ran while one was open for 3% -> 3% of each run, Pallas kernels for 1% -> 2%
where the time goes in v5:
time: 98.3 us; the launch traced here: 97.9 us
  blocking collectives  31.1 us (32%)
  starting transfers between devices  22.9 us (23%)
  waiting for transfers between devices  22.6 us (23%)
  Pallas kernels  15.8 us (16%)
  local copies, waits for them, and re-layouts  3.23 us (3%)
  between operations  1.5 us (2%)
    all_to_all x1, blocking collectives, body(): parts = lax.all_to_all(leaving, GROUP, 0, 0)  18.9 us
    pallas_call x7, Pallas kernels, call(): pl.pallas_call(kernel, out_shape=tuple((jax.ShapeDtypeStruct(shape, dtype...  15.8 us
    all_to_all x1, blocking collectives, body(): sums = lax.all_to_all(sums, 'gz', 0, 0)  12.2 us
    all_to_all x1, starting transfers between devices, body(): parts = lax.all_to_all(sent, GROUP, 0, 0)  12 us
    all_to_all x1, waiting for transfers between devices, body(): parts = lax.all_to_all(sent, GROUP, 0, 0)  8.16 us
    all_to_all x1, waiting for transfers between devices, body(): every = lax.all_to_all(every, GROUP, 0, 0).reshape(512, 128)  7.9 us
    ppermute x1, starting transfers between devices, body(): left = lax.ppermute(own[1:], AXES, onward)  5.11 us
    ppermute x1, waiting for transfers between devices, body(): right = lax.ppermute(own[:3], AXES, [(b, a) for a, b in onward])  4.54 us
  transfers between devices with their start and end apart: 4, of which 4 were waited for; matrix products, arithmetic and copies ran while one was open for 3% of the time, Pallas kernels for 2%

profile of v5, /device:TPU:1, one launch (start us, length us, event | category | flops | bytes accessed | tf_op | source)
XLA Modules:
  0.0 97.9 jit_solution(2483061219222748014)
XLA Ops:
  0.6 0.0 copy-start
  0.6 0.9 copy-done
  1.6 0.0 copy-start.4
  1.6 0.0 copy-start.1
  1.6 0.0 copy-start.2
  1.6 1.6 %pack.1 = bf16[32,32,128]{2,1,0:T(8,128)(2,1)} custom-call(bf16[32,2,16,128]{3,2,1,0:T(8,128)(2,1)S(1)} %copy-done), custom_call_target="tpu_custom_call" | custom-call | flops 100000000 | bytes 1048576 | tf_op jit(solution)/shard_map/pack/pallas_call | solution.py:294
  3.2 0.0 copy-start.5
  3.2 0.0 copy-start.3
  3.2 12.0 %all-to-all-start = ((bf16[32,32,128]{2,1,0:T(8,128)(2,1)}), bf16[32,32,128]{2,1,0:T(8,128)(2,1)S(1)}, u32[]{:S(2)}, u32[]{:S(2)}) async-start(bf16[32,32,128]{2,1,0:T(8,128)(2,1)} %pack.1), calls=%async_computation | async-start | bytes 524288 | tf_op jit(solution)/shard_map/all_to_all | solution.py:315
  15.2 0.0 copy-done.4
  15.2 0.0 copy-done.1
  15.2 0.2 copy.11
  15.4 0.0 copy-done.2
  15.5 0.0 copy-done.5
  15.5 0.6 fusion
  16.8 0.0 copy-done.3
  16.9 0.1 and_convert_fusion
  16.9 0.8 copy.12
  17.7 0.8 reshape.40
  18.7 8.2 %all-to-all-done.parts_ref = bf16[32,32,128]{2,1,0:T(8,128)(2,1)S(1)} async-done(((bf16[32,32,128]{2,1,0:T(8,128)(2,1)}), bf16[32,32,128]{2,1,0:T(8,128)(2,1)S(1)}, u32[]{:S(2)}, u32[]{:S(2)}) %all-to-all-start) | async-done | bytes 262176 | tf_op jit(solution)/shard_map/all_to_all | solution.py:315
  26.8 0.1 broadcast_in_dim.11.mask_ref
  26.9 0.5 arrange.1.own_ref
  27.5 5.1 %collective-permute-start = (bf16[3,256,128]{2,1,0:T(8,128)(2,1)S(1)}, bf16[3,256,128]{2,1,0:T(8,128)(2,1)S(1)}, u32[]{:S(2)}, u32[]{:S(2)}) collective-permute-start(bf16[3,256,128]{2,1,0:T(8,128)(2,1)S(1)} %get-tuple-element.18), channel_id=1, source_target_pairs={{8,16},{16,24},{24,88},{88,80},{80,72},{72,136},{136,144},{144,152... | collective-permute-start | bytes 589832 | tf_op jit(solution)/shard_map/ppermute | solution.py:332
  32.6 1.9 %collective-permute-start.1 = (bf16[3,256,128]{2,1,0:T(8,128)(2,1)S(1)}, bf16[3,256,128]{2,1,0:T(8,128)(2,1)S(1)}, u32[]{:S(2)}, u32[]{:S(2)}) collective-permute-start(bf16[3,256,128]{2,1,0:T(8,128)(2,1)S(1)} %get-tuple-element.17), channel_id=1, source_target_pairs={{16,8},{24,16},{88,24},{80,88},{72,80},{136,72},{144,136},{152,144... | collective-permute-start | bytes 589832 | tf_op jit(solution)/shard_map/ppermute | solution.py:333
  34.5 0.2 copy.13.weight_ref
  34.8 2.0 %collective-permute-done.left_ref = bf16[3,256,128]{2,1,0:T(8,128)(2,1)S(1)} collective-permute-done((bf16[3,256,128]{2,1,0:T(8,128)(2,1)S(1)}, bf16[3,256,128]{2,1,0:T(8,128)(2,1)S(1)}, u32[]{:S(2)}, u32[]{:S(2)}) %collective-permute-start) | collective-permute-done | bytes 196640 | tf_op jit(solution)/shard_map/ppermute | solution.py:332
  36.8 4.5 %collective-permute-done.1.right_ref = bf16[3,256,128]{2,1,0:T(8,128)(2,1)S(1)} collective-permute-done((bf16[3,256,128]{2,1,0:T(8,128)(2,1)S(1)}, bf16[3,256,128]{2,1,0:T(8,128)(2,1)S(1)}, u32[]{:S(2)}, u32[]{:S(2)}) %collective-permute-start.1) | collective-permute-done | bytes 196640 | tf_op jit(solution)/shard_map/ppermute | solution.py:333
  41.3 8.6 %layers.1 = bf16[32,64,128]{2,1,0:T(8,128)(2,1)S(1)} custom-call(bf16[4,256,128]{2,1,0:T(8,128)(2,1)S(1)} %arrange.1.own_ref, bf16[3,256,128]{2,1,0:T(8,128)(2,1)S(1)} %collective-permute-done.left_ref, bf16[3,256,128]{2,1,0:T(8,128)(2,1)S(1)} %collective-permute-done.1.right_ref, bf16[480,288]{1,0:T(8,128)(2,1)S(1)} %copy.13.weight_ref, ...), custom_call_target="tpu_custom_call" | custom-call | flops 8000000000 | bytes 1048576 | tf_op jit(solution)/shard_map/layers/pallas_call | solution.py:294
  50.0 18.9 %all_to_all.20.parts_ref = bf16[32,64,128]{2,1,0:T(8,128)(2,1)S(1)} all-to-all(bf16[32,64,128]{2,1,0:T(8,128)(2,1)S(1)} %layers.1), channel_id=1, replica_groups=mesh['gx'=4,'gy'=8,'gz'=8] {'gx','gy'}, dimensions={0} | all-to-all | bytes 1048576 | tf_op jit(solution)/shard_map/all_to_all | solution.py:354
  69.0 12.2 %all_to_all.21.parts_ref = f32[8,16,128]{2,1,0:T(8,128)S(1)} all-to-all(f32[8,16,128]{2,1,0:T(8,128)S(1)} %gather_sums.1), channel_id=1, replica_groups=mesh['gx'=4,'gy'=8,'gz'=8] {'gz'}, dimensions={0} | all-to-all | bytes 131072 | tf_op jit(solution)/shard_map/all_to_all | solution.py:356
  81.1 0.7 combine.1
  81.8 3.9 %all-to-all-start.3 = ((bf16[32,16,128]{2,1,0:T(8,128)(2,1)}), bf16[32,16,128]{2,1,0:T(8,128)(2,1)S(1)}, u32[]{:S(2)}, u32[]{:S(2)}) async-start(bf16[32,16,128]{2,1,0:T(8,128)(2,1)} %combine.1), calls=%async_computation.3 | async-start | bytes 262144 | tf_op jit(solution)/shard_map/all_to_all | solution.py:358
  85.7 1.7 %unpack.1 = bf16[32,2,16,128]{3,2,1,0:T(8,128)(2,1)} custom-call(bf16[32,64,128]{2,1,0:T(8,128)(2,1)S(1)} %all_to_all.20.parts_ref), custom_call_target="tpu_custom_call" | custom-call | flops 1000000000 | bytes 1048576 | tf_op jit(solution)/shard_map/unpack/pallas_call | solution.py:294
  87.3 7.9 %all-to-all-done.3 = bf16[32,16,128]{2,1,0:T(8,128)(2,1)S(1)} async-done(((bf16[32,16,128]{2,1,0:T(8,128)(2,1)}), bf16[32,16,128]{2,1,0:T(8,128)(2,1)S(1)}, u32[]{:S(2)}, u32[]{:S(2)}) %all-to-all-start.3) | async-done | bytes 131104 | tf_op jit(solution)/shard_map/all_to_all | solution.py:358
  95.2 2.7 %finish.1 = (f32[27,32,32]{2,1,0:T(8,128)}, f32[27,32,32]{2,1,0:T(8,128)}) custom-call(bf16[512,128]{1,0:T(8,128)(2,1)S(1)} %bitcast.22, f32[27,32,32]{2,1,0:T(8,128)S(1)} %bitcast.20, f32[27,32,32]{2,1,0:T(8,128)S(1)} %bitcast.21), custom_call_target="tpu_custom_call" | custom-call | flops 100000000 | bytes 1048576 | tf_op jit(solution)/shard_map/finish/pallas_call | solution.py:294
  (10 shorter events, 0.3 us)
Async XLA Ops:
  0.6 1.0 copy-start
  1.6 13.6 %copy-start.4 = (bf16[3,3,3,32,32]{4,3,2,1,0:T(8,128)(2,1)S(1)}, bf16[3,3,3,32,32]{4,3,2,1,0:T(8,128)(2,1)}, u32[]{:S(2)}) copy-start(bf16[3,3,3,32,32]{4,3,2,1,0:T(8,128)(2,1)} %param.7) | copy-start | bytes 165892
  1.6 13.6 %copy-start.1 = (bf16[3,3,3,32,32]{4,3,2,1,0:T(8,128)(2,1)S(1)}, bf16[3,3,3,32,32]{4,3,2,1,0:T(8,128)(2,1)}, u32[]{:S(2)}) copy-start(bf16[3,3,3,32,32]{4,3,2,1,0:T(8,128)(2,1)} %param.8) | copy-start | bytes 165892
  1.6 13.8 %copy-start.2 = (bf16[3,3,3,32,32]{4,3,2,1,0:T(8,128)(2,1)S(1)}, bf16[3,3,3,32,32]{4,3,2,1,0:T(8,128)(2,1)}, u32[]{:S(2)}) copy-start(bf16[3,3,3,32,32]{4,3,2,1,0:T(8,128)(2,1)} %param.9) | copy-start | bytes 165892
  3.2 12.3 %copy-start.5 = (s32[32]{0:T(128)S(1)}, s32[32]{0:T(128)}, u32[]{:S(2)}) copy-start(s32[32]{0:T(128)} %constant.33.clone) | copy-start | bytes 388
  3.2 13.6 %copy-start.3 = (bf16[3,3,3,32,32]{4,3,2,1,0:T(8,128)(2,1)S(1)}, bf16[3,3,3,32,32]{4,3,2,1,0:T(8,128)(2,1)}, u32[]{:S(2)}) copy-start(bf16[3,3,3,32,32]{4,3,2,1,0:T(8,128)(2,1)} %param.10) | copy-start | bytes 165892
  3.2 23.7 %all-to-all-start = ((bf16[32,32,128]{2,1,0:T(8,128)(2,1)}), bf16[32,32,128]{2,1,0:T(8,128)(2,1)S(1)}, u32[]{:S(2)}, u32[]{:S(2)}) async-start(bf16[32,32,128]{2,1,0:T(8,128)(2,1)} %pack.1), calls=%async_computation | async-start | bytes 524288 | tf_op jit(solution)/shard_map/all_to_all | solution.py:315
  27.5 9.3 %collective-permute-start = (bf16[3,256,128]{2,1,0:T(8,128)(2,1)S(1)}, bf16[3,256,128]{2,1,0:T(8,128)(2,1)S(1)}, u32[]{:S(2)}, u32[]{:S(2)}) collective-permute-start(bf16[3,256,128]{2,1,0:T(8,128)(2,1)S(1)} %get-tuple-element.18), channel_id=1, source_target_pairs={{8,16},{16,24},{24,88},{88,80},{80,72},{72,136},{136,144},{144,152... | collective-permute-start | bytes 589832 | tf_op jit(solution)/shard_map/ppermute | solution.py:332
  32.6 8.7 %collective-permute-start.1 = (bf16[3,256,128]{2,1,0:T(8,128)(2,1)S(1)}, bf16[3,256,128]{2,1,0:T(8,128)(2,1)S(1)}, u32[]{:S(2)}, u32[]{:S(2)}) collective-permute-start(bf16[3,256,128]{2,1,0:T(8,128)(2,1)S(1)} %get-tuple-element.17), channel_id=1, source_target_pairs={{16,8},{24,16},{88,24},{80,88},{72,80},{136,72},{144,136},{152,144... | collective-permute-start | bytes 589832 | tf_op jit(solution)/shard_map/ppermute | solution.py:333
  81.8 13.4 %all-to-all-start.3 = ((bf16[32,16,128]{2,1,0:T(8,128)(2,1)}), bf16[32,16,128]{2,1,0:T(8,128)(2,1)S(1)}, u32[]{:S(2)}, u32[]{:S(2)}) async-start(bf16[32,16,128]{2,1,0:T(8,128)(2,1)} %combine.1), calls=%async_computation.3 | async-start | bytes 262144 | tf_op jit(solution)/shard_map/all_to_all | solution.py:358

commit v6 on v5

--- a/solution.py
+++ b/solution.py
@@ -70,12 +70,23 @@
             out_ref[LINE[i], at] = tiles[i].astype(BF16)
 
 
-def arrange(parts_ref, own_ref):
+def arrange(parts_ref, odd_ref, own_ref, first_ref, second_ref):
     for g in range(4):
         tiles = exchange([parts_ref[8 * g + j].astype(F32) for j in range(8)], (4, 5, 6))
         for i in range(8):
             plane = 2 * g + i % 2
             own_ref[i // 2, 32 * plane : 32 * plane + 32] = tiles[i].astype(BF16)
+    odd = odd_ref[0] > 0
+
+    @pl.when(odd)
+    def _():
+        first_ref[...] = own_ref[0:3]
+        second_ref[...] = own_ref[1:4]
+
+    @pl.when(jnp.logical_not(odd))
+    def _():
+        first_ref[...] = own_ref[1:4]
+        second_ref[...] = own_ref[0:3]
 
 
 def unpack(parts_ref, out_ref, mixed_ref):
@@ -111,22 +122,29 @@
     return before(product[0:32]) + product[32:64] + after(product[64:96])
 
 
-def near(ref, z, x):
-    return jnp.concatenate(
-        [
-            jnp.concatenate([ref[z + at + offset, 32 * x : 32 * x + 96] for offset in range(3)], axis=0)
-            for at in range(2)
-        ],
-        axis=1,
-    )
+def near(refs, z, x):
+    def block(ref, at):
+        rows = ref[at, max(32 * x - 32, 0) : min(32 * x + 64, 256)]
+        blank = jnp.zeros((32, 128), BF16)
+        if x == 0:
+            return [blank, rows]
+        if x == PLANES - 1:
+            return [rows, blank]
+        return [rows]
+
+    columns = []
+    for at in range(2):
+        rows = sum((block(ref, z + at + offset) for ref in refs for offset in range(3)), [])
+        columns.append(jnp.concatenate(rows, axis=0))
+    return jnp.concatenate(columns, axis=1)
 
 
 def tile_of(x):
-    return slice(32 * x + 32, 32 * x + 64)
+    return slice(32 * x, 32 * x + 32)
 
 
 def correlate(ref, z, targets):
-    rows = jnp.concatenate([near(ref, z, x) for x in range(PLANES)], axis=1)
+    rows = jnp.concatenate([near((ref,), z, x) for x in range(PLANES)], axis=1)
     return lax.dot_general(
         rows,
         jnp.concatenate(targets, axis=1),
@@ -136,93 +154,84 @@
 
 
 def layers(
+    width,
     own_ref,
-    left_ref,
-    right_ref,
+    first_ref,
+    second_ref,
+    odd_ref,
     weight_ref,
-    mask_ref,
+    joint_ref,
+    column_ref,
     out_ref,
     p_vol,
     p_hid,
     p_tan,
     p_jv,
     slopes,
-    sums_first,
-    sums_second,
     packed,
 ):
-    blank = jnp.zeros((32, 128), BF16)
-    for ref, count in ((p_vol, 10), (p_hid, 8), (p_tan, 8), (p_jv, 6)):
-        for z in range(count):
-            ref[z, 0:32] = blank
-            ref[z, 288:320] = blank
-    for z in range(3):
-        p_vol[z, 32:288] = left_ref[z]
-        p_vol[7 + z, 32:288] = right_ref[z]
-    for z in range(OWN):
-        p_vol[3 + z, 32:288] = own_ref[z]
-    sums_first[...] = jnp.zeros_like(sums_first)
-    sums_second[...] = jnp.zeros_like(sums_second)
-
-    def first(step, carry):
-        z = 2 * step
+    odd = odd_ref[0] > 0
+
+    @pl.when(odd)
+    def _():
+        p_vol[0:3] = first_ref[...]
+        p_vol[7:10] = second_ref[...]
+
+    @pl.when(jnp.logical_not(odd))
+    def _():
+        p_vol[0:3] = second_ref[...]
+        p_vol[7:10] = first_ref[...]
+
+    p_vol[3:7] = own_ref[...]
+
+    def inside(column):
+        at = column_ref[0] + column
+        return (at >= 0) & (at < width)
+
+    for z in range(0, 8, 2):
         for x in range(PLANES):
-            product = jnp.dot(weight_ref[0:192, :], near(p_vol, z, x), preferred_element_type=F32)
+            product = jnp.dot(weight_ref[0:192, :], near((p_vol,), z, x), preferred_element_type=F32)
             for at in range(2):
                 part = product[:, 128 * at : 128 * at + 128]
-                inside = mask_ref[z + at] > 0.0
+                here = inside(z + at - 2)
                 hidden, slope = gelu_pair(fold(part[0:96]))
                 tangent = slope * fold(part[96:192])
-                p_hid[z + at, tile_of(x)] = jnp.where(inside, hidden, 0.0).astype(BF16)
-                p_tan[z + at, tile_of(x)] = jnp.where(inside, tangent, 0.0).astype(BF16)
-                slopes[z + at, x] = slope
-        return carry
-
-    lax.fori_loop(0, 4, first, 0)
-
-    def second(step, carry):
-        z = 2 * step
+                p_hid[z + at, tile_of(x)] = jnp.where(here, hidden, 0.0).astype(BF16)
+                p_tan[z + at, tile_of(x)] = jnp.where(here, tangent, 0.0).astype(BF16)
+                if 2 <= z + at < 6:
+                    slopes[z + at - 2, x] = slope
+
+    for z in range(0, 6, 2):
         for x in range(PLANES):
-            product = jnp.dot(weight_ref[192:288, :], near(p_tan, z, x), preferred_element_type=F32)
-            product = product + jnp.dot(
-                weight_ref[288:384, :], near(p_hid, z, x), preferred_element_type=F32
-            )
+            product = jnp.dot(joint_ref[...], near((p_tan, p_hid), z, x), preferred_element_type=F32)
             for at in range(2):
                 jv = fold(product[:, 128 * at : 128 * at + 128])
-                jv = jnp.where(mask_ref[8 + z + at] > 0.0, jv, 0.0)
+                jv = jnp.where(inside(z + at - 1), jv, 0.0)
                 p_jv[z + at, tile_of(x)] = jv.astype(BF16)
-        return carry
-
-    lax.fori_loop(0, 3, second, 0)
 
     def spread(tiles):
         both = [
-            jnp.concatenate(
-                [after(tile), tile, before(tile), jnp.zeros_like(tile)], axis=0
-            )
+            jnp.concatenate([after(tile), tile, before(tile), jnp.zeros_like(tile)], axis=0)
             for tile in tiles
         ]
         return jnp.concatenate(both, axis=1).astype(BF16)
 
-    def third(step, carry):
-        z = 2 * step
+    sums_first = sums_second = 0.0
+    for z in range(0, OWN, 2):
         targets = [
             spread([p_jv[z + at + 1, tile_of(x)].astype(F32) for at in range(2)])
             for x in range(PLANES)
         ]
-        sums_second[...] += correlate(p_hid.at[pl.ds(1, 6)], z, targets)
+        sums_second = sums_second + correlate(p_hid, z + 1, targets)
         targets = []
         for x in range(PLANES):
-            product = jnp.dot(weight_ref[384:480, :], near(p_jv, z, x), preferred_element_type=F32)
+            product = jnp.dot(weight_ref[192:288, :], near((p_jv,), z, x), preferred_element_type=F32)
             tiles = []
             for at in range(2):
-                back = slopes[z + at + 2, x] * fold(product[:, 128 * at : 128 * at + 128])
+                back = slopes[z + at, x] * fold(product[:, 128 * at : 128 * at + 128])
                 tiles.append(back.astype(BF16).astype(F32))
             targets.append(spread(tiles))
-        sums_first[...] += correlate(p_vol.at[pl.ds(2, 6)], z, targets)
-        return carry
-
-    lax.fori_loop(0, 2, third, 0)
+        sums_first = sums_first + correlate(p_vol, z + 2, targets)
 
     for g in range(4):
         tiles = [p_jv[1 + i // 2, tile_of(2 * g + i % 2)].astype(F32) for i in range(8)]
@@ -230,11 +239,8 @@
         for j in range(8):
             out_ref[8 * g + j, 0:32] = tiles[j].astype(BF16)
 
-    low = jnp.where(
-        lanes_of((288, 128)) < 96, sums_second[...], pltpu.roll(sums_first[...], 96, 1)
-    )
-    rest = pltpu.roll(sums_first[...], 96, 1)
-    packed[0:288] = low
+    rest = pltpu.roll(sums_first, 96, 1)
+    packed[0:288] = jnp.where(lanes_of((288, 128)) < 96, sums_second, rest)
     packed[288:432] = jnp.where(
         lanes_of((144, 128)) < 64, rest[0:144], pltpu.roll(rest[144:288], 64, 1)
     )
@@ -277,24 +283,38 @@
         first_ref[at[2]] = damped(far[:, 32:64], d_first_ref[at[2]])
 
 
-def cell_masks(column, width):
-    at = jnp.concatenate([jnp.arange(8) - 2, jnp.arange(8) - 1]).astype(jnp.int32) + column
-    inside = (at >= 0) & (at < width)
-    return jnp.broadcast_to(inside[:, None, None], (16, 32, 128)).astype(F32)
-
-
-def filters(w_first, v_first, w_second, v_second):
-    flipped = jnp.transpose(jnp.flip(w_second, (0, 1, 2)), (0, 1, 2, 4, 3))
-    stacked = jnp.stack([w_first, v_first, w_second, v_second, flipped])
-    return jnp.transpose(stacked, (0, 2, 5, 3, 1, 4)).reshape(480, 288)
+def filters(w_first_ref, v_first_ref, w_second_ref, v_second_ref, rows_ref, joint_ref):
+    def tall(ref):
+        return jnp.concatenate(
+            [
+                jnp.concatenate(
+                    [ref[9 * (k % 3) + 3 * row + k // 3].astype(F32) for k in range(9)], axis=0
+                )
+                for row in range(3)
+            ],
+            axis=1,
+        )
+
+    def turned(refs):
+        return jnp.concatenate([tall(ref) for ref in refs], axis=0).T.astype(BF16)
+
+    rows_ref[0:96] = turned([w_first_ref])
+    rows_ref[96:192] = turned([v_first_ref])
+    joint_ref[...] = turned([w_second_ref, v_second_ref])
+    for row in range(3):
+        blocks = [
+            w_second_ref[26 - (9 * (k % 3) + 3 * row + k // 3)].astype(F32) for k in range(9)
+        ]
+        rows_ref[192 + 32 * row : 224 + 32 * row] = jnp.concatenate(blocks, axis=1).astype(BF16)
 
 
 def call(kernel, operands, outputs, scratch, name, limit, flops):
     vmem = pl.BlockSpec(memory_space=pltpu.VMEM)
+    smem = pl.BlockSpec(memory_space=pltpu.SMEM)
     return pl.pallas_call(
         kernel,
         out_shape=tuple(jax.ShapeDtypeStruct(shape, dtype) for shape, dtype in outputs),
-        in_specs=[vmem] * len(operands),
+        in_specs=[smem if x.dtype == jnp.int32 else vmem for x in operands],
         out_specs=(vmem,) * len(outputs),
         scratch_shapes=[pltpu.VMEM(shape, dtype) for shape, dtype in scratch],
         compiler_params=pltpu.CompilerParams(vmem_limit_bytes=limit << 20),
@@ -314,36 +334,47 @@
     (sent,) = call(pack, (volume,), [((members,) + small, BF16)], [((1024, 128), F32)], "pack", 8, 10**8)
     parts = lax.all_to_all(sent, GROUP, 0, 0)
 
-    member = lax.axis_index("gx") * n_gy + lax.axis_index("gy")
-    place = jnp.sum(jnp.where(jnp.array(LINE) == member, jnp.arange(members), 0)).astype(jnp.int32)
-    masks = cell_masks(OWN * (lax.axis_index("gz") * members + place), width * n_gz)
-    weights = filters(w_first, v_first, w_second, v_second)
+    z = (lax.axis_index("gy") // 4) * 4 + lax.axis_index("gx")
+    x = lax.axis_index("gy") & 3
+    place = jnp.where(x == 0, 31 - z, 3 * z + jnp.where((z & 1) == 0, x - 1, 3 - x))
+    odd = (place & 1).reshape(1)
+    column = (OWN * (lax.axis_index("gz") * members + place)).reshape(1)
+    blocks = [w.reshape(27, channels, channels) for w in (w_first, v_first, w_second, v_second)]
+    weights = call(
+        filters, blocks, [((288, 288), BF16), ((96, 576), BF16)], [], "filters", 8, 2 * 10**8
+    )
     damping = tuple(
         factor * 0.1 * v.astype(F32).reshape(27, channels, channels) for v in (v_first, v_second)
     )
-    parts, masks, weights, damping = lax.optimization_barrier((parts, masks, weights, damping))
-
-    (own,) = call(arrange, (parts,), [((OWN, 256, 128), BF16)], [], "arrange", 8, 10**8)
-
-    def device(at):
-        return LINE[at % members] * n_gz + at // members
-
-    onward = [(device(i), device(i + 1)) for i in range(members * n_gz - 1)]
-    left = lax.ppermute(own[1:], AXES, onward)
-    right = lax.ppermute(own[:3], AXES, [(b, a) for a, b in onward])
+    parts, odd, column, weights, damping = lax.optimization_barrier(
+        (parts, odd, column, weights, damping)
+    )
+
+    halo = ((OWN - 1, 256, 128), BF16)
+    own, first, second = call(
+        arrange, (parts, odd), [((OWN, 256, 128), BF16), halo, halo], [], "arrange", 8, 10**8
+    )
+
+    def swapped(start):
+        def device(at):
+            return LINE[at % members] * n_gz + at // members
+
+        pairs = [(device(i), device(i + 1)) for i in range(start, members * n_gz - 1, 2)]
+        return pairs + [(b, a) for a, b in pairs]
+
+    first = lax.ppermute(first, AXES, swapped(0))
+    second = lax.ppermute(second, AXES, swapped(1))
 
     (leaving,) = call(
-        layers,
-        (own, left, right, weights, masks),
+        lambda *refs: layers(width * n_gz, *refs),
+        (own, first, second, odd, *weights, column),
         [((members, 64, 128), BF16)],
         [
-            ((10, 320, 128), BF16),
-            ((8, 320, 128), BF16),
-            ((8, 320, 128), BF16),
-            ((6, 320, 128), BF16),
-            ((8, PLANES) + small, F32),
-            ((288, 128), F32),
-            ((288, 128), F32),
+            ((10, 256, 128), BF16),
+            ((8, 256, 128), BF16),
+            ((8, 256, 128), BF16),
+            ((6, 256, 128), BF16),
+            ((OWN, PLANES) + small, F32),
             ((512, 128), F32),
         ],
         "layers",

time: 98.3 us -> 92 us (0.936)
  Pallas kernels: 15.8 us -> 13.4 us
  local copies, waits for them, and re-layouts: 3.23 us -> 0.96 us
  starting transfers between devices: 22.9 us -> 21.2 us
  blocking collectives: 31.1 us -> 32.1 us
    all_to_all x1, waiting for transfers between devices: 8.16 us -> 11 us  [body(): parts = lax.all_to_all(sent, GROUP, 0, 0)]
    pallas_call x7 -> x8, Pallas kernels: 15.8 us -> 13.4 us  [call(): pl.pallas_call(kernel, out_shape=tuple((jax.ShapeDtypeStruct(shape, dtype...]
    ppermute x2, waiting for transfers between devices: 6.56 us -> 4.19 us  [the longest x1 4.19 us: body(): second = lax.ppermute(second, AXES, swapped(1))]
    ppermute x2, starting transfers between devices: 7.03 us -> 5.38 us  [the longest x1 4.46 us: body(): second = lax.ppermute(second, AXES, swapped(1))]
  transfers between devices with their start and end apart: 4 -> 4, of which waited for: 4 -> 3; matrix products, arithmetic and copies ran while one was open for 3% -> 0% of each run, Pallas kernels for 2% -> 2%
where the time goes in v6:
time: 92 us; the launch traced here: 91.6 us
  blocking collectives  32.1 us (35%)
  waiting for transfers between devices  23 us (25%)
  starting transfers between devices  21.2 us (23%)
  Pallas kernels  13.4 us (15%)
  local copies, waits for them, and re-layouts  0.96 us (1%)
    all_to_all x1, blocking collectives, body(): parts = lax.all_to_all(leaving, GROUP, 0, 0)  19.6 us
    pallas_call x8, Pallas kernels, call(): pl.pallas_call(kernel, out_shape=tuple((jax.ShapeDtypeStruct(shape, dtype...  13.4 us
    all_to_all x1, blocking collectives, body(): sums = lax.all_to_all(sums, 'gz', 0, 0)  12.6 us
    all_to_all x1, starting transfers between devices, body(): parts = lax.all_to_all(sent, GROUP, 0, 0)  12 us
    all_to_all x1, waiting for transfers between devices, body(): parts = lax.all_to_all(sent, GROUP, 0, 0)  11 us
    all_to_all x1, waiting for transfers between devices, body(): every = lax.all_to_all(every, GROUP, 0, 0).reshape(512, 128)  7.85 us
    ppermute x1, starting transfers between devices, body(): second = lax.ppermute(second, AXES, swapped(1))  4.46 us
    ppermute x1, waiting for transfers between devices, body(): second = lax.ppermute(second, AXES, swapped(1))  4.19 us
  transfers between devices with their start and end apart: 4, of which 3 were waited for; matrix products, arithmetic and copies ran while one was open for 0% of the time, Pallas kernels for 2%

profile of v6, /device:TPU:1, one launch (start us, length us, event | category | flops | bytes accessed | tf_op | source)
XLA Modules:
  0.0 91.6 jit_solution(8031407200758973197)
XLA Ops:
  0.6 0.0 copy-start.2
  0.6 0.9 %copy-done.2 = bf16[32,2,16,128]{3,2,1,0:T(8,128)(2,1)S(1)} copy-done((bf16[32,2,16,128]{3,2,1,0:T(8,128)(2,1)S(1)}, bf16[32,2,16,128]{3,2,1,0:T(8,128)(2,1)}, u32[]{:S(2)}) %copy-start.2) | copy-done | bytes 262168
  1.6 0.0 copy-start.3
  1.6 0.0 copy-start.4
  1.6 1.6 %pack.1 = bf16[32,32,128]{2,1,0:T(8,128)(2,1)} custom-call(bf16[32,2,16,128]{3,2,1,0:T(8,128)(2,1)S(1)} %copy-done.2), custom_call_target="tpu_custom_call" | custom-call | flops 100000000 | bytes 1048576 | tf_op jit(solution)/shard_map/pack/pallas_call | solution.py:314
  3.2 0.0 copy-start
  3.2 0.0 copy-start.1
  3.2 12.0 %all-to-all-start = ((bf16[32,32,128]{2,1,0:T(8,128)(2,1)}), bf16[32,32,128]{2,1,0:T(8,128)(2,1)S(1)}, u32[]{:S(2)}, u32[]{:S(2)}) async-start(bf16[32,32,128]{2,1,0:T(8,128)(2,1)} %pack.1), calls=%async_computation | async-start | bytes 524288 | tf_op jit(solution)/shard_map/all_to_all | solution.py:335
  15.2 0.0 copy-done.3
  15.2 0.0 copy-done.4
  15.2 0.0 copy-done
  15.2 0.0 copy-done.1
  15.2 0.5 filters.1
  15.8 11.0 %all-to-all-done.parts_ref = bf16[32,32,128]{2,1,0:T(8,128)(2,1)S(1)} async-done(((bf16[32,32,128]{2,1,0:T(8,128)(2,1)}), bf16[32,32,128]{2,1,0:T(8,128)(2,1)S(1)}, u32[]{:S(2)}, u32[]{:S(2)}) %all-to-all-start) | async-done | bytes 262176 | tf_op jit(solution)/shard_map/all_to_all | solution.py:335
  26.8 0.6 arrange.1
  27.4 0.9 %collective-permute-start = (bf16[3,256,128]{2,1,0:T(8,128)(2,1)S(1)}, bf16[3,256,128]{2,1,0:T(8,128)(2,1)S(1)}, u32[]{:S(2)}, u32[]{:S(2)}) collective-permute-start(bf16[3,256,128]{2,1,0:T(8,128)(2,1)S(1)} %get-tuple-element.22), channel_id=1, source_target_pairs={{8,16},{24,88},{80,72},{136,144},{152,216},{208,200},{40,48},{56,1... | collective-permute-start | bytes 589832 | tf_op jit(solution)/shard_map/ppermute | solution.py:365
  28.3 4.5 %collective-permute-start.1 = (bf16[3,256,128]{2,1,0:T(8,128)(2,1)S(1)}, bf16[3,256,128]{2,1,0:T(8,128)(2,1)S(1)}, u32[]{:S(2)}, u32[]{:S(2)}) collective-permute-start(bf16[3,256,128]{2,1,0:T(8,128)(2,1)S(1)} %get-tuple-element.23), channel_id=1, source_target_pairs={{16,24},{88,80},{72,136},{144,152},{216,208},{200,40},{48,56},{120... | collective-permute-start | bytes 589832 | tf_op jit(solution)/shard_map/ppermute | solution.py:366
  32.8 0.0 collective-permute-done.refs_1_
  32.8 4.2 %collective-permute-done.1.refs_2_ = bf16[3,256,128]{2,1,0:T(8,128)(2,1)S(1)} collective-permute-done((bf16[3,256,128]{2,1,0:T(8,128)(2,1)S(1)}, bf16[3,256,128]{2,1,0:T(8,128)(2,1)S(1)}, u32[]{:S(2)}, u32[]{:S(2)}) %collective-permute-start.1) | collective-permute-done | bytes 196640 | tf_op jit(solution)/shard_map/ppermute | solution.py:366
  37.0 5.7 %layers.1 = bf16[32,64,128]{2,1,0:T(8,128)(2,1)S(1)} custom-call(bf16[4,256,128]{2,1,0:T(8,128)(2,1)S(1)} %get-tuple-element.21.refs_0_, bf16[3,256,128]{2,1,0:T(8,128)(2,1)S(1)} %collective-permute-done.refs_1_, bf16[3,256,128]{2,1,0:T(8,128)(2,1)S(1)} %collective-permute-done.1.refs_2_, s32[1]{0:T(128)} %bitcast.odd_ref.refs_3_, ...), custom_call_target="tpu_custom_call" | custom-call | flops 8000000000 | bytes 1048576 | tf_op jit(solution)/shard_map/layers/pallas_call | solution.py:314
  42.7 19.6 %all_to_all.20.parts_ref = bf16[32,64,128]{2,1,0:T(8,128)(2,1)S(1)} all-to-all(bf16[32,64,128]{2,1,0:T(8,128)(2,1)S(1)} %layers.1), channel_id=1, replica_groups=mesh['gx'=4,'gy'=8,'gz'=8] {'gx','gy'}, dimensions={0} | all-to-all | bytes 1048576 | tf_op jit(solution)/shard_map/all_to_all | solution.py:385
  62.3 12.6 %all_to_all.21.parts_ref = f32[8,16,128]{2,1,0:T(8,128)S(1)} all-to-all(f32[8,16,128]{2,1,0:T(8,128)S(1)} %gather_sums.1), channel_id=1, replica_groups=mesh['gx'=4,'gy'=8,'gz'=8] {'gz'}, dimensions={0} | all-to-all | bytes 131072 | tf_op jit(solution)/shard_map/all_to_all | solution.py:387
  74.9 0.7 combine.1
  75.5 3.9 %all-to-all-start.3 = ((bf16[32,16,128]{2,1,0:T(8,128)(2,1)}), bf16[32,16,128]{2,1,0:T(8,128)(2,1)S(1)}, u32[]{:S(2)}, u32[]{:S(2)}) async-start(bf16[32,16,128]{2,1,0:T(8,128)(2,1)} %combine.1), calls=%async_computation.3 | async-start | bytes 262144 | tf_op jit(solution)/shard_map/all_to_all | solution.py:389
  79.4 1.7 %unpack.1 = bf16[32,2,16,128]{3,2,1,0:T(8,128)(2,1)} custom-call(bf16[32,64,128]{2,1,0:T(8,128)(2,1)S(1)} %all_to_all.20.parts_ref), custom_call_target="tpu_custom_call" | custom-call | flops 1000000000 | bytes 1048576 | tf_op jit(solution)/shard_map/unpack/pallas_call | solution.py:314
  81.1 7.9 %all-to-all-done.3 = bf16[32,16,128]{2,1,0:T(8,128)(2,1)S(1)} async-done(((bf16[32,16,128]{2,1,0:T(8,128)(2,1)}), bf16[32,16,128]{2,1,0:T(8,128)(2,1)S(1)}, u32[]{:S(2)}, u32[]{:S(2)}) %all-to-all-start.3) | async-done | bytes 131104 | tf_op jit(solution)/shard_map/all_to_all | solution.py:389
  88.9 2.7 %finish.1 = (f32[27,32,32]{2,1,0:T(8,128)}, f32[27,32,32]{2,1,0:T(8,128)}) custom-call(bf16[512,128]{1,0:T(8,128)(2,1)S(1)} %bitcast.15, f32[27,32,32]{2,1,0:T(8,128)S(1)} %bitcast.11, f32[27,32,32]{2,1,0:T(8,128)S(1)} %bitcast.12), custom_call_target="tpu_custom_call" | custom-call | flops 100000000 | bytes 1048576 | tf_op jit(solution)/shard_map/finish/pallas_call | solution.py:314
  (3 shorter events, 0.1 us)
Async XLA Ops:
  0.6 1.0 %copy-start.2 = (bf16[32,2,16,128]{3,2,1,0:T(8,128)(2,1)S(1)}, bf16[32,2,16,128]{3,2,1,0:T(8,128)(2,1)}, u32[]{:S(2)}) copy-start(bf16[32,2,16,128]{3,2,1,0:T(8,128)(2,1)} %cells_ref.1) | copy-start | bytes 786436
  1.6 13.6 %copy-start.3 = (bf16[3,3,3,32,32]{4,3,2,1,0:T(8,128)(2,1)S(1)}, bf16[3,3,3,32,32]{4,3,2,1,0:T(8,128)(2,1)}, u32[]{:S(2)}) copy-start(bf16[3,3,3,32,32]{4,3,2,1,0:T(8,128)(2,1)} %param.6) | copy-start | bytes 165892
  1.6 13.6 %copy-start.4 = (bf16[3,3,3,32,32]{4,3,2,1,0:T(8,128)(2,1)S(1)}, bf16[3,3,3,32,32]{4,3,2,1,0:T(8,128)(2,1)}, u32[]{:S(2)}) copy-start(bf16[3,3,3,32,32]{4,3,2,1,0:T(8,128)(2,1)} %param.7) | copy-start | bytes 165892
  3.2 12.1 %copy-start = (bf16[3,3,3,32,32]{4,3,2,1,0:T(8,128)(2,1)S(1)}, bf16[3,3,3,32,32]{4,3,2,1,0:T(8,128)(2,1)}, u32[]{:S(2)}) copy-start(bf16[3,3,3,32,32]{4,3,2,1,0:T(8,128)(2,1)} %param.8) | copy-start | bytes 165892
  3.2 12.1 %copy-start.1 = (bf16[3,3,3,32,32]{4,3,2,1,0:T(8,128)(2,1)S(1)}, bf16[3,3,3,32,32]{4,3,2,1,0:T(8,128)(2,1)}, u32[]{:S(2)}) copy-start(bf16[3,3,3,32,32]{4,3,2,1,0:T(8,128)(2,1)} %param.9) | copy-start | bytes 165892
  3.2 23.7 %all-to-all-start = ((bf16[32,32,128]{2,1,0:T(8,128)(2,1)}), bf16[32,32,128]{2,1,0:T(8,128)(2,1)S(1)}, u32[]{:S(2)}, u32[]{:S(2)}) async-start(bf16[32,32,128]{2,1,0:T(8,128)(2,1)} %pack.1), calls=%async_computation | async-start | bytes 524288 | tf_op jit(solution)/shard_map/all_to_all | solution.py:335
  27.4 5.4 %collective-permute-start = (bf16[3,256,128]{2,1,0:T(8,128)(2,1)S(1)}, bf16[3,256,128]{2,1,0:T(8,128)(2,1)S(1)}, u32[]{:S(2)}, u32[]{:S(2)}) collective-permute-start(bf16[3,256,128]{2,1,0:T(8,128)(2,1)S(1)} %get-tuple-element.22), channel_id=1, source_target_pairs={{8,16},{24,88},{80,72},{136,144},{152,216},{208,200},{40,48},{56,1... | collective-permute-start | bytes 589832 | tf_op jit(solution)/shard_map/ppermute | solution.py:365
  28.3 8.7 %collective-permute-start.1 = (bf16[3,256,128]{2,1,0:T(8,128)(2,1)S(1)}, bf16[3,256,128]{2,1,0:T(8,128)(2,1)S(1)}, u32[]{:S(2)}, u32[]{:S(2)}) collective-permute-start(bf16[3,256,128]{2,1,0:T(8,128)(2,1)S(1)} %get-tuple-element.23), channel_id=1, source_target_pairs={{16,24},{88,80},{72,136},{144,152},{216,208},{200,40},{48,56},{120... | collective-permute-start | bytes 589832 | tf_op jit(solution)/shard_map/ppermute | solution.py:366
  75.5 13.4 %all-to-all-start.3 = ((bf16[32,16,128]{2,1,0:T(8,128)(2,1)}), bf16[32,16,128]{2,1,0:T(8,128)(2,1)S(1)}, u32[]{:S(2)}, u32[]{:S(2)}) async-start(bf16[32,16,128]{2,1,0:T(8,128)(2,1)} %combine.1), calls=%async_computation.3 | async-start | bytes 262144 | tf_op jit(solution)/shard_map/all_to_all | solution.py:389

commit v7 on v6

--- a/solution.py
+++ b/solution.py
@@ -60,14 +60,11 @@
 
 def pack(cells_ref, out_ref, sorted_ref):
     sorted_ref[...] = jnp.dot(
-        cells_ref[...].reshape(1024, 128), permutation(False), preferred_element_type=F32
-    )
-    for part in range(2):
-        at = slice(16 * part, 16 * part + 16)
-        tiles = [sorted_ref[pl.ds(512 * part + i, 16, stride=32)] for i in range(32)]
-        tiles = exchange(tiles, (0, 1, 2, 3, 4))
-        for i in range(MEMBERS):
-            out_ref[LINE[i], at] = tiles[i].astype(BF16)
+        cells_ref[...].reshape(256, 128), permutation(False), preferred_element_type=F32
+    )
+    tiles = exchange([sorted_ref[pl.ds(i, 8, stride=32)] for i in range(32)], (0, 1, 2, 3, 4))
+    for i in range(MEMBERS):
+        out_ref[LINE[i]] = tiles[i].astype(BF16)
 
 
 def arrange(parts_ref, odd_ref, own_ref, first_ref, second_ref):
@@ -246,16 +243,11 @@
     )
     packed[432:512] = jnp.zeros((80, 128), F32)
     for member in range(MEMBERS):
-        rows = packed[16 * member : 16 * member + 16]
-        high = rows.astype(BF16)
-        out_ref[member, 32:48] = high
-        out_ref[member, 48:64] = (rows - high.astype(F32)).astype(BF16)
+        out_ref[member, 32:48] = packed[16 * member : 16 * member + 16].astype(BF16)
 
 
 def gather_sums(parts_ref, out_ref):
-    total = jnp.sum(
-        parts_ref[:, 32:48].astype(F32) + parts_ref[:, 48:64].astype(F32), axis=0
-    )
+    total = jnp.sum(parts_ref[:, 32:48].astype(F32), axis=0)
     for member in range(8):
         out_ref[member] = total
 
@@ -266,21 +258,28 @@
         out_ref[member] = total
 
 
-def finish(scale, packed_ref, d_first_ref, d_second_ref, first_ref, second_ref):
+def finish(scale, packed_ref, d_first_ref, d_second_ref, first_ref, second_ref, rest_ref):
+    depth = pl.program_id(0)
+
+    @pl.when(depth == 0)
+    def _():
+        rest = packed_ref[288:432, :].astype(F32)
+        rest_ref[0:144] = rest
+        rest_ref[144:288] = pltpu.roll(rest, 64, 1)
+
     def damped(summed, damping):
         return scale * summed + damping
 
-    rest = packed_ref[288:432, :].astype(F32)
-    rest = jnp.concatenate([rest, pltpu.roll(rest, 64, 1)], axis=0)
-    for block in range(9):
-        low = packed_ref[32 * block : 32 * block + 32, :].astype(F32)
-        far = rest[32 * block : 32 * block + 32]
-        at = [9 * (block % 3) + 3 * row + block // 3 for row in range(3)]
+    for column in range(3):
+        block = pl.ds(pl.multiple_of(96 * column + 32 * depth, 32), 32)
+        low = packed_ref[block, :].astype(F32)
+        far = rest_ref[block, :]
         for row in range(3):
-            second_ref[at[row]] = damped(low[:, 32 * row : 32 * row + 32], d_second_ref[at[row]])
-        first_ref[at[0]] = damped(low[:, 96:128], d_first_ref[at[0]])
-        first_ref[at[1]] = damped(far[:, 0:32], d_first_ref[at[1]])
-        first_ref[at[2]] = damped(far[:, 32:64], d_first_ref[at[2]])
+            at = 3 * row + column
+            second_ref[at] = damped(low[:, 32 * row : 32 * row + 32], d_second_ref[at])
+        first_ref[column] = damped(low[:, 96:128], d_first_ref[column])
+        first_ref[3 + column] = damped(far[:, 0:32], d_first_ref[3 + column])
+        first_ref[6 + column] = damped(far[:, 32:64], d_first_ref[6 + column])
 
 
 def filters(w_first_ref, v_first_ref, w_second_ref, v_second_ref, rows_ref, joint_ref):
@@ -331,7 +330,16 @@
     factor = math.sqrt(27.0 * channels)
     small = (channels, 128)
 
-    (sent,) = call(pack, (volume,), [((members,) + small, BF16)], [((1024, 128), F32)], "pack", 8, 10**8)
+    sent = pl.pallas_call(
+        pack,
+        grid=(channels // 8,),
+        out_shape=jax.ShapeDtypeStruct((members,) + small, BF16),
+        in_specs=[pl.BlockSpec((8, depth, height, width), lambda i: (i, 0, 0, 0))],
+        out_specs=pl.BlockSpec((members, 8, 128), lambda i: (0, i, 0)),
+        scratch_shapes=[pltpu.VMEM((256, 128), F32)],
+        compiler_params=pltpu.CompilerParams(dimension_semantics=("arbitrary",)),
+        name="pack",
+    )(volume)
     parts = lax.all_to_all(sent, GROUP, 0, 0)
 
     z = (lax.axis_index("gy") // 4) * 4 + lax.axis_index("gx")
@@ -368,7 +376,7 @@
     (leaving,) = call(
         lambda *refs: layers(width * n_gz, *refs),
         (own, first, second, odd, *weights, column),
-        [((members, 64, 128), BF16)],
+        [((members, 48, 128), BF16)],
         [
             ((10, 256, 128), BF16),
             ((8, 256, 128), BF16),
@@ -396,15 +404,19 @@
         8,
         10**9,
     )
-    gv_first, gv_second = call(
+    third = pl.BlockSpec((9, channels, channels), lambda i: (i, 0, 0))
+    gv_first, gv_second = pl.pallas_call(
         lambda *refs: finish(factor / count_all, *refs),
-        (every,) + damping,
-        [((27, channels, channels), F32)] * 2,
-        [],
-        "finish",
-        8,
-        10**8,
-    )
+        grid=(3,),
+        out_shape=(jax.ShapeDtypeStruct((27, channels, channels), F32),) * 2,
+        in_specs=[pl.BlockSpec((512, 128), lambda i: (0, 0)), third, third],
+        out_specs=(third, third),
+        scratch_shapes=[pltpu.VMEM((288, 128), F32)],
+        compiler_params=pltpu.CompilerParams(
+            dimension_semantics=("arbitrary",), vmem_limit_bytes=8 << 20
+        ),
+        name="finish",
+    )(every, *damping)
     return (out, gv_first.reshape(v_first.shape), gv_second.reshape(v_first.shape))
 
 

time: 92 us -> 90.2 us (0.980)
  blocking collectives: 32.1 us -> 29.5 us
  Pallas kernels: 13.4 us -> 15.1 us
  local copies, waits for them, and re-layouts: 0.96 us -> 0.02 us
    pallas_call x0 -> x2, Pallas kernels: none -> 6.07 us  [the longest x1 4.21 us: body(): pl.pallas_call(pack, grid=(channels // 8,), out_shape=jax.ShapeDtypeStruc...]
    pallas_call x8 -> x6, Pallas kernels: 13.4 us -> 9.06 us  [call(): pl.pallas_call(kernel, out_shape=tuple((jax.ShapeDtypeStruct(shape, dtype...]
    all_to_all x1, blocking collectives: 19.6 us -> 17.1 us  [body(): parts = lax.all_to_all(leaving, GROUP, 0, 0)]
    unnamed x10 -> x8, local copies, waits for them, and re-layouts: 0.96 us -> 0.02 us
where the time goes in v7:
time: 90.2 us; the launch traced here: 89.8 us
  blocking collectives  29.5 us (33%)
  waiting for transfers between devices  23 us (25%)
  starting transfers between devices  21.2 us (24%)
  Pallas kernels  15.1 us (17%)
    all_to_all x1, blocking collectives, body(): parts = lax.all_to_all(leaving, GROUP, 0, 0)  17.1 us
    all_to_all x1, blocking collectives, body(): sums = lax.all_to_all(sums, 'gz', 0, 0)  12.4 us
    all_to_all x1, starting transfers between devices, body(): parts = lax.all_to_all(sent, GROUP, 0, 0)  12 us
    all_to_all x1, waiting for transfers between devices, body(): parts = lax.all_to_all(sent, GROUP, 0, 0)  11 us
    pallas_call x6, Pallas kernels, call(): pl.pallas_call(kernel, out_shape=tuple((jax.ShapeDtypeStruct(shape, dtype...  9.06 us
    all_to_all x1, waiting for transfers between devices, body(): every = lax.all_to_all(every, GROUP, 0, 0).reshape(512, 128)  7.85 us
    ppermute x1, starting transfers between devices, body(): second = lax.ppermute(second, AXES, swapped(1))  4.45 us
    pallas_call x1, Pallas kernels, body(): pl.pallas_call(pack, grid=(channels // 8,), out_shape=jax.ShapeDtypeStruc...  4.21 us
  transfers between devices with their start and end apart: 4, of which 3 were waited for; matrix products, arithmetic and copies ran while one was open for 0% of the time, Pallas kernels for 2%

profile of v7, /device:TPU:1, one launch (start us, length us, event | category | flops | bytes accessed | tf_op | source)
XLA Modules:
  0.0 89.8 jit_solution(6464263184992746817)
XLA Ops:
  0.6 0.0 copy-start.2
  0.6 0.0 copy-start.3
  0.7 4.2 %pack.1 = bf16[32,32,128]{2,1,0:T(8,128)(2,1)} custom-call(bf16[32,2,16,128]{3,2,1,0:T(8,128)(2,1)} %cells_ref.1), custom_call_target="tpu_custom_call" | custom-call | tf_op jit(solution)/shard_map/pack/pallas_call | solution.py:333
  4.9 0.0 copy-start
  4.9 0.0 copy-start.1
  4.9 12.0 %all-to-all-start = ((bf16[32,32,128]{2,1,0:T(8,128)(2,1)}), bf16[32,32,128]{2,1,0:T(8,128)(2,1)S(1)}, u32[]{:S(2)}, u32[]{:S(2)}) async-start(bf16[32,32,128]{2,1,0:T(8,128)(2,1)} %pack.1), calls=%async_computation | async-start | bytes 524288 | tf_op jit(solution)/shard_map/all_to_all | solution.py:343
  16.9 0.0 copy-done.2
  16.9 0.0 copy-done.3
  16.9 0.0 copy-done
  16.9 0.0 copy-done.1
  16.9 0.5 filters.1
  17.5 11.0 %all-to-all-done.parts_ref = bf16[32,32,128]{2,1,0:T(8,128)(2,1)S(1)} async-done(((bf16[32,32,128]{2,1,0:T(8,128)(2,1)}), bf16[32,32,128]{2,1,0:T(8,128)(2,1)S(1)}, u32[]{:S(2)}, u32[]{:S(2)}) %all-to-all-start) | async-done | bytes 262176 | tf_op jit(solution)/shard_map/all_to_all | solution.py:343
  28.5 0.6 arrange.1
  29.1 0.9 %collective-permute-start = (bf16[3,256,128]{2,1,0:T(8,128)(2,1)S(1)}, bf16[3,256,128]{2,1,0:T(8,128)(2,1)S(1)}, u32[]{:S(2)}, u32[]{:S(2)}) collective-permute-start(bf16[3,256,128]{2,1,0:T(8,128)(2,1)S(1)} %get-tuple-element.22), channel_id=1, source_target_pairs={{8,16},{24,88},{80,72},{136,144},{152,216},{208,200},{40,48},{56,1... | collective-permute-start | bytes 589832 | tf_op jit(solution)/shard_map/ppermute | solution.py:373
  30.0 4.5 %collective-permute-start.1 = (bf16[3,256,128]{2,1,0:T(8,128)(2,1)S(1)}, bf16[3,256,128]{2,1,0:T(8,128)(2,1)S(1)}, u32[]{:S(2)}, u32[]{:S(2)}) collective-permute-start(bf16[3,256,128]{2,1,0:T(8,128)(2,1)S(1)} %get-tuple-element.23), channel_id=1, source_target_pairs={{16,24},{88,80},{72,136},{144,152},{216,208},{200,40},{48,56},{120... | collective-permute-start | bytes 589832 | tf_op jit(solution)/shard_map/ppermute | solution.py:374
  34.5 0.0 collective-permute-done.refs_1_
  34.5 4.2 %collective-permute-done.1.refs_2_ = bf16[3,256,128]{2,1,0:T(8,128)(2,1)S(1)} collective-permute-done((bf16[3,256,128]{2,1,0:T(8,128)(2,1)S(1)}, bf16[3,256,128]{2,1,0:T(8,128)(2,1)S(1)}, u32[]{:S(2)}, u32[]{:S(2)}) %collective-permute-start.1) | collective-permute-done | bytes 196640 | tf_op jit(solution)/shard_map/ppermute | solution.py:374
  38.7 5.7 %layers.1 = bf16[32,48,128]{2,1,0:T(8,128)(2,1)S(1)} custom-call(bf16[4,256,128]{2,1,0:T(8,128)(2,1)S(1)} %get-tuple-element.21.refs_0_, bf16[3,256,128]{2,1,0:T(8,128)(2,1)S(1)} %collective-permute-done.refs_1_, bf16[3,256,128]{2,1,0:T(8,128)(2,1)S(1)} %collective-permute-done.1.refs_2_, s32[1]{0:T(128)} %bitcast.odd_ref.refs_3_, ...), custom_call_target="tpu_custom_call" | custom-call | flops 8000000000 | bytes 1048576 | tf_op jit(solution)/shard_map/layers/pallas_call | solution.py:313
  44.3 17.1 %all_to_all.20.parts_ref = bf16[32,48,128]{2,1,0:T(8,128)(2,1)S(1)} all-to-all(bf16[32,48,128]{2,1,0:T(8,128)(2,1)S(1)} %layers.1), channel_id=1, replica_groups=mesh['gx'=4,'gy'=8,'gz'=8] {'gx','gy'}, dimensions={0} | all-to-all | bytes 786432 | tf_op jit(solution)/shard_map/all_to_all | solution.py:393
  61.5 12.4 %all_to_all.21.parts_ref = f32[8,16,128]{2,1,0:T(8,128)S(1)} all-to-all(f32[8,16,128]{2,1,0:T(8,128)S(1)} %gather_sums.1), channel_id=1, replica_groups=mesh['gx'=4,'gy'=8,'gz'=8] {'gz'}, dimensions={0} | all-to-all | bytes 131072 | tf_op jit(solution)/shard_map/all_to_all | solution.py:395
  73.9 0.7 combine.1
  74.5 3.9 %all-to-all-start.3 = ((bf16[32,16,128]{2,1,0:T(8,128)(2,1)}), bf16[32,16,128]{2,1,0:T(8,128)(2,1)S(1)}, u32[]{:S(2)}, u32[]{:S(2)}) async-start(bf16[32,16,128]{2,1,0:T(8,128)(2,1)} %combine.1), calls=%async_computation.3 | async-start | bytes 262144 | tf_op jit(solution)/shard_map/all_to_all | solution.py:397
  78.4 1.7 %unpack.1 = bf16[32,2,16,128]{3,2,1,0:T(8,128)(2,1)} custom-call(bf16[32,48,128]{2,1,0:T(8,128)(2,1)S(1)} %all_to_all.20.parts_ref), custom_call_target="tpu_custom_call" | custom-call | flops 1000000000 | bytes 1048576 | tf_op jit(solution)/shard_map/unpack/pallas_call | solution.py:313
  80.1 7.9 %all-to-all-done.3 = bf16[32,16,128]{2,1,0:T(8,128)(2,1)S(1)} async-done(((bf16[32,16,128]{2,1,0:T(8,128)(2,1)}), bf16[32,16,128]{2,1,0:T(8,128)(2,1)S(1)}, u32[]{:S(2)}, u32[]{:S(2)}) %all-to-all-start.3) | async-done | bytes 131104 | tf_op jit(solution)/shard_map/all_to_all | solution.py:397
  87.9 1.9 %finish.1 = (f32[27,32,32]{2,1,0:T(8,128)}, f32[27,32,32]{2,1,0:T(8,128)}) custom-call(bf16[512,128]{1,0:T(8,128)(2,1)S(1)} %bitcast.15, f32[27,32,32]{2,1,0:T(8,128)S(1)} %bitcast.11, f32[27,32,32]{2,1,0:T(8,128)S(1)} %bitcast.12), custom_call_target="tpu_custom_call" | custom-call | tf_op jit(solution)/shard_map/finish/pallas_call | solution.py:408
  (3 shorter events, 0.1 us)
Async XLA Ops:
  0.6 16.3 %copy-start.2 = (bf16[3,3,3,32,32]{4,3,2,1,0:T(8,128)(2,1)S(1)}, bf16[3,3,3,32,32]{4,3,2,1,0:T(8,128)(2,1)}, u32[]{:S(2)}) copy-start(bf16[3,3,3,32,32]{4,3,2,1,0:T(8,128)(2,1)} %param.6) | copy-start | bytes 165892
  0.6 16.3 %copy-start.3 = (bf16[3,3,3,32,32]{4,3,2,1,0:T(8,128)(2,1)S(1)}, bf16[3,3,3,32,32]{4,3,2,1,0:T(8,128)(2,1)}, u32[]{:S(2)}) copy-start(bf16[3,3,3,32,32]{4,3,2,1,0:T(8,128)(2,1)} %param.7) | copy-start | bytes 165892
  4.9 12.1 %copy-start = (bf16[3,3,3,32,32]{4,3,2,1,0:T(8,128)(2,1)S(1)}, bf16[3,3,3,32,32]{4,3,2,1,0:T(8,128)(2,1)}, u32[]{:S(2)}) copy-start(bf16[3,3,3,32,32]{4,3,2,1,0:T(8,128)(2,1)} %param.8) | copy-start | bytes 165892
  4.9 12.1 %copy-start.1 = (bf16[3,3,3,32,32]{4,3,2,1,0:T(8,128)(2,1)S(1)}, bf16[3,3,3,32,32]{4,3,2,1,0:T(8,128)(2,1)}, u32[]{:S(2)}) copy-start(bf16[3,3,3,32,32]{4,3,2,1,0:T(8,128)(2,1)} %param.9) | copy-start | bytes 165892
  4.9 23.7 %all-to-all-start = ((bf16[32,32,128]{2,1,0:T(8,128)(2,1)}), bf16[32,32,128]{2,1,0:T(8,128)(2,1)S(1)}, u32[]{:S(2)}, u32[]{:S(2)}) async-start(bf16[32,32,128]{2,1,0:T(8,128)(2,1)} %pack.1), calls=%async_computation | async-start | bytes 524288 | tf_op jit(solution)/shard_map/all_to_all | solution.py:343
  29.1 5.4 %collective-permute-start = (bf16[3,256,128]{2,1,0:T(8,128)(2,1)S(1)}, bf16[3,256,128]{2,1,0:T(8,128)(2,1)S(1)}, u32[]{:S(2)}, u32[]{:S(2)}) collective-permute-start(bf16[3,256,128]{2,1,0:T(8,128)(2,1)S(1)} %get-tuple-element.22), channel_id=1, source_target_pairs={{8,16},{24,88},{80,72},{136,144},{152,216},{208,200},{40,48},{56,1... | collective-permute-start | bytes 589832 | tf_op jit(solution)/shard_map/ppermute | solution.py:373
  30.0 8.7 %collective-permute-start.1 = (bf16[3,256,128]{2,1,0:T(8,128)(2,1)S(1)}, bf16[3,256,128]{2,1,0:T(8,128)(2,1)S(1)}, u32[]{:S(2)}, u32[]{:S(2)}) collective-permute-start(bf16[3,256,128]{2,1,0:T(8,128)(2,1)S(1)} %get-tuple-element.23), channel_id=1, source_target_pairs={{16,24},{88,80},{72,136},{144,152},{216,208},{200,40},{48,56},{120... | collective-permute-start | bytes 589832 | tf_op jit(solution)/shard_map/ppermute | solution.py:374
  74.5 13.4 %all-to-all-start.3 = ((bf16[32,16,128]{2,1,0:T(8,128)(2,1)}), bf16[32,16,128]{2,1,0:T(8,128)(2,1)S(1)}, u32[]{:S(2)}, u32[]{:S(2)}) async-start(bf16[32,16,128]{2,1,0:T(8,128)(2,1)} %combine.1), calls=%async_computation.3 | async-start | bytes 262144 | tf_op jit(solution)/shard_map/all_to_all | solution.py:397

commit v8 on v7

--- a/solution.py
+++ b/solution.py
@@ -16,17 +16,29 @@
 MEMBERS = 32
 
 
-def closed_line():
-    def member(z, x):
-        return (z % 4) * 8 + (z // 4) * 4 + x
-
-    line = []
-    for z in range(8):
-        line += [member(z, x) for x in ((1, 2, 3) if z % 2 == 0 else (3, 2, 1))]
-    return tuple(line + [member(z, 0) for z in reversed(range(8))])
-
-
-LINE = closed_line()
+CHIPS = (
+    (
+        0, 1, 11, 10, 13, 3, 2, 12, 22, 23, 20, 21, 31, 32, 33, 30,
+        40, 43, 42, 41, 51, 50, 53, 52, 62, 61, 71, 72, 73, 63, 60, 70,
+    ),
+    (
+        70, 71, 1, 2, 72, 62, 63, 53, 43, 33, 23, 13, 12, 11, 21, 22,
+        32, 42, 52, 51, 61, 60, 50, 40, 41, 31, 30, 20, 10, 0, 3, 73,
+    ),
+)
+LINES = tuple(tuple(c // 10 % 4 * 8 + c // 40 * 4 + c % 10 for c in chips) for chips in CHIPS)
+
+
+def member_at(place):
+    return jnp.where((lax.axis_index("gz") & 1) == 0, LINES[0][place], LINES[1][place])
+
+
+def own_place():
+    member = lax.axis_index("gx") * 8 + lax.axis_index("gy")
+    place = jnp.int32(0)
+    for at in range(MEMBERS):
+        place = jnp.where(member == member_at(at), at, place)
+    return place
 
 
 def lanes_of(shape):
@@ -60,20 +72,22 @@
 
 def pack(cells_ref, out_ref, sorted_ref):
     sorted_ref[...] = jnp.dot(
-        cells_ref[...].reshape(256, 128), permutation(False), preferred_element_type=F32
-    )
-    tiles = exchange([sorted_ref[pl.ds(i, 8, stride=32)] for i in range(32)], (0, 1, 2, 3, 4))
-    for i in range(MEMBERS):
-        out_ref[LINE[i]] = tiles[i].astype(BF16)
-
-
-def arrange(parts_ref, odd_ref, own_ref, first_ref, second_ref):
+        cells_ref[...].reshape(1024, 128), permutation(False), preferred_element_type=F32
+    )
+    for part in range(4):
+        tiles = [sorted_ref[pl.ds(256 * part + i, 8, stride=32)] for i in range(32)]
+        tiles = exchange(tiles, (0, 1, 2, 3, 4))
+        for i in range(MEMBERS):
+            out_ref[member_at(i), 8 * part : 8 * part + 8] = tiles[i].astype(BF16)
+
+
+def arrange(parts_ref, own_ref, first_ref, second_ref):
     for g in range(4):
         tiles = exchange([parts_ref[8 * g + j].astype(F32) for j in range(8)], (4, 5, 6))
         for i in range(8):
             plane = 2 * g + i % 2
             own_ref[i // 2, 32 * plane : 32 * plane + 32] = tiles[i].astype(BF16)
-    odd = odd_ref[0] > 0
+    odd = (own_place() & 1) == 1
 
     @pl.when(odd)
     def _():
@@ -89,7 +103,7 @@
 def unpack(parts_ref, out_ref, mixed_ref):
     for part in range(2):
         at = slice(16 * part, 16 * part + 16)
-        tiles = [parts_ref[LINE[i], at].astype(F32) for i in range(MEMBERS)]
+        tiles = [parts_ref[member_at(i), at].astype(F32) for i in range(MEMBERS)]
         tiles = exchange(tiles, (0, 1, 2, 3, 4))
         for i in range(32):
             mixed_ref[pl.ds(512 * part + i, 16, stride=32)] = tiles[i]
@@ -155,10 +169,8 @@
     own_ref,
     first_ref,
     second_ref,
-    odd_ref,
     weight_ref,
     joint_ref,
-    column_ref,
     out_ref,
     p_vol,
     p_hid,
@@ -167,7 +179,9 @@
     slopes,
     packed,
 ):
-    odd = odd_ref[0] > 0
+    place = own_place()
+    column = OWN * (lax.axis_index("gz") * MEMBERS + place)
+    odd = (place & 1) == 1
 
     @pl.when(odd)
     def _():
@@ -181,9 +195,8 @@
 
     p_vol[3:7] = own_ref[...]
 
-    def inside(column):
-        at = column_ref[0] + column
-        return (at >= 0) & (at < width)
+    def inside(offset):
+        return (column + offset >= 0) & (column + offset < width)
 
     for z in range(0, 8, 2):
         for x in range(PLANES):
@@ -309,11 +322,10 @@
 
 def call(kernel, operands, outputs, scratch, name, limit, flops):
     vmem = pl.BlockSpec(memory_space=pltpu.VMEM)
-    smem = pl.BlockSpec(memory_space=pltpu.SMEM)
     return pl.pallas_call(
         kernel,
         out_shape=tuple(jax.ShapeDtypeStruct(shape, dtype) for shape, dtype in outputs),
-        in_specs=[smem if x.dtype == jnp.int32 else vmem for x in operands],
+        in_specs=[vmem] * len(operands),
         out_specs=(vmem,) * len(outputs),
         scratch_shapes=[pltpu.VMEM(shape, dtype) for shape, dtype in scratch],
         compiler_params=pltpu.CompilerParams(vmem_limit_bytes=limit << 20),
@@ -330,23 +342,11 @@
     factor = math.sqrt(27.0 * channels)
     small = (channels, 128)
 
-    sent = pl.pallas_call(
-        pack,
-        grid=(channels // 8,),
-        out_shape=jax.ShapeDtypeStruct((members,) + small, BF16),
-        in_specs=[pl.BlockSpec((8, depth, height, width), lambda i: (i, 0, 0, 0))],
-        out_specs=pl.BlockSpec((members, 8, 128), lambda i: (0, i, 0)),
-        scratch_shapes=[pltpu.VMEM((256, 128), F32)],
-        compiler_params=pltpu.CompilerParams(dimension_semantics=("arbitrary",)),
-        name="pack",
-    )(volume)
+    (sent,) = call(
+        pack, (volume,), [((members,) + small, BF16)], [((1024, 128), F32)], "pack", 8, 10**8
+    )
     parts = lax.all_to_all(sent, GROUP, 0, 0)
 
-    z = (lax.axis_index("gy") // 4) * 4 + lax.axis_index("gx")
-    x = lax.axis_index("gy") & 3
-    place = jnp.where(x == 0, 31 - z, 3 * z + jnp.where((z & 1) == 0, x - 1, 3 - x))
-    odd = (place & 1).reshape(1)
-    column = (OWN * (lax.axis_index("gz") * members + place)).reshape(1)
     blocks = [w.reshape(27, channels, channels) for w in (w_first, v_first, w_second, v_second)]
     weights = call(
         filters, blocks, [((288, 288), BF16), ((96, 576), BF16)], [], "filters", 8, 2 * 10**8
@@ -354,18 +354,17 @@
     damping = tuple(
         factor * 0.1 * v.astype(F32).reshape(27, channels, channels) for v in (v_first, v_second)
     )
-    parts, odd, column, weights, damping = lax.optimization_barrier(
-        (parts, odd, column, weights, damping)
-    )
+    parts, weights, damping = lax.optimization_barrier((parts, weights, damping))
 
     halo = ((OWN - 1, 256, 128), BF16)
     own, first, second = call(
-        arrange, (parts, odd), [((OWN, 256, 128), BF16), halo, halo], [], "arrange", 8, 10**8
+        arrange, (parts,), [((OWN, 256, 128), BF16), halo, halo], [], "arrange", 8, 10**8
     )
 
     def swapped(start):
         def device(at):
-            return LINE[at % members] * n_gz + at // members
+            gz, place = divmod(at, members)
+            return LINES[gz % 2][place] * n_gz + gz
 
         pairs = [(device(i), device(i + 1)) for i in range(start, members * n_gz - 1, 2)]
         return pairs + [(b, a) for a, b in pairs]
@@ -375,7 +374,7 @@
 
     (leaving,) = call(
         lambda *refs: layers(width * n_gz, *refs),
-        (own, first, second, odd, *weights, column),
+        (own, first, second, *weights),
         [((members, 48, 128), BF16)],
         [
             ((10, 256, 128), BF16),

time: 90.2 us -> 90.1 us (level)
  blocking collectives: 29.5 us -> 32.1 us
  Pallas kernels: 15.1 us -> 12.6 us
  starting transfers between devices: 21.2 us -> 18.8 us
  waiting for transfers between devices: 23 us -> 24.5 us
  local copies, waits for them, and re-layouts: 0.02 us -> 0.96 us
    all_to_all x1, blocking collectives: 17.1 us -> 21.4 us  [body(): parts = lax.all_to_all(leaving, GROUP, 0, 0)]
    pallas_call x1 -> x0, Pallas kernels: 4.21 us -> none  [body(): pl.pallas_call(pack, grid=(channels // 8,), out_shape=jax.ShapeDtypeStruc...]
    ppermute x1, starting transfers between devices: 4.45 us -> 1.98 us  [body(): second = lax.ppermute(second, AXES, swapped(1))]
    pallas_call x6 -> x7, Pallas kernels: 9.06 us -> 10.8 us  [call(): pl.pallas_call(kernel, out_shape=tuple((jax.ShapeDtypeStruct(shape, dtype...]
    ppermute x1, waiting for transfers between devices: 0.01 us -> 1.69 us  [body(): first = lax.ppermute(first, AXES, swapped(0))]
    all_to_all x1, blocking collectives: 12.4 us -> 10.7 us  [body(): sums = lax.all_to_all(sums, 'gz', 0, 0)]
    unnamed x8 -> x10, local copies, waits for them, and re-layouts: 0.02 us -> 0.96 us
  transfers between devices with their start and end apart: 4 -> 4, of which waited for: 3 -> 4; matrix products, arithmetic and copies ran while one was open for 0% -> 0% of each run, Pallas kernels for 2% -> 2%
where the time goes in v8:
time: 90.1 us; the launch traced here: 89.8 us
  blocking collectives  32.1 us (36%)
  waiting for transfers between devices  24.5 us (27%)
  starting transfers between devices  18.8 us (21%)
  Pallas kernels  12.6 us (14%)
  local copies, waits for them, and re-layouts  0.96 us (1%)
    all_to_all x1, blocking collectives, body(): parts = lax.all_to_all(leaving, GROUP, 0, 0)  21.4 us
    all_to_all x1, starting transfers between devices, body(): parts = lax.all_to_all(sent, GROUP, 0, 0)  12 us
    all_to_all x1, waiting for transfers between devices, body(): parts = lax.all_to_all(sent, GROUP, 0, 0)  11 us
    pallas_call x7, Pallas kernels, call(): pl.pallas_call(kernel, out_shape=tuple((jax.ShapeDtypeStruct(shape, dtype...  10.8 us
    all_to_all x1, blocking collectives, body(): sums = lax.all_to_all(sums, 'gz', 0, 0)  10.7 us
    all_to_all x1, waiting for transfers between devices, body(): every = lax.all_to_all(every, GROUP, 0, 0).reshape(512, 128)  7.8 us
    ppermute x1, waiting for transfers between devices, body(): second = lax.ppermute(second, AXES, swapped(1))  3.93 us
    all_to_all x1, starting transfers between devices, body(): every = lax.all_to_all(every, GROUP, 0, 0).reshape(512, 128)  3.86 us
  transfers between devices with their start and end apart: 4, of which 4 were waited for; matrix products, arithmetic and copies ran while one was open for 0% of the time, Pallas kernels for 2%

profile of v8, /device:TPU:1, one launch (start us, length us, event | category | flops | bytes accessed | tf_op | source)
XLA Modules:
  0.0 89.8 jit_solution(8630277117673295936)
XLA Ops:
  0.6 0.0 copy-start.2
  0.6 0.9 %copy-done.2 = bf16[32,2,16,128]{3,2,1,0:T(8,128)(2,1)S(1)} copy-done((bf16[32,2,16,128]{3,2,1,0:T(8,128)(2,1)S(1)}, bf16[32,2,16,128]{3,2,1,0:T(8,128)(2,1)}, u32[]{:S(2)}) %copy-start.2) | copy-done | bytes 262168
  1.6 0.0 copy-start.3
  1.6 0.0 copy-start.4
  1.6 1.6 %pack.1 = bf16[32,32,128]{2,1,0:T(8,128)(2,1)} custom-call(bf16[32,2,16,128]{3,2,1,0:T(8,128)(2,1)S(1)} %copy-done.2), custom_call_target="tpu_custom_call" | custom-call | flops 100000000 | bytes 1048576 | tf_op jit(solution)/shard_map/pack/pallas_call | solution.py:325
  3.2 0.0 copy-start
  3.2 0.0 copy-start.1
  3.2 12.0 %all-to-all-start = ((bf16[32,32,128]{2,1,0:T(8,128)(2,1)}), bf16[32,32,128]{2,1,0:T(8,128)(2,1)S(1)}, u32[]{:S(2)}, u32[]{:S(2)}) async-start(bf16[32,32,128]{2,1,0:T(8,128)(2,1)} %pack.1), calls=%async_computation | async-start | bytes 524288 | tf_op jit(solution)/shard_map/all_to_all | solution.py:348
  15.2 0.0 copy-done.3
  15.2 0.0 copy-done.4
  15.2 0.0 copy-done
  15.2 0.0 copy-done.1
  15.2 0.5 filters.1
  15.8 11.0 %all-to-all-done.parts_ref = bf16[32,32,128]{2,1,0:T(8,128)(2,1)S(1)} async-done(((bf16[32,32,128]{2,1,0:T(8,128)(2,1)}), bf16[32,32,128]{2,1,0:T(8,128)(2,1)S(1)}, u32[]{:S(2)}, u32[]{:S(2)}) %all-to-all-start) | async-done | bytes 262176 | tf_op jit(solution)/shard_map/all_to_all | solution.py:348
  26.9 0.6 arrange.1
  27.4 0.9 %collective-permute-start = (bf16[3,256,128]{2,1,0:T(8,128)(2,1)S(1)}, bf16[3,256,128]{2,1,0:T(8,128)(2,1)S(1)}, u32[]{:S(2)}, u32[]{:S(2)}) collective-permute-start(bf16[3,256,128]{2,1,0:T(8,128)(2,1)S(1)} %get-tuple-element.19), channel_id=1, source_target_pairs={{0,8},{72,64},{88,24},{16,80},{144,152},{128,136},{200,208},{216,1... | collective-permute-start | bytes 589832 | tf_op jit(solution)/shard_map/ppermute | solution.py:372
  28.4 2.0 %collective-permute-start.1 = (bf16[3,256,128]{2,1,0:T(8,128)(2,1)S(1)}, bf16[3,256,128]{2,1,0:T(8,128)(2,1)S(1)}, u32[]{:S(2)}, u32[]{:S(2)}) collective-permute-start(bf16[3,256,128]{2,1,0:T(8,128)(2,1)S(1)} %get-tuple-element.20), channel_id=1, source_target_pairs={{8,72},{64,88},{24,16},{80,144},{152,128},{136,200},{208,216},{192... | collective-permute-start | bytes 589832 | tf_op jit(solution)/shard_map/ppermute | solution.py:373
  30.3 1.7 %collective-permute-done.refs_1_ = bf16[3,256,128]{2,1,0:T(8,128)(2,1)S(1)} collective-permute-done((bf16[3,256,128]{2,1,0:T(8,128)(2,1)S(1)}, bf16[3,256,128]{2,1,0:T(8,128)(2,1)S(1)}, u32[]{:S(2)}, u32[]{:S(2)}) %collective-permute-start) | collective-permute-done | bytes 196640 | tf_op jit(solution)/shard_map/ppermute | solution.py:372
  32.0 3.9 %collective-permute-done.1.refs_2_ = bf16[3,256,128]{2,1,0:T(8,128)(2,1)S(1)} collective-permute-done((bf16[3,256,128]{2,1,0:T(8,128)(2,1)S(1)}, bf16[3,256,128]{2,1,0:T(8,128)(2,1)S(1)}, u32[]{:S(2)}, u32[]{:S(2)}) %collective-permute-start.1) | collective-permute-done | bytes 196640 | tf_op jit(solution)/shard_map/ppermute | solution.py:373
  36.0 5.7 %layers.1 = bf16[32,48,128]{2,1,0:T(8,128)(2,1)S(1)} custom-call(bf16[4,256,128]{2,1,0:T(8,128)(2,1)S(1)} %get-tuple-element.18.refs_0_, bf16[3,256,128]{2,1,0:T(8,128)(2,1)S(1)} %collective-permute-done.refs_1_, bf16[3,256,128]{2,1,0:T(8,128)(2,1)S(1)} %collective-permute-done.1.refs_2_, bf16[288,288]{1,0:T(8,128)(2,1)S(1)} %get-tuple-element.21.refs_3_, ...), custom_call_target="tpu_custom_call" | custom-call | flops 8000000000 | bytes 1048576 | tf_op jit(solution)/shard_map/layers/pallas_call | solution.py:325
  41.7 21.4 %all_to_all.20.parts_ref = bf16[32,48,128]{2,1,0:T(8,128)(2,1)S(1)} all-to-all(bf16[32,48,128]{2,1,0:T(8,128)(2,1)S(1)} %layers.1), channel_id=1, replica_groups=mesh['gx'=4,'gy'=8,'gz'=8] {'gx','gy'}, dimensions={0} | all-to-all | bytes 786432 | tf_op jit(solution)/shard_map/all_to_all | solution.py:392
  63.1 10.7 %all_to_all.21.parts_ref = f32[8,16,128]{2,1,0:T(8,128)S(1)} all-to-all(f32[8,16,128]{2,1,0:T(8,128)S(1)} %gather_sums.1), channel_id=1, replica_groups=mesh['gx'=4,'gy'=8,'gz'=8] {'gz'}, dimensions={0} | all-to-all | bytes 131072 | tf_op jit(solution)/shard_map/all_to_all | solution.py:394
  73.8 0.7 combine.1
  74.5 3.9 %all-to-all-start.3 = ((bf16[32,16,128]{2,1,0:T(8,128)(2,1)}), bf16[32,16,128]{2,1,0:T(8,128)(2,1)S(1)}, u32[]{:S(2)}, u32[]{:S(2)}) async-start(bf16[32,16,128]{2,1,0:T(8,128)(2,1)} %combine.1), calls=%async_computation.3 | async-start | bytes 262144 | tf_op jit(solution)/shard_map/all_to_all | solution.py:396
  78.4 1.7 %unpack.1 = bf16[32,2,16,128]{3,2,1,0:T(8,128)(2,1)} custom-call(bf16[32,48,128]{2,1,0:T(8,128)(2,1)S(1)} %all_to_all.20.parts_ref), custom_call_target="tpu_custom_call" | custom-call | flops 1000000000 | bytes 1048576 | tf_op jit(solution)/shard_map/unpack/pallas_call | solution.py:325
  80.1 7.8 %all-to-all-done.3 = bf16[32,16,128]{2,1,0:T(8,128)(2,1)S(1)} async-done(((bf16[32,16,128]{2,1,0:T(8,128)(2,1)}), bf16[32,16,128]{2,1,0:T(8,128)(2,1)S(1)}, u32[]{:S(2)}, u32[]{:S(2)}) %all-to-all-start.3) | async-done | bytes 131104 | tf_op jit(solution)/shard_map/all_to_all | solution.py:396
  87.9 1.9 %finish.1 = (f32[27,32,32]{2,1,0:T(8,128)}, f32[27,32,32]{2,1,0:T(8,128)}) custom-call(bf16[512,128]{1,0:T(8,128)(2,1)S(1)} %bitcast.13, f32[27,32,32]{2,1,0:T(8,128)S(1)} %bitcast.9, f32[27,32,32]{2,1,0:T(8,128)S(1)} %bitcast.10), custom_call_target="tpu_custom_call" | custom-call | tf_op jit(solution)/shard_map/finish/pallas_call | solution.py:407
  (3 shorter events, 0.1 us)
Async XLA Ops:
  0.6 1.0 %copy-start.2 = (bf16[32,2,16,128]{3,2,1,0:T(8,128)(2,1)S(1)}, bf16[32,2,16,128]{3,2,1,0:T(8,128)(2,1)}, u32[]{:S(2)}) copy-start(bf16[32,2,16,128]{3,2,1,0:T(8,128)(2,1)} %cells_ref.1) | copy-start | bytes 786436
  1.6 13.6 %copy-start.3 = (bf16[3,3,3,32,32]{4,3,2,1,0:T(8,128)(2,1)S(1)}, bf16[3,3,3,32,32]{4,3,2,1,0:T(8,128)(2,1)}, u32[]{:S(2)}) copy-start(bf16[3,3,3,32,32]{4,3,2,1,0:T(8,128)(2,1)} %param.6) | copy-start | bytes 165892
  1.6 13.6 %copy-start.4 = (bf16[3,3,3,32,32]{4,3,2,1,0:T(8,128)(2,1)S(1)}, bf16[3,3,3,32,32]{4,3,2,1,0:T(8,128)(2,1)}, u32[]{:S(2)}) copy-start(bf16[3,3,3,32,32]{4,3,2,1,0:T(8,128)(2,1)} %param.7) | copy-start | bytes 165892
  3.2 12.0 %copy-start = (bf16[3,3,3,32,32]{4,3,2,1,0:T(8,128)(2,1)S(1)}, bf16[3,3,3,32,32]{4,3,2,1,0:T(8,128)(2,1)}, u32[]{:S(2)}) copy-start(bf16[3,3,3,32,32]{4,3,2,1,0:T(8,128)(2,1)} %param.8) | copy-start | bytes 165892
  3.2 12.0 %copy-start.1 = (bf16[3,3,3,32,32]{4,3,2,1,0:T(8,128)(2,1)S(1)}, bf16[3,3,3,32,32]{4,3,2,1,0:T(8,128)(2,1)}, u32[]{:S(2)}) copy-start(bf16[3,3,3,32,32]{4,3,2,1,0:T(8,128)(2,1)} %param.9) | copy-start | bytes 165892
  3.2 23.7 %all-to-all-start = ((bf16[32,32,128]{2,1,0:T(8,128)(2,1)}), bf16[32,32,128]{2,1,0:T(8,128)(2,1)S(1)}, u32[]{:S(2)}, u32[]{:S(2)}) async-start(bf16[32,32,128]{2,1,0:T(8,128)(2,1)} %pack.1), calls=%async_computation | async-start | bytes 524288 | tf_op jit(solution)/shard_map/all_to_all | solution.py:348
  27.4 4.6 %collective-permute-start = (bf16[3,256,128]{2,1,0:T(8,128)(2,1)S(1)}, bf16[3,256,128]{2,1,0:T(8,128)(2,1)S(1)}, u32[]{:S(2)}, u32[]{:S(2)}) collective-permute-start(bf16[3,256,128]{2,1,0:T(8,128)(2,1)S(1)} %get-tuple-element.19), channel_id=1, source_target_pairs={{0,8},{72,64},{88,24},{16,80},{144,152},{128,136},{200,208},{216,1... | collective-permute-start | bytes 589832 | tf_op jit(solution)/shard_map/ppermute | solution.py:372
  28.4 7.6 %collective-permute-start.1 = (bf16[3,256,128]{2,1,0:T(8,128)(2,1)S(1)}, bf16[3,256,128]{2,1,0:T(8,128)(2,1)S(1)}, u32[]{:S(2)}, u32[]{:S(2)}) collective-permute-start(bf16[3,256,128]{2,1,0:T(8,128)(2,1)S(1)} %get-tuple-element.20), channel_id=1, source_target_pairs={{8,72},{64,88},{24,16},{80,144},{152,128},{136,200},{208,216},{192... | collective-permute-start | bytes 589832 | tf_op jit(solution)/shard_map/ppermute | solution.py:373
  74.5 13.4 %all-to-all-start.3 = ((bf16[32,16,128]{2,1,0:T(8,128)(2,1)}), bf16[32,16,128]{2,1,0:T(8,128)(2,1)S(1)}, u32[]{:S(2)}, u32[]{:S(2)}) async-start(bf16[32,16,128]{2,1,0:T(8,128)(2,1)} %combine.1), calls=%async_computation.3 | async-start | bytes 262144 | tf_op jit(solution)/shard_map/all_to_all | solution.py:396

commit v9 on v8

--- a/solution.py
+++ b/solution.py
@@ -16,17 +16,17 @@
 MEMBERS = 32
 
 
-CHIPS = (
-    (
-        0, 1, 11, 10, 13, 3, 2, 12, 22, 23, 20, 21, 31, 32, 33, 30,
-        40, 43, 42, 41, 51, 50, 53, 52, 62, 61, 71, 72, 73, 63, 60, 70,
-    ),
-    (
-        70, 71, 1, 2, 72, 62, 63, 53, 43, 33, 23, 13, 12, 11, 21, 22,
-        32, 42, 52, 51, 61, 60, 50, 40, 41, 31, 30, 20, 10, 0, 3, 73,
-    ),
-)
-LINES = tuple(tuple(c // 10 % 4 * 8 + c // 40 * 4 + c % 10 for c in chips) for chips in CHIPS)
+def snake():
+    def member(z, x):
+        return z % 4 * 8 + z // 4 * 4 + x
+
+    line = []
+    for z in range(8):
+        line += [member(z, x) for x in ((1, 2, 3) if z % 2 == 0 else (3, 2, 1))]
+    return tuple(line + [member(z, 0) for z in reversed(range(8))])
+
+
+LINES = (snake(), snake()[:1] + snake()[:0:-1])
 
 
 def member_at(place):
@@ -347,6 +347,9 @@
     )
     parts = lax.all_to_all(sent, GROUP, 0, 0)
 
+    parts, w_first, w_second, v_first, v_second = lax.optimization_barrier(
+        (parts, w_first, w_second, v_first, v_second)
+    )
     blocks = [w.reshape(27, channels, channels) for w in (w_first, v_first, w_second, v_second)]
     weights = call(
         filters, blocks, [((288, 288), BF16), ((96, 576), BF16)], [], "filters", 8, 2 * 10**8
@@ -354,7 +357,6 @@
     damping = tuple(
         factor * 0.1 * v.astype(F32).reshape(27, channels, channels) for v in (v_first, v_second)
     )
-    parts, weights, damping = lax.optimization_barrier((parts, weights, damping))
 
     halo = ((OWN - 1, 256, 128), BF16)
     own, first, second = call(

time: 90.1 us -> 87.4 us (0.970)
  blocking collectives: 32.1 us -> 54.6 us
  waiting for transfers between devices: 24.5 us -> 12.2 us
  starting transfers between devices: 18.8 us -> 6.7 us
    all_to_all x0 -> x1, blocking collectives: none -> 23.5 us  [body(): parts = lax.all_to_all(sent, GROUP, 0, 0)]
    all_to_all x1 -> x0, starting transfers between devices: 12 us -> none  [body(): parts = lax.all_to_all(sent, GROUP, 0, 0)]
    all_to_all x1 -> x0, waiting for transfers between devices: 11 us -> none  [body(): parts = lax.all_to_all(sent, GROUP, 0, 0)]
    all_to_all x1, blocking collectives: 21.4 us -> 17.8 us  [body(): parts = lax.all_to_all(leaving, GROUP, 0, 0)]
    all_to_all x1, blocking collectives: 10.7 us -> 13.3 us  [body(): sums = lax.all_to_all(sums, 'gz', 0, 0)]
  transfers between devices with their start and end apart: 4 -> 3, of which waited for: 4 -> 3; matrix products, arithmetic and copies ran while one was open for 0% -> 0% of each run, Pallas kernels for 2% -> 3%
where the time goes in v9:
time: 87.4 us; the launch traced here: 87.1 us
  blocking collectives  54.6 us (62%)
  waiting for transfers between devices  12.2 us (14%)
  Pallas kernels  11.8 us (14%)
  starting transfers between devices  6.7 us (8%)
  local copies, waits for them, and re-layouts  0.97 us (1%)
    all_to_all x1, blocking collectives, body(): parts = lax.all_to_all(sent, GROUP, 0, 0)  23.5 us
    all_to_all x1, blocking collectives, body(): parts = lax.all_to_all(leaving, GROUP, 0, 0)  17.8 us
    all_to_all x1, blocking collectives, body(): sums = lax.all_to_all(sums, 'gz', 0, 0)  13.3 us
    pallas_call x7, Pallas kernels, call(): pl.pallas_call(kernel, out_shape=tuple((jax.ShapeDtypeStruct(shape, dtype...  9.96 us
    all_to_all x1, waiting for transfers between devices, body(): every = lax.all_to_all(every, GROUP, 0, 0).reshape(512, 128)  7.69 us
    all_to_all x1, starting transfers between devices, body(): every = lax.all_to_all(every, GROUP, 0, 0).reshape(512, 128)  3.86 us
    ppermute x1, waiting for transfers between devices, body(): second = lax.ppermute(second, AXES, swapped(1))  3.25 us
    ppermute x1, starting transfers between devices, body(): second = lax.ppermute(second, AXES, swapped(1))  2.74 us
  transfers between devices with their start and end apart: 3, of which 3 were waited for; matrix products, arithmetic and copies ran while one was open for 0% of the time, Pallas kernels for 3%

profile of v9, /device:TPU:1, one launch (start us, length us, event | category | flops | bytes accessed | tf_op | source)
XLA Modules:
  0.0 87.1 jit_solution(13919778040217452360)
XLA Ops:
  0.6 0.0 copy-start.2
  0.6 0.9 %copy-done.2 = bf16[32,2,16,128]{3,2,1,0:T(8,128)(2,1)S(1)} copy-done((bf16[32,2,16,128]{3,2,1,0:T(8,128)(2,1)S(1)}, bf16[32,2,16,128]{3,2,1,0:T(8,128)(2,1)}, u32[]{:S(2)}) %copy-start.2) | copy-done | bytes 262168
  1.6 0.9 pack.1
  2.4 0.0 copy-start.1
  2.5 0.0 copy-start.3
  2.5 0.0 copy-start.4
  2.5 23.5 %all_to_all.20.parts_ref = bf16[32,32,128]{2,1,0:T(8,128)(2,1)S(1)} all-to-all(bf16[32,32,128]{2,1,0:T(8,128)(2,1)S(1)} %pack.1), channel_id=1, replica_groups=mesh['gx'=4,'gy'=8,'gz'=8] {'gx','gy'}, dimensions={0} | all-to-all | bytes 524288 | tf_op jit(solution)/shard_map/all_to_all | solution.py:348
  25.9 0.0 copy-start
  25.9 0.6 arrange.1
  26.5 0.1 collective-permute-start
  26.6 2.7 %collective-permute-start.1 = (bf16[3,256,128]{2,1,0:T(8,128)(2,1)S(1)}, bf16[3,256,128]{2,1,0:T(8,128)(2,1)S(1)}, u32[]{:S(2)}, u32[]{:S(2)}) collective-permute-start(bf16[3,256,128]{2,1,0:T(8,128)(2,1)S(1)} %get-tuple-element.18), channel_id=1, source_target_pairs={{16,24},{88,80},{72,136},{144,152},{216,208},{200,40},{48,56},{120... | collective-permute-start | bytes 589832 | tf_op jit(solution)/shard_map/ppermute | solution.py:375
  29.4 0.0 copy-done.1
  29.4 0.0 copy-done.3
  29.4 0.0 copy-done.4
  29.4 0.0 copy-done
  29.4 0.5 filters.1
  29.9 1.2 %collective-permute-done.refs_1_ = bf16[3,256,128]{2,1,0:T(8,128)(2,1)S(1)} collective-permute-done((bf16[3,256,128]{2,1,0:T(8,128)(2,1)S(1)}, bf16[3,256,128]{2,1,0:T(8,128)(2,1)S(1)}, u32[]{:S(2)}, u32[]{:S(2)}) %collective-permute-start) | collective-permute-done | bytes 196640 | tf_op jit(solution)/shard_map/ppermute | solution.py:374
  31.1 3.2 %collective-permute-done.1.refs_2_ = bf16[3,256,128]{2,1,0:T(8,128)(2,1)S(1)} collective-permute-done((bf16[3,256,128]{2,1,0:T(8,128)(2,1)S(1)}, bf16[3,256,128]{2,1,0:T(8,128)(2,1)S(1)}, u32[]{:S(2)}, u32[]{:S(2)}) %collective-permute-start.1) | collective-permute-done | bytes 196640 | tf_op jit(solution)/shard_map/ppermute | solution.py:375
  34.4 5.6 %layers.1 = bf16[32,48,128]{2,1,0:T(8,128)(2,1)S(1)} custom-call(bf16[4,256,128]{2,1,0:T(8,128)(2,1)S(1)} %get-tuple-element.16.refs_0_, bf16[3,256,128]{2,1,0:T(8,128)(2,1)S(1)} %collective-permute-done.refs_1_, bf16[3,256,128]{2,1,0:T(8,128)(2,1)S(1)} %collective-permute-done.1.refs_2_, bf16[288,288]{1,0:T(8,128)(2,1)S(1)} %get-tuple-element.23.refs_3_, ...), custom_call_target="tpu_custom_call" | custom-call | flops 8000000000 | bytes 1048576 | tf_op jit(solution)/shard_map/layers/pallas_call | solution.py:325
  40.0 17.8 %all_to_all.21.parts_ref = bf16[32,48,128]{2,1,0:T(8,128)(2,1)S(1)} all-to-all(bf16[32,48,128]{2,1,0:T(8,128)(2,1)S(1)} %layers.1), channel_id=1, replica_groups=mesh['gx'=4,'gy'=8,'gz'=8] {'gx','gy'}, dimensions={0} | all-to-all | bytes 786432 | tf_op jit(solution)/shard_map/all_to_all | solution.py:394
  57.9 13.3 %all_to_all.22.parts_ref = f32[8,16,128]{2,1,0:T(8,128)S(1)} all-to-all(f32[8,16,128]{2,1,0:T(8,128)S(1)} %gather_sums.1), channel_id=1, replica_groups=mesh['gx'=4,'gy'=8,'gz'=8] {'gz'}, dimensions={0} | all-to-all | bytes 131072 | tf_op jit(solution)/shard_map/all_to_all | solution.py:396
  71.2 0.7 combine.1
  71.8 3.9 %all-to-all-start.3 = ((bf16[32,16,128]{2,1,0:T(8,128)(2,1)}), bf16[32,16,128]{2,1,0:T(8,128)(2,1)S(1)}, u32[]{:S(2)}, u32[]{:S(2)}) async-start(bf16[32,16,128]{2,1,0:T(8,128)(2,1)} %combine.1), calls=%async_computation.3 | async-start | bytes 262144 | tf_op jit(solution)/shard_map/all_to_all | solution.py:398
  75.7 0.1 convert_multiply_fusion
  75.8 1.7 %unpack.1 = bf16[32,2,16,128]{3,2,1,0:T(8,128)(2,1)} custom-call(bf16[32,48,128]{2,1,0:T(8,128)(2,1)S(1)} %all_to_all.21.parts_ref), custom_call_target="tpu_custom_call" | custom-call | flops 1000000000 | bytes 1048576 | tf_op jit(solution)/shard_map/unpack/pallas_call | solution.py:325
  77.5 7.7 %all-to-all-done.3 = bf16[32,16,128]{2,1,0:T(8,128)(2,1)S(1)} async-done(((bf16[32,16,128]{2,1,0:T(8,128)(2,1)}), bf16[32,16,128]{2,1,0:T(8,128)(2,1)S(1)}, u32[]{:S(2)}, u32[]{:S(2)}) %all-to-all-start.3) | async-done | bytes 131104 | tf_op jit(solution)/shard_map/all_to_all | solution.py:398
  85.2 1.9 %finish.1 = (f32[27,32,32]{2,1,0:T(8,128)}, f32[27,32,32]{2,1,0:T(8,128)}) custom-call(bf16[512,128]{1,0:T(8,128)(2,1)S(1)} %bitcast.13, f32[27,32,32]{2,1,0:T(8,128)S(1)} %bitcast.10, f32[27,32,32]{2,1,0:T(8,128)S(1)} %bitcast.9), custom_call_target="tpu_custom_call" | custom-call | tf_op jit(solution)/shard_map/finish/pallas_call | solution.py:409
  (1 shorter events, 0.0 us)
Async XLA Ops:
  0.6 1.0 %copy-start.2 = (bf16[32,2,16,128]{3,2,1,0:T(8,128)(2,1)S(1)}, bf16[32,2,16,128]{3,2,1,0:T(8,128)(2,1)}, u32[]{:S(2)}) copy-start(bf16[32,2,16,128]{3,2,1,0:T(8,128)(2,1)} %cells_ref.1) | copy-start | bytes 786436
  2.4 26.9 %copy-start.1 = (bf16[3,3,3,32,32]{4,3,2,1,0:T(8,128)(2,1)S(1)}, bf16[3,3,3,32,32]{4,3,2,1,0:T(8,128)(2,1)}, u32[]{:S(2)}) copy-start(bf16[3,3,3,32,32]{4,3,2,1,0:T(8,128)(2,1)} %param.9) | copy-start | bytes 165892
  2.5 26.9 %copy-start.3 = (bf16[3,3,3,32,32]{4,3,2,1,0:T(8,128)(2,1)S(1)}, bf16[3,3,3,32,32]{4,3,2,1,0:T(8,128)(2,1)}, u32[]{:S(2)}) copy-start(bf16[3,3,3,32,32]{4,3,2,1,0:T(8,128)(2,1)} %param.6) | copy-start | bytes 165892
  2.5 26.9 %copy-start.4 = (bf16[3,3,3,32,32]{4,3,2,1,0:T(8,128)(2,1)S(1)}, bf16[3,3,3,32,32]{4,3,2,1,0:T(8,128)(2,1)}, u32[]{:S(2)}) copy-start(bf16[3,3,3,32,32]{4,3,2,1,0:T(8,128)(2,1)} %param.7) | copy-start | bytes 165892
  25.9 3.4 %copy-start = (bf16[3,3,3,32,32]{4,3,2,1,0:T(8,128)(2,1)S(1)}, bf16[3,3,3,32,32]{4,3,2,1,0:T(8,128)(2,1)}, u32[]{:S(2)}) copy-start(bf16[3,3,3,32,32]{4,3,2,1,0:T(8,128)(2,1)} %param.8) | copy-start | bytes 165892
  26.5 4.6 %collective-permute-start = (bf16[3,256,128]{2,1,0:T(8,128)(2,1)S(1)}, bf16[3,256,128]{2,1,0:T(8,128)(2,1)S(1)}, u32[]{:S(2)}, u32[]{:S(2)}) collective-permute-start(bf16[3,256,128]{2,1,0:T(8,128)(2,1)S(1)} %get-tuple-element.17), channel_id=1, source_target_pairs={{8,16},{24,88},{80,72},{136,144},{152,216},{208,200},{40,48},{56,1... | collective-permute-start | bytes 589832 | tf_op jit(solution)/shard_map/ppermute | solution.py:374
  26.6 7.8 %collective-permute-start.1 = (bf16[3,256,128]{2,1,0:T(8,128)(2,1)S(1)}, bf16[3,256,128]{2,1,0:T(8,128)(2,1)S(1)}, u32[]{:S(2)}, u32[]{:S(2)}) collective-permute-start(bf16[3,256,128]{2,1,0:T(8,128)(2,1)S(1)} %get-tuple-element.18), channel_id=1, source_target_pairs={{16,24},{88,80},{72,136},{144,152},{216,208},{200,40},{48,56},{120... | collective-permute-start | bytes 589832 | tf_op jit(solution)/shard_map/ppermute | solution.py:375
  71.8 13.4 %all-to-all-start.3 = ((bf16[32,16,128]{2,1,0:T(8,128)(2,1)}), bf16[32,16,128]{2,1,0:T(8,128)(2,1)S(1)}, u32[]{:S(2)}, u32[]{:S(2)}) async-start(bf16[32,16,128]{2,1,0:T(8,128)(2,1)} %combine.1), calls=%async_computation.3 | async-start | bytes 262144 | tf_op jit(solution)/shard_map/all_to_all | solution.py:398

commit v10 on v9

--- a/solution.py
+++ b/solution.py
@@ -70,13 +70,20 @@
     return jnp.where(hit, 1.0, 0.0).astype(BF16)
 
 
-def pack(cells_ref, out_ref, sorted_ref):
-    sorted_ref[...] = jnp.dot(
-        cells_ref[...].reshape(1024, 128), permutation(False), preferred_element_type=F32
-    )
+def pack(cells_ref, out_ref, cells, sorted_ref, arrived):
+    def fetch(part):
+        at = pl.ds(8 * part, 8)
+        return pltpu.make_async_copy(cells_ref.at[at], cells.at[at], arrived.at[part])
+
     for part in range(4):
-        tiles = [sorted_ref[pl.ds(256 * part + i, 8, stride=32)] for i in range(32)]
-        tiles = exchange(tiles, (0, 1, 2, 3, 4))
+        fetch(part).start()
+    order = permutation(False)
+    for part in range(4):
+        fetch(part).wait()
+        sorted_ref[...] = jnp.dot(
+            cells[8 * part : 8 * part + 8].reshape(256, 128), order, preferred_element_type=F32
+        )
+        tiles = exchange([sorted_ref[pl.ds(i, 8, stride=32)] for i in range(32)], (0, 1, 2, 3, 4))
         for i in range(MEMBERS):
             out_ref[member_at(i), 8 * part : 8 * part + 8] = tiles[i].astype(BF16)
 
@@ -98,17 +105,6 @@
     def _():
         first_ref[...] = own_ref[1:4]
         second_ref[...] = own_ref[0:3]
-
-
-def unpack(parts_ref, out_ref, mixed_ref):
-    for part in range(2):
-        at = slice(16 * part, 16 * part + 16)
-        tiles = [parts_ref[member_at(i), at].astype(F32) for i in range(MEMBERS)]
-        tiles = exchange(tiles, (0, 1, 2, 3, 4))
-        for i in range(32):
-            mixed_ref[pl.ds(512 * part + i, 16, stride=32)] = tiles[i]
-    moved = jnp.dot(mixed_ref[...].astype(BF16), permutation(True), preferred_element_type=F32)
-    out_ref[...] = moved.astype(BF16).reshape(32, 2, 16, 128)
 
 
 def gelu_pair(pre):
@@ -271,28 +267,55 @@
         out_ref[member] = total
 
 
-def finish(scale, packed_ref, d_first_ref, d_second_ref, first_ref, second_ref, rest_ref):
-    depth = pl.program_id(0)
-
-    @pl.when(depth == 0)
-    def _():
-        rest = packed_ref[288:432, :].astype(F32)
-        rest_ref[0:144] = rest
-        rest_ref[144:288] = pltpu.roll(rest, 64, 1)
-
-    def damped(summed, damping):
-        return scale * summed + damping
-
-    for column in range(3):
-        block = pl.ds(pl.multiple_of(96 * column + 32 * depth, 32), 32)
-        low = packed_ref[block, :].astype(F32)
-        far = rest_ref[block, :]
-        for row in range(3):
-            at = 3 * row + column
-            second_ref[at] = damped(low[:, 32 * row : 32 * row + 32], d_second_ref[at])
-        first_ref[column] = damped(low[:, 96:128], d_first_ref[column])
-        first_ref[3 + column] = damped(far[:, 0:32], d_first_ref[3 + column])
-        first_ref[6 + column] = damped(far[:, 32:64], d_first_ref[6 + column])
+def finish(
+    scale,
+    packed_ref,
+    d_first_ref,
+    d_second_ref,
+    parts_ref,
+    first_ref,
+    second_ref,
+    jv_ref,
+    first,
+    second,
+    jv,
+    mixed_ref,
+    left,
+):
+    leaving = []
+
+    def leave(source, target, at):
+        leaving.append(pltpu.make_async_copy(source.at[at], target.at[at], left.at[len(leaving)]))
+        leaving[-1].start()
+
+    rest = packed_ref[288:432, :].astype(F32)
+    rest = jnp.concatenate([rest, pltpu.roll(rest, 64, 1)], axis=0)
+    for depth in range(3):
+        for column in range(3):
+            block = slice(96 * column + 32 * depth, 96 * column + 32 * depth + 32)
+            low = packed_ref[block, :].astype(F32)
+            far = rest[block]
+            for row in range(3):
+                at = 9 * depth + 3 * row + column
+                second[at] = scale * low[:, 32 * row : 32 * row + 32] + d_second_ref[at]
+            for row, summed in enumerate((low[:, 96:128], far[:, 0:32], far[:, 32:64])):
+                at = 9 * depth + 3 * row + column
+                first[at] = scale * summed + d_first_ref[at]
+        leave(first, first_ref, pl.ds(9 * depth, 9))
+        leave(second, second_ref, pl.ds(9 * depth, 9))
+
+    order = permutation(True)
+    for part in range(2):
+        at = slice(16 * part, 16 * part + 16)
+        tiles = [parts_ref[member_at(i), at].astype(F32) for i in range(MEMBERS)]
+        tiles = exchange(tiles, (0, 1, 2, 3, 4))
+        for i in range(32):
+            mixed_ref[pl.ds(i, 16, stride=32)] = tiles[i]
+        moved = jnp.dot(mixed_ref[...].astype(BF16), order, preferred_element_type=F32)
+        jv[at] = moved.astype(BF16).reshape(16, 2, 16, 128)
+        leave(jv, jv_ref, pl.ds(16 * part, 16))
+    for copy in leaving:
+        copy.wait()
 
 
 def filters(w_first_ref, v_first_ref, w_second_ref, v_second_ref, rows_ref, joint_ref):
@@ -342,9 +365,20 @@
     factor = math.sqrt(27.0 * channels)
     small = (channels, 128)
 
-    (sent,) = call(
-        pack, (volume,), [((members,) + small, BF16)], [((1024, 128), F32)], "pack", 8, 10**8
-    )
+    sent = pl.pallas_call(
+        pack,
+        out_shape=jax.ShapeDtypeStruct((members,) + small, BF16),
+        in_specs=[pl.BlockSpec(memory_space=pltpu.HBM)],
+        out_specs=pl.BlockSpec(memory_space=pltpu.VMEM),
+        scratch_shapes=[
+            pltpu.VMEM(volume.shape, BF16),
+            pltpu.VMEM((256, 128), F32),
+            pltpu.SemaphoreType.DMA((4,)),
+        ],
+        compiler_params=pltpu.CompilerParams(vmem_limit_bytes=8 << 20),
+        cost_estimate=pl.CostEstimate(flops=10**8, bytes_accessed=1, transcendentals=0),
+        name="pack",
+    )(pltpu.with_memory_space_constraint(volume, pltpu.HBM))
     parts = lax.all_to_all(sent, GROUP, 0, 0)
 
     parts, w_first, w_second, v_first, v_second = lax.optimization_barrier(
@@ -373,6 +407,7 @@
 
     first = lax.ppermute(first, AXES, swapped(0))
     second = lax.ppermute(second, AXES, swapped(1))
+    first, second, damping = lax.optimization_barrier((first, second, damping))
 
     (leaving,) = call(
         lambda *refs: layers(width * n_gz, *refs),
@@ -396,28 +431,28 @@
     sums = lax.all_to_all(sums, "gz", 0, 0)
     (every,) = call(combine, (sums,), [((members, 16, 128), BF16)], [], "combine", 8, 10**8)
     every = lax.all_to_all(every, GROUP, 0, 0).reshape(512, 128)
-    (out,) = call(
-        unpack,
-        (parts,),
-        [(volume.shape, BF16)],
-        [((1024, 128), F32)],
-        "unpack",
-        8,
-        10**9,
-    )
-    third = pl.BlockSpec((9, channels, channels), lambda i: (i, 0, 0))
-    gv_first, gv_second = pl.pallas_call(
+    hbm = pl.BlockSpec(memory_space=pltpu.HBM)
+    filter_shape = (27, channels, channels)
+    gv_first, gv_second, out = pl.pallas_call(
         lambda *refs: finish(factor / count_all, *refs),
-        grid=(3,),
-        out_shape=(jax.ShapeDtypeStruct((27, channels, channels), F32),) * 2,
-        in_specs=[pl.BlockSpec((512, 128), lambda i: (0, 0)), third, third],
-        out_specs=(third, third),
-        scratch_shapes=[pltpu.VMEM((288, 128), F32)],
-        compiler_params=pltpu.CompilerParams(
-            dimension_semantics=("arbitrary",), vmem_limit_bytes=8 << 20
+        out_shape=(
+            jax.ShapeDtypeStruct(filter_shape, F32),
+            jax.ShapeDtypeStruct(filter_shape, F32),
+            jax.ShapeDtypeStruct(volume.shape, BF16),
         ),
+        in_specs=[pl.BlockSpec(memory_space=pltpu.VMEM)] * 4,
+        out_specs=(hbm,) * 3,
+        scratch_shapes=[
+            pltpu.VMEM(filter_shape, F32),
+            pltpu.VMEM(filter_shape, F32),
+            pltpu.VMEM(volume.shape, BF16),
+            pltpu.VMEM((512, 128), F32),
+            pltpu.SemaphoreType.DMA((8,)),
+        ],
+        compiler_params=pltpu.CompilerParams(vmem_limit_bytes=8 << 20),
+        cost_estimate=pl.CostEstimate(flops=10**9, bytes_accessed=1 << 20, transcendentals=0),
         name="finish",
-    )(every, *damping)
+    )(every, *damping, parts)
     return (out, gv_first.reshape(v_first.shape), gv_second.reshape(v_first.shape))
 
 

time: 87.4 us -> 89.9 us (1.029)
  blocking collectives: 54.6 us -> 67.5 us
  waiting for transfers between devices: 12.2 us -> 4.36 us
  starting transfers between devices: 6.7 us -> 2.84 us
  Pallas kernels: 11.8 us -> 14.1 us
  local copies, waits for them, and re-layouts: 0.97 us -> 0.02 us
    all_to_all x0 -> x1, blocking collectives: none -> 12.9 us  [body(): every = lax.all_to_all(every, GROUP, 0, 0).reshape(512, 128)]
    all_to_all x1 -> x0, waiting for transfers between devices: 7.69 us -> none  [body(): every = lax.all_to_all(every, GROUP, 0, 0).reshape(512, 128)]
    pallas_call x1 -> x2, Pallas kernels: 1.86 us -> 7.34 us  [the longest x1 4.12 us: body(): pl.pallas_call(lambda *refs: finish(factor / count_all, *refs), out_shape...]
    all_to_all x1 -> x0, starting transfers between devices: 3.86 us -> none  [body(): every = lax.all_to_all(every, GROUP, 0, 0).reshape(512, 128)]
    pallas_call x7 -> x5, Pallas kernels: 9.96 us -> 6.75 us  [call(): pl.pallas_call(kernel, out_shape=tuple((jax.ShapeDtypeStruct(shape, dtype...]
    unnamed x10 -> x8, local copies, waits for them, and re-layouts: 0.97 us -> 0.02 us
  transfers between devices with their start and end apart: 3 -> 2, of which waited for: 3 -> 2; matrix products, arithmetic and copies ran while one was open for 0% -> 0% of each run, Pallas kernels for 3% -> 1%
where the time goes in v10:
time: 89.9 us; the launch traced here: 89.6 us
  blocking collectives  67.5 us (75%)
  Pallas kernels  14.1 us (16%)
  waiting for transfers between devices  4.36 us (5%)
  starting transfers between devices  2.84 us (3%)
    all_to_all x1, blocking collectives, body(): parts = lax.all_to_all(sent, GROUP, 0, 0)  23.5 us
    all_to_all x1, blocking collectives, body(): parts = lax.all_to_all(leaving, GROUP, 0, 0)  17.8 us
    all_to_all x1, blocking collectives, body(): sums = lax.all_to_all(sums, 'gz', 0, 0)  13.2 us
    all_to_all x1, blocking collectives, body(): every = lax.all_to_all(every, GROUP, 0, 0).reshape(512, 128)  12.9 us
    pallas_call x5, Pallas kernels, call(): pl.pallas_call(kernel, out_shape=tuple((jax.ShapeDtypeStruct(shape, dtype...  6.75 us
    pallas_call x1, Pallas kernels, body(): pl.pallas_call(lambda *refs: finish(factor / count_all, *refs), out_shape...  4.12 us
    ppermute x1, waiting for transfers between devices, body(): second = lax.ppermute(second, AXES, swapped(1))  3.25 us
    pallas_call x1, Pallas kernels, body(): pl.pallas_call(pack, out_shape=jax.ShapeDtypeStruct((members,) + small, B...  3.22 us
  transfers between devices with their start and end apart: 2, of which 2 were waited for; matrix products, arithmetic and copies ran while one was open for 0% of the time, Pallas kernels for 1%

profile of v10, /device:TPU:1, one launch (start us, length us, event | category | flops | bytes accessed | tf_op | source)
XLA Modules:
  0.0 89.6 jit_solution(621745195406064375)
XLA Ops:
  0.6 3.2 %pack.1 = bf16[32,32,128]{2,1,0:T(8,128)(2,1)S(1)} custom-call(bf16[32,2,16,128]{3,2,1,0:T(8,128)(2,1)} %cells_ref.1), custom_call_target="tpu_custom_call" | custom-call | flops 100000000 | bytes 1 | tf_op jit(solution)/shard_map/pack/pallas_call | solution.py:368
  3.9 0.0 copy-start.1
  3.9 0.0 copy-start.2
  3.9 0.0 copy-start.3
  3.9 23.5 %all_to_all.20.parts_ref = bf16[32,32,128]{2,1,0:T(8,128)(2,1)S(1)} all-to-all(bf16[32,32,128]{2,1,0:T(8,128)(2,1)S(1)} %pack.1), channel_id=1, replica_groups=mesh['gx'=4,'gy'=8,'gz'=8] {'gx','gy'}, dimensions={0} | all-to-all | bytes 524288 | tf_op jit(solution)/shard_map/all_to_all | solution.py:382
  27.3 0.0 copy-start
  27.4 0.6 arrange.1
  27.9 0.1 collective-permute-start
  28.0 2.7 %collective-permute-start.1 = (bf16[3,256,128]{2,1,0:T(8,128)(2,1)S(1)}, bf16[3,256,128]{2,1,0:T(8,128)(2,1)S(1)}, u32[]{:S(2)}, u32[]{:S(2)}) collective-permute-start(bf16[3,256,128]{2,1,0:T(8,128)(2,1)S(1)} %get-tuple-element.23), channel_id=1, source_target_pairs={{16,24},{88,80},{72,136},{144,152},{216,208},{200,40},{48,56},{120... | collective-permute-start | bytes 589832 | tf_op jit(solution)/shard_map/ppermute | solution.py:409
  30.8 0.0 copy-done.1
  30.8 0.0 copy-done.2
  30.8 0.0 copy-done.3
  30.8 0.0 copy-done
  30.8 0.5 filters.1
  31.3 0.1 convert_multiply_fusion
  31.4 1.1 %collective-permute-done.refs_1_ = bf16[3,256,128]{2,1,0:T(8,128)(2,1)S(1)} collective-permute-done((bf16[3,256,128]{2,1,0:T(8,128)(2,1)S(1)}, bf16[3,256,128]{2,1,0:T(8,128)(2,1)S(1)}, u32[]{:S(2)}, u32[]{:S(2)}) %collective-permute-start) | collective-permute-done | bytes 196640 | tf_op jit(solution)/shard_map/ppermute | solution.py:408
  32.5 3.2 %collective-permute-done.1.refs_2_ = bf16[3,256,128]{2,1,0:T(8,128)(2,1)S(1)} collective-permute-done((bf16[3,256,128]{2,1,0:T(8,128)(2,1)S(1)}, bf16[3,256,128]{2,1,0:T(8,128)(2,1)S(1)}, u32[]{:S(2)}, u32[]{:S(2)}) %collective-permute-start.1) | collective-permute-done | bytes 196640 | tf_op jit(solution)/shard_map/ppermute | solution.py:409
  35.8 5.7 %layers.1 = bf16[32,48,128]{2,1,0:T(8,128)(2,1)S(1)} custom-call(bf16[4,256,128]{2,1,0:T(8,128)(2,1)S(1)} %get-tuple-element.21.refs_0_, bf16[3,256,128]{2,1,0:T(8,128)(2,1)S(1)} %collective-permute-done.refs_1_, bf16[3,256,128]{2,1,0:T(8,128)(2,1)S(1)} %collective-permute-done.1.refs_2_, bf16[288,288]{1,0:T(8,128)(2,1)S(1)} %get-tuple-element.30.refs_3_, ...), custom_call_target="tpu_custom_call" | custom-call | flops 8000000000 | bytes 1048576 | tf_op jit(solution)/shard_map/layers/pallas_call | solution.py:348
  41.4 17.8 %all_to_all.21.parts_ref.refs_3_ = bf16[32,48,128]{2,1,0:T(8,128)(2,1)S(1)} all-to-all(bf16[32,48,128]{2,1,0:T(8,128)(2,1)S(1)} %layers.1), channel_id=1, replica_groups=mesh['gx'=4,'gy'=8,'gz'=8] {'gx','gy'}, dimensions={0} | all-to-all | bytes 786432 | tf_op jit(solution)/shard_map/all_to_all | solution.py:429
  59.3 13.2 %all_to_all.22.parts_ref = f32[8,16,128]{2,1,0:T(8,128)S(1)} all-to-all(f32[8,16,128]{2,1,0:T(8,128)S(1)} %gather_sums.1), channel_id=1, replica_groups=mesh['gx'=4,'gy'=8,'gz'=8] {'gz'}, dimensions={0} | all-to-all | bytes 131072 | tf_op jit(solution)/shard_map/all_to_all | solution.py:431
  72.6 12.9 %all_to_all.23 = bf16[32,16,128]{2,1,0:T(8,128)(2,1)S(1)} all-to-all(bf16[32,16,128]{2,1,0:T(8,128)(2,1)S(1)} %combine.1), channel_id=1, replica_groups=mesh['gx'=4,'gy'=8,'gz'=8] {'gx','gy'}, dimensions={0} | all-to-all | bytes 262144 | tf_op jit(solution)/shard_map/all_to_all | solution.py:433
  85.5 4.1 %finish.1 = (f32[27,32,32]{2,1,0:T(8,128)}, f32[27,32,32]{2,1,0:T(8,128)}, bf16[32,2,16,128]{3,2,1,0:T(8,128)(2,1)}) custom-call(bf16[512,128]{1,0:T(8,128)(2,1)S(1)} %bitcast.15, f32[27,32,32]{2,1,0:T(8,128)S(1)} %bitcast.12, f32[27,32,32]{2,1,0:T(8,128)S(1)} %bitcast.11, bf16[32,48,128]{2,1,0:T(8,128)(2,1)S(1)} %all_to_all.21.parts_ref.refs_3_), custom_call_target="tpu_custom_call" | custom-call | flops 1000000000 | bytes 1048576 | tf_op jit(solution)/shard_map/finish/pallas_call | solution.py:436
  (2 shorter events, 0.1 us)
Async XLA Ops:
  3.9 26.9 %copy-start.1 = (bf16[3,3,3,32,32]{4,3,2,1,0:T(8,128)(2,1)S(1)}, bf16[3,3,3,32,32]{4,3,2,1,0:T(8,128)(2,1)}, u32[]{:S(2)}) copy-start(bf16[3,3,3,32,32]{4,3,2,1,0:T(8,128)(2,1)} %param.9) | copy-start | bytes 165892
  3.9 26.9 %copy-start.2 = (bf16[3,3,3,32,32]{4,3,2,1,0:T(8,128)(2,1)S(1)}, bf16[3,3,3,32,32]{4,3,2,1,0:T(8,128)(2,1)}, u32[]{:S(2)}) copy-start(bf16[3,3,3,32,32]{4,3,2,1,0:T(8,128)(2,1)} %param.6) | copy-start | bytes 165892
  3.9 26.9 %copy-start.3 = (bf16[3,3,3,32,32]{4,3,2,1,0:T(8,128)(2,1)S(1)}, bf16[3,3,3,32,32]{4,3,2,1,0:T(8,128)(2,1)}, u32[]{:S(2)}) copy-start(bf16[3,3,3,32,32]{4,3,2,1,0:T(8,128)(2,1)} %param.7) | copy-start | bytes 165892
  27.3 3.4 %copy-start = (bf16[3,3,3,32,32]{4,3,2,1,0:T(8,128)(2,1)S(1)}, bf16[3,3,3,32,32]{4,3,2,1,0:T(8,128)(2,1)}, u32[]{:S(2)}) copy-start(bf16[3,3,3,32,32]{4,3,2,1,0:T(8,128)(2,1)} %param.8) | copy-start | bytes 165892
  27.9 4.6 %collective-permute-start = (bf16[3,256,128]{2,1,0:T(8,128)(2,1)S(1)}, bf16[3,256,128]{2,1,0:T(8,128)(2,1)S(1)}, u32[]{:S(2)}, u32[]{:S(2)}) collective-permute-start(bf16[3,256,128]{2,1,0:T(8,128)(2,1)S(1)} %get-tuple-element.22), channel_id=1, source_target_pairs={{8,16},{24,88},{80,72},{136,144},{152,216},{208,200},{40,48},{56,1... | collective-permute-start | bytes 589832 | tf_op jit(solution)/shard_map/ppermute | solution.py:408
  28.0 7.8 %collective-permute-start.1 = (bf16[3,256,128]{2,1,0:T(8,128)(2,1)S(1)}, bf16[3,256,128]{2,1,0:T(8,128)(2,1)S(1)}, u32[]{:S(2)}, u32[]{:S(2)}) collective-permute-start(bf16[3,256,128]{2,1,0:T(8,128)(2,1)S(1)} %get-tuple-element.23), channel_id=1, source_target_pairs={{16,24},{88,80},{72,136},{144,152},{216,208},{200,40},{48,56},{120... | collective-permute-start | bytes 589832 | tf_op jit(solution)/shard_map/ppermute | solution.py:409

commit v11 on v10

--- a/solution.py
+++ b/solution.py
@@ -70,20 +70,13 @@
     return jnp.where(hit, 1.0, 0.0).astype(BF16)
 
 
-def pack(cells_ref, out_ref, cells, sorted_ref, arrived):
-    def fetch(part):
-        at = pl.ds(8 * part, 8)
-        return pltpu.make_async_copy(cells_ref.at[at], cells.at[at], arrived.at[part])
-
+def pack(cells_ref, out_ref, sorted_ref):
+    sorted_ref[...] = jnp.dot(
+        cells_ref[...].reshape(1024, 128), permutation(False), preferred_element_type=F32
+    )
     for part in range(4):
-        fetch(part).start()
-    order = permutation(False)
-    for part in range(4):
-        fetch(part).wait()
-        sorted_ref[...] = jnp.dot(
-            cells[8 * part : 8 * part + 8].reshape(256, 128), order, preferred_element_type=F32
-        )
-        tiles = exchange([sorted_ref[pl.ds(i, 8, stride=32)] for i in range(32)], (0, 1, 2, 3, 4))
+        tiles = [sorted_ref[pl.ds(256 * part + i, 8, stride=32)] for i in range(32)]
+        tiles = exchange(tiles, (0, 1, 2, 3, 4))
         for i in range(MEMBERS):
             out_ref[member_at(i), 8 * part : 8 * part + 8] = tiles[i].astype(BF16)
 
@@ -278,7 +271,6 @@
     jv_ref,
     first,
     second,
-    jv,
     mixed_ref,
     left,
 ):
@@ -312,8 +304,7 @@
         for i in range(32):
             mixed_ref[pl.ds(i, 16, stride=32)] = tiles[i]
         moved = jnp.dot(mixed_ref[...].astype(BF16), order, preferred_element_type=F32)
-        jv[at] = moved.astype(BF16).reshape(16, 2, 16, 128)
-        leave(jv, jv_ref, pl.ds(16 * part, 16))
+        jv_ref[at] = moved.astype(BF16).reshape(16, 2, 16, 128)
     for copy in leaving:
         copy.wait()
 
@@ -365,20 +356,9 @@
     factor = math.sqrt(27.0 * channels)
     small = (channels, 128)
 
-    sent = pl.pallas_call(
-        pack,
-        out_shape=jax.ShapeDtypeStruct((members,) + small, BF16),
-        in_specs=[pl.BlockSpec(memory_space=pltpu.HBM)],
-        out_specs=pl.BlockSpec(memory_space=pltpu.VMEM),
-        scratch_shapes=[
-            pltpu.VMEM(volume.shape, BF16),
-            pltpu.VMEM((256, 128), F32),
-            pltpu.SemaphoreType.DMA((4,)),
-        ],
-        compiler_params=pltpu.CompilerParams(vmem_limit_bytes=8 << 20),
-        cost_estimate=pl.CostEstimate(flops=10**8, bytes_accessed=1, transcendentals=0),
-        name="pack",
-    )(pltpu.with_memory_space_constraint(volume, pltpu.HBM))
+    (sent,) = call(
+        pack, (volume,), [((members,) + small, BF16)], [((1024, 128), F32)], "pack", 8, 10**8
+    )
     parts = lax.all_to_all(sent, GROUP, 0, 0)
 
     parts, w_first, w_second, v_first, v_second = lax.optimization_barrier(
@@ -441,13 +421,12 @@
             jax.ShapeDtypeStruct(volume.shape, BF16),
         ),
         in_specs=[pl.BlockSpec(memory_space=pltpu.VMEM)] * 4,
-        out_specs=(hbm,) * 3,
+        out_specs=(hbm, hbm, pl.BlockSpec(memory_space=pltpu.VMEM)),
         scratch_shapes=[
             pltpu.VMEM(filter_shape, F32),
             pltpu.VMEM(filter_shape, F32),
-            pltpu.VMEM(volume.shape, BF16),
             pltpu.VMEM((512, 128), F32),
-            pltpu.SemaphoreType.DMA((8,)),
+            pltpu.SemaphoreType.DMA((6,)),
         ],
         compiler_params=pltpu.CompilerParams(vmem_limit_bytes=8 << 20),
         cost_estimate=pl.CostEstimate(flops=10**9, bytes_accessed=1 << 20, transcendentals=0),

time: 89.9 us -> 88.6 us (0.986)
  Pallas kernels: 14.1 us -> 11.8 us
  local copies, waits for them, and re-layouts: 0.02 us -> 0.97 us
    pallas_call x1 -> x0, Pallas kernels: 3.22 us -> none  [body(): pl.pallas_call(pack, out_shape=jax.ShapeDtypeStruct((members,) + small, B...]
    unnamed x8 -> x10, local copies, waits for them, and re-layouts: 0.02 us -> 0.97 us
    pallas_call x5 -> x6, Pallas kernels: 6.75 us -> 7.6 us  [call(): pl.pallas_call(kernel, out_shape=tuple((jax.ShapeDtypeStruct(shape, dtype...]
where the time goes in v11:
time: 88.6 us; the launch traced here: 88.4 us
  blocking collectives  67.5 us (76%)
  Pallas kernels  11.8 us (13%)
  waiting for transfers between devices  4.36 us (5%)
  starting transfers between devices  2.84 us (3%)
  local copies, waits for them, and re-layouts  0.97 us (1%)
    all_to_all x1, blocking collectives, body(): parts = lax.all_to_all(sent, GROUP, 0, 0)  23.5 us
    all_to_all x1, blocking collectives, body(): parts = lax.all_to_all(leaving, GROUP, 0, 0)  17.8 us
    all_to_all x1, blocking collectives, body(): sums = lax.all_to_all(sums, 'gz', 0, 0)  13.3 us
    all_to_all x1, blocking collectives, body(): every = lax.all_to_all(every, GROUP, 0, 0).reshape(512, 128)  12.9 us
    pallas_call x6, Pallas kernels, call(): pl.pallas_call(kernel, out_shape=tuple((jax.ShapeDtypeStruct(shape, dtype...  7.6 us
    pallas_call x1, Pallas kernels, body(): pl.pallas_call(lambda *refs: finish(factor / count_all, *refs), out_shape...  4.24 us
    ppermute x1, waiting for transfers between devices, body(): second = lax.ppermute(second, AXES, swapped(1))  3.25 us
    ppermute x1, starting transfers between devices, body(): second = lax.ppermute(second, AXES, swapped(1))  2.74 us
  transfers between devices with their start and end apart: 2, of which 2 were waited for; matrix products, arithmetic and copies ran while one was open for 0% of the time, Pallas kernels for 1%

profile of v11, /device:TPU:1, one launch (start us, length us, event | category | flops | bytes accessed | tf_op | source)
XLA Modules:
  0.0 88.4 jit_solution(17640261806055072153)
XLA Ops:
  0.6 0.0 copy-start.2
  0.6 0.9 %copy-done.2 = bf16[32,2,16,128]{3,2,1,0:T(8,128)(2,1)S(1)} copy-done((bf16[32,2,16,128]{3,2,1,0:T(8,128)(2,1)S(1)}, bf16[32,2,16,128]{3,2,1,0:T(8,128)(2,1)}, u32[]{:S(2)}) %copy-start.2) | copy-done | bytes 262168
  1.6 0.9 pack.1
  2.4 0.0 copy-start.1
  2.5 0.0 copy-start.3
  2.5 0.0 copy-start.4
  2.5 23.5 %all_to_all.20.parts_ref = bf16[32,32,128]{2,1,0:T(8,128)(2,1)S(1)} all-to-all(bf16[32,32,128]{2,1,0:T(8,128)(2,1)S(1)} %pack.1), channel_id=1, replica_groups=mesh['gx'=4,'gy'=8,'gz'=8] {'gx','gy'}, dimensions={0} | all-to-all | bytes 524288 | tf_op jit(solution)/shard_map/all_to_all | solution.py:362
  25.9 0.0 copy-start
  25.9 0.6 arrange.1
  26.5 0.1 collective-permute-start
  26.6 2.7 %collective-permute-start.1 = (bf16[3,256,128]{2,1,0:T(8,128)(2,1)S(1)}, bf16[3,256,128]{2,1,0:T(8,128)(2,1)S(1)}, u32[]{:S(2)}, u32[]{:S(2)}) collective-permute-start(bf16[3,256,128]{2,1,0:T(8,128)(2,1)S(1)} %get-tuple-element.23), channel_id=1, source_target_pairs={{16,24},{88,80},{72,136},{144,152},{216,208},{200,40},{48,56},{120... | collective-permute-start | bytes 589832 | tf_op jit(solution)/shard_map/ppermute | solution.py:389
  29.4 0.0 copy-done.1
  29.4 0.0 copy-done.3
  29.4 0.0 copy-done.4
  29.4 0.0 copy-done
  29.4 0.5 filters.1
  29.9 0.1 convert_multiply_fusion
  30.0 1.1 %collective-permute-done.refs_1_ = bf16[3,256,128]{2,1,0:T(8,128)(2,1)S(1)} collective-permute-done((bf16[3,256,128]{2,1,0:T(8,128)(2,1)S(1)}, bf16[3,256,128]{2,1,0:T(8,128)(2,1)S(1)}, u32[]{:S(2)}, u32[]{:S(2)}) %collective-permute-start) | collective-permute-done | bytes 196640 | tf_op jit(solution)/shard_map/ppermute | solution.py:388
  31.1 3.2 %collective-permute-done.1.refs_2_ = bf16[3,256,128]{2,1,0:T(8,128)(2,1)S(1)} collective-permute-done((bf16[3,256,128]{2,1,0:T(8,128)(2,1)S(1)}, bf16[3,256,128]{2,1,0:T(8,128)(2,1)S(1)}, u32[]{:S(2)}, u32[]{:S(2)}) %collective-permute-start.1) | collective-permute-done | bytes 196640 | tf_op jit(solution)/shard_map/ppermute | solution.py:389
  34.4 5.6 %layers.1 = bf16[32,48,128]{2,1,0:T(8,128)(2,1)S(1)} custom-call(bf16[4,256,128]{2,1,0:T(8,128)(2,1)S(1)} %get-tuple-element.21.refs_0_, bf16[3,256,128]{2,1,0:T(8,128)(2,1)S(1)} %collective-permute-done.refs_1_, bf16[3,256,128]{2,1,0:T(8,128)(2,1)S(1)} %collective-permute-done.1.refs_2_, bf16[288,288]{1,0:T(8,128)(2,1)S(1)} %get-tuple-element.30.refs_3_, ...), custom_call_target="tpu_custom_call" | custom-call | flops 8000000000 | bytes 1048576 | tf_op jit(solution)/shard_map/layers/pallas_call | solution.py:339
  40.0 17.8 %all_to_all.21.parts_ref.refs_3_ = bf16[32,48,128]{2,1,0:T(8,128)(2,1)S(1)} all-to-all(bf16[32,48,128]{2,1,0:T(8,128)(2,1)S(1)} %layers.1), channel_id=1, replica_groups=mesh['gx'=4,'gy'=8,'gz'=8] {'gx','gy'}, dimensions={0} | all-to-all | bytes 786432 | tf_op jit(solution)/shard_map/all_to_all | solution.py:409
  57.9 13.3 %all_to_all.22.parts_ref = f32[8,16,128]{2,1,0:T(8,128)S(1)} all-to-all(f32[8,16,128]{2,1,0:T(8,128)S(1)} %gather_sums.1), channel_id=1, replica_groups=mesh['gx'=4,'gy'=8,'gz'=8] {'gz'}, dimensions={0} | all-to-all | bytes 131072 | tf_op jit(solution)/shard_map/all_to_all | solution.py:411
  71.2 12.9 %all_to_all.23 = bf16[32,16,128]{2,1,0:T(8,128)(2,1)S(1)} all-to-all(bf16[32,16,128]{2,1,0:T(8,128)(2,1)S(1)} %combine.1), channel_id=1, replica_groups=mesh['gx'=4,'gy'=8,'gz'=8] {'gx','gy'}, dimensions={0} | all-to-all | bytes 262144 | tf_op jit(solution)/shard_map/all_to_all | solution.py:413
  84.1 4.2 %finish.1 = (f32[27,32,32]{2,1,0:T(8,128)}, f32[27,32,32]{2,1,0:T(8,128)}, bf16[32,2,16,128]{3,2,1,0:T(8,128)(2,1)}) custom-call(bf16[512,128]{1,0:T(8,128)(2,1)S(1)} %bitcast.15, f32[27,32,32]{2,1,0:T(8,128)S(1)} %bitcast.12, f32[27,32,32]{2,1,0:T(8,128)S(1)} %bitcast.11, bf16[32,48,128]{2,1,0:T(8,128)(2,1)S(1)} %all_to_all.21.parts_ref.refs_3_), custom_call_target="tpu_custom_call" | custom-call | flops 1000000000 | bytes 1048576 | tf_op jit(solution)/shard_map/finish/pallas_call | solution.py:416
  (2 shorter events, 0.1 us)
Async XLA Ops:
  0.6 1.0 %copy-start.2 = (bf16[32,2,16,128]{3,2,1,0:T(8,128)(2,1)S(1)}, bf16[32,2,16,128]{3,2,1,0:T(8,128)(2,1)}, u32[]{:S(2)}) copy-start(bf16[32,2,16,128]{3,2,1,0:T(8,128)(2,1)} %cells_ref.1) | copy-start | bytes 786436
  2.4 26.9 %copy-start.1 = (bf16[3,3,3,32,32]{4,3,2,1,0:T(8,128)(2,1)S(1)}, bf16[3,3,3,32,32]{4,3,2,1,0:T(8,128)(2,1)}, u32[]{:S(2)}) copy-start(bf16[3,3,3,32,32]{4,3,2,1,0:T(8,128)(2,1)} %param.9) | copy-start | bytes 165892
  2.5 26.9 %copy-start.3 = (bf16[3,3,3,32,32]{4,3,2,1,0:T(8,128)(2,1)S(1)}, bf16[3,3,3,32,32]{4,3,2,1,0:T(8,128)(2,1)}, u32[]{:S(2)}) copy-start(bf16[3,3,3,32,32]{4,3,2,1,0:T(8,128)(2,1)} %param.6) | copy-start | bytes 165892
  2.5 26.9 %copy-start.4 = (bf16[3,3,3,32,32]{4,3,2,1,0:T(8,128)(2,1)S(1)}, bf16[3,3,3,32,32]{4,3,2,1,0:T(8,128)(2,1)}, u32[]{:S(2)}) copy-start(bf16[3,3,3,32,32]{4,3,2,1,0:T(8,128)(2,1)} %param.7) | copy-start | bytes 165892
  25.9 3.4 %copy-start = (bf16[3,3,3,32,32]{4,3,2,1,0:T(8,128)(2,1)S(1)}, bf16[3,3,3,32,32]{4,3,2,1,0:T(8,128)(2,1)}, u32[]{:S(2)}) copy-start(bf16[3,3,3,32,32]{4,3,2,1,0:T(8,128)(2,1)} %param.8) | copy-start | bytes 165892
  26.5 4.6 %collective-permute-start = (bf16[3,256,128]{2,1,0:T(8,128)(2,1)S(1)}, bf16[3,256,128]{2,1,0:T(8,128)(2,1)S(1)}, u32[]{:S(2)}, u32[]{:S(2)}) collective-permute-start(bf16[3,256,128]{2,1,0:T(8,128)(2,1)S(1)} %get-tuple-element.22), channel_id=1, source_target_pairs={{8,16},{24,88},{80,72},{136,144},{152,216},{208,200},{40,48},{56,1... | collective-permute-start | bytes 589832 | tf_op jit(solution)/shard_map/ppermute | solution.py:388
  26.6 7.8 %collective-permute-start.1 = (bf16[3,256,128]{2,1,0:T(8,128)(2,1)S(1)}, bf16[3,256,128]{2,1,0:T(8,128)(2,1)S(1)}, u32[]{:S(2)}, u32[]{:S(2)}) collective-permute-start(bf16[3,256,128]{2,1,0:T(8,128)(2,1)S(1)} %get-tuple-element.23), channel_id=1, source_target_pairs={{16,24},{88,80},{72,136},{144,152},{216,208},{200,40},{48,56},{120... | collective-permute-start | bytes 589832 | tf_op jit(solution)/shard_map/ppermute | solution.py:389

commit v12 on v9

--- a/solution.py
+++ b/solution.py
@@ -133,19 +133,20 @@
     return before(product[0:32]) + product[32:64] + after(product[64:96])
 
 
-def near(refs, z, x):
-    def block(ref, at):
+def near(groups, z, x, whole=False):
+    def block(column):
+        ref, at = column
         rows = ref[at, max(32 * x - 32, 0) : min(32 * x + 64, 256)]
         blank = jnp.zeros((32, 128), BF16)
-        if x == 0:
+        if whole and x == 0:
             return [blank, rows]
-        if x == PLANES - 1:
+        if whole and x == PLANES - 1:
             return [rows, blank]
         return [rows]
 
     columns = []
     for at in range(2):
-        rows = sum((block(ref, z + at + offset) for ref in refs for offset in range(3)), [])
+        rows = sum((block(group[z + at + offset]) for group in groups for offset in range(3)), [])
         columns.append(jnp.concatenate(rows, axis=0))
     return jnp.concatenate(columns, axis=1)
 
@@ -154,8 +155,8 @@
     return slice(32 * x, 32 * x + 32)
 
 
-def correlate(ref, z, targets):
-    rows = jnp.concatenate([near((ref,), z, x) for x in range(PLANES)], axis=1)
+def correlate(group, z, targets):
+    rows = jnp.concatenate([near((group,), z, x, True) for x in range(PLANES)], axis=1)
     return lax.dot_general(
         rows,
         jnp.concatenate(targets, axis=1),
@@ -171,8 +172,10 @@
     second_ref,
     weight_ref,
     joint_ref,
+    edge_ref,
+    edge_joint_ref,
     out_ref,
-    p_vol,
+    p_halo,
     p_hid,
     p_tan,
     p_jv,
@@ -183,24 +186,33 @@
     column = OWN * (lax.axis_index("gz") * MEMBERS + place)
     odd = (place & 1) == 1
 
-    @pl.when(odd)
-    def _():
-        p_vol[0:3] = first_ref[...]
-        p_vol[7:10] = second_ref[...]
-
-    @pl.when(jnp.logical_not(odd))
-    def _():
-        p_vol[0:3] = second_ref[...]
-        p_vol[7:10] = first_ref[...]
-
-    p_vol[3:7] = own_ref[...]
-
     def inside(offset):
         return (column + offset >= 0) & (column + offset < width)
 
+    for at in range(3):
+        p_halo[at] = jnp.where(odd, first_ref[at], second_ref[at])
+        p_halo[3 + at] = jnp.where(odd, second_ref[at], first_ref[at])
+    volume = [(p_halo, at) for at in range(3)]
+    volume += [(own_ref, at) for at in range(OWN)]
+    volume += [(p_halo, 3 + at) for at in range(3)]
+    hidden_columns = [(p_hid, at) for at in range(8)]
+    tangent_columns = [(p_tan, at) for at in range(8)]
+    jv_columns = [(p_jv, at) for at in range(6)]
+
+    def weights(ref, edge, rows, x):
+        if x == 0:
+            return edge[0, rows]
+        if x == PLANES - 1:
+            return edge[1, rows]
+        return ref[rows]
+
     for z in range(0, 8, 2):
         for x in range(PLANES):
-            product = jnp.dot(weight_ref[0:192, :], near((p_vol,), z, x), preferred_element_type=F32)
+            product = jnp.dot(
+                weights(weight_ref, edge_ref, slice(0, 192), x),
+                near((volume,), z, x),
+                preferred_element_type=F32,
+            )
             for at in range(2):
                 part = product[:, 128 * at : 128 * at + 128]
                 here = inside(z + at - 2)
@@ -213,11 +225,21 @@
 
     for z in range(0, 6, 2):
         for x in range(PLANES):
-            product = jnp.dot(joint_ref[...], near((p_tan, p_hid), z, x), preferred_element_type=F32)
+            product = jnp.dot(
+                weights(joint_ref, edge_joint_ref, slice(0, 96), x),
+                near((tangent_columns, hidden_columns), z, x),
+                preferred_element_type=F32,
+            )
             for at in range(2):
                 jv = fold(product[:, 128 * at : 128 * at + 128])
                 jv = jnp.where(inside(z + at - 1), jv, 0.0)
                 p_jv[z + at, tile_of(x)] = jv.astype(BF16)
+
+    for g in range(4):
+        tiles = [p_jv[1 + i // 2, tile_of(2 * g + i % 2)].astype(F32) for i in range(8)]
+        tiles = exchange(tiles, (4, 5, 6))
+        for j in range(8):
+            out_ref[8 * g + j, 0:32] = tiles[j].astype(BF16)
 
     def spread(tiles):
         both = [
@@ -232,22 +254,20 @@
             spread([p_jv[z + at + 1, tile_of(x)].astype(F32) for at in range(2)])
             for x in range(PLANES)
         ]
-        sums_second = sums_second + correlate(p_hid, z + 1, targets)
+        sums_second = sums_second + correlate(hidden_columns, z + 1, targets)
         targets = []
         for x in range(PLANES):
-            product = jnp.dot(weight_ref[192:288, :], near((p_jv,), z, x), preferred_element_type=F32)
+            product = jnp.dot(
+                weights(weight_ref, edge_ref, slice(192, 288), x),
+                near((jv_columns,), z, x),
+                preferred_element_type=F32,
+            )
             tiles = []
             for at in range(2):
                 back = slopes[z + at, x] * fold(product[:, 128 * at : 128 * at + 128])
                 tiles.append(back.astype(BF16).astype(F32))
             targets.append(spread(tiles))
-        sums_first = sums_first + correlate(p_vol, z + 2, targets)
-
-    for g in range(4):
-        tiles = [p_jv[1 + i // 2, tile_of(2 * g + i % 2)].astype(F32) for i in range(8)]
-        tiles = exchange(tiles, (4, 5, 6))
-        for j in range(8):
-            out_ref[8 * g + j, 0:32] = tiles[j].astype(BF16)
+        sums_first = sums_first + correlate(volume, z + 2, targets)
 
     rest = pltpu.roll(sums_first, 96, 1)
     packed[0:288] = jnp.where(lanes_of((288, 128)) < 96, sums_second, rest)
@@ -295,29 +315,39 @@
         first_ref[6 + column] = damped(far[:, 32:64], d_first_ref[6 + column])
 
 
-def filters(w_first_ref, v_first_ref, w_second_ref, v_second_ref, rows_ref, joint_ref):
-    def tall(ref):
-        return jnp.concatenate(
-            [
-                jnp.concatenate(
-                    [ref[9 * (k % 3) + 3 * row + k // 3].astype(F32) for k in range(9)], axis=0
-                )
-                for row in range(3)
-            ],
-            axis=1,
-        )
-
-    def turned(refs):
-        return jnp.concatenate([tall(ref) for ref in refs], axis=0).T.astype(BF16)
-
-    rows_ref[0:96] = turned([w_first_ref])
-    rows_ref[96:192] = turned([v_first_ref])
-    joint_ref[...] = turned([w_second_ref, v_second_ref])
-    for row in range(3):
+def filters(
+    w_first_ref, v_first_ref, w_second_ref, v_second_ref, rows_ref, joint_ref, edge_ref, edge_joint_ref
+):
+    def turned(refs, depths):
+        blocks = [(x, z) for z in range(3) for x in depths]
+        tall = [
+            jnp.concatenate(
+                [
+                    jnp.concatenate([ref[9 * x + 3 * row + z].astype(F32) for x, z in blocks], axis=0)
+                    for row in range(3)
+                ],
+                axis=1,
+            )
+            for ref in refs
+        ]
+        return jnp.concatenate(tall, axis=0).T.astype(BF16)
+
+    def flipped(row, depths):
         blocks = [
-            w_second_ref[26 - (9 * (k % 3) + 3 * row + k // 3)].astype(F32) for k in range(9)
+            w_second_ref[26 - (9 * x + 3 * row + z)].astype(F32) for z in range(3) for x in depths
         ]
-        rows_ref[192 + 32 * row : 224 + 32 * row] = jnp.concatenate(blocks, axis=1).astype(BF16)
+        return jnp.concatenate(blocks, axis=1).astype(BF16)
+
+    for depths, rows, joint in (
+        ((0, 1, 2), rows_ref, joint_ref),
+        ((1, 2), edge_ref.at[0], edge_joint_ref.at[0]),
+        ((0, 1), edge_ref.at[1], edge_joint_ref.at[1]),
+    ):
+        rows[0:96] = turned([w_first_ref], depths)
+        rows[96:192] = turned([v_first_ref], depths)
+        joint[...] = turned([w_second_ref, v_second_ref], depths)
+        for row in range(3):
+            rows[192 + 32 * row : 224 + 32 * row] = flipped(row, depths)
 
 
 def call(kernel, operands, outputs, scratch, name, limit, flops):
@@ -352,7 +382,13 @@
     )
     blocks = [w.reshape(27, channels, channels) for w in (w_first, v_first, w_second, v_second)]
     weights = call(
-        filters, blocks, [((288, 288), BF16), ((96, 576), BF16)], [], "filters", 8, 2 * 10**8
+        filters,
+        blocks,
+        [((288, 288), BF16), ((96, 576), BF16), ((2, 288, 192), BF16), ((2, 96, 384), BF16)],
+        [],
+        "filters",
+        8,
+        2 * 10**8,
     )
     damping = tuple(
         factor * 0.1 * v.astype(F32).reshape(27, channels, channels) for v in (v_first, v_second)
@@ -379,7 +415,7 @@
         (own, first, second, *weights),
         [((members, 48, 128), BF16)],
         [
-            ((10, 256, 128), BF16),
+            ((6, 256, 128), BF16),
             ((8, 256, 128), BF16),
             ((8, 256, 128), BF16),
             ((6, 256, 128), BF16),

time: 87.4 us -> 86.8 us (level)
  no operation moved by 1% of the time
where the time goes in v12:
time: 86.8 us; the launch traced here: 86.5 us
  blocking collectives  54.5 us (63%)
  waiting for transfers between devices  11.8 us (14%)
  Pallas kernels  11.6 us (13%)
  starting transfers between devices  6.7 us (8%)
  local copies, waits for them, and re-layouts  0.97 us (1%)
    all_to_all x1, blocking collectives, body(): parts = lax.all_to_all(sent, GROUP, 0, 0)  23.5 us
    all_to_all x1, blocking collectives, body(): parts = lax.all_to_all(leaving, GROUP, 0, 0)  17.8 us
    all_to_all x1, blocking collectives, body(): sums = lax.all_to_all(sums, 'gz', 0, 0)  13.3 us
    pallas_call x7, Pallas kernels, call(): pl.pallas_call(kernel, out_shape=tuple((jax.ShapeDtypeStruct(shape, dtype...  9.76 us
    all_to_all x1, waiting for transfers between devices, body(): every = lax.all_to_all(every, GROUP, 0, 0).reshape(512, 128)  7.69 us
    all_to_all x1, starting transfers between devices, body(): every = lax.all_to_all(every, GROUP, 0, 0).reshape(512, 128)  3.86 us
    ppermute x1, waiting for transfers between devices, body(): second = lax.ppermute(second, AXES, swapped(1))  3.25 us
    ppermute x1, starting transfers between devices, body(): second = lax.ppermute(second, AXES, swapped(1))  2.74 us
  transfers between devices with their start and end apart: 3, of which 3 were waited for; matrix products, arithmetic and copies ran while one was open for 0% of the time, Pallas kernels for 3%

profile of v12, /device:TPU:1, one launch (start us, length us, event | category | flops | bytes accessed | tf_op | source)
XLA Modules:
  0.0 86.5 jit_solution(10851894980473369653)
XLA Ops:
  0.6 0.0 copy-start.2
  0.6 0.9 %copy-done.2 = bf16[32,2,16,128]{3,2,1,0:T(8,128)(2,1)S(1)} copy-done((bf16[32,2,16,128]{3,2,1,0:T(8,128)(2,1)S(1)}, bf16[32,2,16,128]{3,2,1,0:T(8,128)(2,1)}, u32[]{:S(2)}) %copy-start.2) | copy-done | bytes 262168
  1.6 0.9 pack.1
  2.4 0.0 copy-start.1
  2.5 0.0 copy-start.3
  2.5 0.0 copy-start.4
  2.5 23.5 %all_to_all.20.parts_ref = bf16[32,32,128]{2,1,0:T(8,128)(2,1)S(1)} all-to-all(bf16[32,32,128]{2,1,0:T(8,128)(2,1)S(1)} %pack.1), channel_id=1, replica_groups=mesh['gx'=4,'gy'=8,'gz'=8] {'gx','gy'}, dimensions={0} | all-to-all | bytes 524288 | tf_op jit(solution)/shard_map/all_to_all | solution.py:378
  25.9 0.0 copy-start
  25.9 0.6 arrange.1
  26.5 0.1 collective-permute-start
  26.6 2.7 %collective-permute-start.1 = (bf16[3,256,128]{2,1,0:T(8,128)(2,1)S(1)}, bf16[3,256,128]{2,1,0:T(8,128)(2,1)S(1)}, u32[]{:S(2)}, u32[]{:S(2)}) collective-permute-start(bf16[3,256,128]{2,1,0:T(8,128)(2,1)S(1)} %get-tuple-element.20), channel_id=1, source_target_pairs={{16,24},{88,80},{72,136},{144,152},{216,208},{200,40},{48,56},{120... | collective-permute-start | bytes 589832 | tf_op jit(solution)/shard_map/ppermute | solution.py:411
  29.4 0.0 copy-done.1
  29.4 0.0 copy-done.3
  29.4 0.0 copy-done.4
  29.4 0.0 copy-done
  29.4 0.9 %filters.1 = (bf16[288,288]{1,0:T(8,128)(2,1)S(1)}, bf16[96,576]{1,0:T(8,128)(2,1)S(1)}, bf16[2,288,192]{2,1,0:T(8,128)(2,1)S(1)}, bf16[2,96,384]{2,1,0:T(8,128)(2,1)S(1)}) custom-call(bf16[27,32,32]{2,1,0:T(8,128)(2,1)S(1)} %bitcast.14, bf16[27,32,32]{2,1,0:T(8,128)(2,1)S(1)} %bitcast.11, bf16[27,32,32]{2,1,0:T(8,128)(2,1)S(1)} %bitcast.15, ...), custom_call_target="tpu_custom_call" | custom-call | flops 200000000 | bytes 1048576 | tf_op jit(solution)/shard_map/filters/pallas_call | solution.py:355
  30.3 0.8 collective-permute-done.refs_1_
  31.1 3.2 %collective-permute-done.1.refs_2_ = bf16[3,256,128]{2,1,0:T(8,128)(2,1)S(1)} collective-permute-done((bf16[3,256,128]{2,1,0:T(8,128)(2,1)S(1)}, bf16[3,256,128]{2,1,0:T(8,128)(2,1)S(1)}, u32[]{:S(2)}, u32[]{:S(2)}) %collective-permute-start.1) | collective-permute-done | bytes 196640 | tf_op jit(solution)/shard_map/ppermute | solution.py:411
  34.4 5.1 %layers.1 = bf16[32,48,128]{2,1,0:T(8,128)(2,1)S(1)} custom-call(bf16[4,256,128]{2,1,0:T(8,128)(2,1)S(1)} %get-tuple-element.18.refs_0_, bf16[3,256,128]{2,1,0:T(8,128)(2,1)S(1)} %collective-permute-done.refs_1_, bf16[3,256,128]{2,1,0:T(8,128)(2,1)S(1)} %collective-permute-done.1.refs_2_, bf16[288,288]{1,0:T(8,128)(2,1)S(1)} %get-tuple-element.25.refs_3_, ...), custom_call_target="tpu_custom_call" | custom-call | flops 8000000000 | bytes 1048576 | tf_op jit(solution)/shard_map/layers/pallas_call | solution.py:355
  39.4 17.8 %all_to_all.21.parts_ref = bf16[32,48,128]{2,1,0:T(8,128)(2,1)S(1)} all-to-all(bf16[32,48,128]{2,1,0:T(8,128)(2,1)S(1)} %layers.1), channel_id=1, replica_groups=mesh['gx'=4,'gy'=8,'gz'=8] {'gx','gy'}, dimensions={0} | all-to-all | bytes 786432 | tf_op jit(solution)/shard_map/all_to_all | solution.py:430
  57.3 13.3 %all_to_all.22.parts_ref = f32[8,16,128]{2,1,0:T(8,128)S(1)} all-to-all(f32[8,16,128]{2,1,0:T(8,128)S(1)} %gather_sums.1), channel_id=1, replica_groups=mesh['gx'=4,'gy'=8,'gz'=8] {'gz'}, dimensions={0} | all-to-all | bytes 131072 | tf_op jit(solution)/shard_map/all_to_all | solution.py:432
  70.6 0.7 combine.1
  71.2 3.9 %all-to-all-start.3 = ((bf16[32,16,128]{2,1,0:T(8,128)(2,1)}), bf16[32,16,128]{2,1,0:T(8,128)(2,1)S(1)}, u32[]{:S(2)}, u32[]{:S(2)}) async-start(bf16[32,16,128]{2,1,0:T(8,128)(2,1)} %combine.1), calls=%async_computation.3 | async-start | bytes 262144 | tf_op jit(solution)/shard_map/all_to_all | solution.py:434
  75.1 0.1 convert_multiply_fusion
  75.2 1.7 %unpack.1 = bf16[32,2,16,128]{3,2,1,0:T(8,128)(2,1)} custom-call(bf16[32,48,128]{2,1,0:T(8,128)(2,1)S(1)} %all_to_all.21.parts_ref), custom_call_target="tpu_custom_call" | custom-call | flops 1000000000 | bytes 1048576 | tf_op jit(solution)/shard_map/unpack/pallas_call | solution.py:355
  76.9 7.7 %all-to-all-done.3 = bf16[32,16,128]{2,1,0:T(8,128)(2,1)S(1)} async-done(((bf16[32,16,128]{2,1,0:T(8,128)(2,1)}), bf16[32,16,128]{2,1,0:T(8,128)(2,1)S(1)}, u32[]{:S(2)}, u32[]{:S(2)}) %all-to-all-start.3) | async-done | bytes 131104 | tf_op jit(solution)/shard_map/all_to_all | solution.py:434
  84.6 1.9 %finish.1 = (f32[27,32,32]{2,1,0:T(8,128)}, f32[27,32,32]{2,1,0:T(8,128)}) custom-call(bf16[512,128]{1,0:T(8,128)(2,1)S(1)} %bitcast.13, f32[27,32,32]{2,1,0:T(8,128)S(1)} %bitcast.10, f32[27,32,32]{2,1,0:T(8,128)S(1)} %bitcast.9), custom_call_target="tpu_custom_call" | custom-call | tf_op jit(solution)/shard_map/finish/pallas_call | solution.py:445
  (1 shorter events, 0.0 us)
Async XLA Ops:
  0.6 1.0 %copy-start.2 = (bf16[32,2,16,128]{3,2,1,0:T(8,128)(2,1)S(1)}, bf16[32,2,16,128]{3,2,1,0:T(8,128)(2,1)}, u32[]{:S(2)}) copy-start(bf16[32,2,16,128]{3,2,1,0:T(8,128)(2,1)} %cells_ref.1) | copy-start | bytes 786436
  2.4 26.9 %copy-start.1 = (bf16[3,3,3,32,32]{4,3,2,1,0:T(8,128)(2,1)S(1)}, bf16[3,3,3,32,32]{4,3,2,1,0:T(8,128)(2,1)}, u32[]{:S(2)}) copy-start(bf16[3,3,3,32,32]{4,3,2,1,0:T(8,128)(2,1)} %param.9) | copy-start | bytes 165892
  2.5 26.9 %copy-start.3 = (bf16[3,3,3,32,32]{4,3,2,1,0:T(8,128)(2,1)S(1)}, bf16[3,3,3,32,32]{4,3,2,1,0:T(8,128)(2,1)}, u32[]{:S(2)}) copy-start(bf16[3,3,3,32,32]{4,3,2,1,0:T(8,128)(2,1)} %param.6) | copy-start | bytes 165892
  2.5 26.9 %copy-start.4 = (bf16[3,3,3,32,32]{4,3,2,1,0:T(8,128)(2,1)S(1)}, bf16[3,3,3,32,32]{4,3,2,1,0:T(8,128)(2,1)}, u32[]{:S(2)}) copy-start(bf16[3,3,3,32,32]{4,3,2,1,0:T(8,128)(2,1)} %param.7) | copy-start | bytes 165892
  25.9 3.4 %copy-start = (bf16[3,3,3,32,32]{4,3,2,1,0:T(8,128)(2,1)S(1)}, bf16[3,3,3,32,32]{4,3,2,1,0:T(8,128)(2,1)}, u32[]{:S(2)}) copy-start(bf16[3,3,3,32,32]{4,3,2,1,0:T(8,128)(2,1)} %param.8) | copy-start | bytes 165892
  26.5 4.6 %collective-permute-start = (bf16[3,256,128]{2,1,0:T(8,128)(2,1)S(1)}, bf16[3,256,128]{2,1,0:T(8,128)(2,1)S(1)}, u32[]{:S(2)}, u32[]{:S(2)}) collective-permute-start(bf16[3,256,128]{2,1,0:T(8,128)(2,1)S(1)} %get-tuple-element.19), channel_id=1, source_target_pairs={{8,16},{24,88},{80,72},{136,144},{152,216},{208,200},{40,48},{56,1... | collective-permute-start | bytes 589832 | tf_op jit(solution)/shard_map/ppermute | solution.py:410
  26.6 7.8 %collective-permute-start.1 = (bf16[3,256,128]{2,1,0:T(8,128)(2,1)S(1)}, bf16[3,256,128]{2,1,0:T(8,128)(2,1)S(1)}, u32[]{:S(2)}, u32[]{:S(2)}) collective-permute-start(bf16[3,256,128]{2,1,0:T(8,128)(2,1)S(1)} %get-tuple-element.20), channel_id=1, source_target_pairs={{16,24},{88,80},{72,136},{144,152},{216,208},{200,40},{48,56},{120... | collective-permute-start | bytes 589832 | tf_op jit(solution)/shard_map/ppermute | solution.py:411
  71.2 13.4 %all-to-all-start.3 = ((bf16[32,16,128]{2,1,0:T(8,128)(2,1)}), bf16[32,16,128]{2,1,0:T(8,128)(2,1)S(1)}, u32[]{:S(2)}, u32[]{:S(2)}) async-start(bf16[32,16,128]{2,1,0:T(8,128)(2,1)} %combine.1), calls=%async_computation.3 | async-start | bytes 262144 | tf_op jit(solution)/shard_map/all_to_all | solution.py:434

commit v13 on v12

--- a/solution.py
+++ b/solution.py
@@ -409,6 +409,7 @@
 
     first = lax.ppermute(first, AXES, swapped(0))
     second = lax.ppermute(second, AXES, swapped(1))
+    first, second, damping = lax.optimization_barrier((first, second, damping))
 
     (leaving,) = call(
         lambda *refs: layers(width * n_gz, *refs),
@@ -430,8 +431,6 @@
     parts = lax.all_to_all(leaving, GROUP, 0, 0)
     (sums,) = call(gather_sums, (parts,), [((n_gz, 16, 128), F32)], [], "gather_sums", 8, 10**8)
     sums = lax.all_to_all(sums, "gz", 0, 0)
-    (every,) = call(combine, (sums,), [((members, 16, 128), BF16)], [], "combine", 8, 10**8)
-    every = lax.all_to_all(every, GROUP, 0, 0).reshape(512, 128)
     (out,) = call(
         unpack,
         (parts,),
@@ -441,6 +440,9 @@
         8,
         10**9,
     )
+    sums, out = lax.optimization_barrier((sums, out))
+    (every,) = call(combine, (sums,), [((members, 16, 128), BF16)], [], "combine", 8, 10**8)
+    every = lax.all_to_all(every, GROUP, 0, 0).reshape(512, 128)
     third = pl.BlockSpec((9, channels, channels), lambda i: (i, 0, 0))
     gv_first, gv_second = pl.pallas_call(
         lambda *refs: finish(factor / count_all, *refs),

time: 86.8 us -> 86.5 us (level)
  starting transfers between devices: 6.7 us -> 11.5 us
  waiting for transfers between devices: 11.8 us -> 7.12 us
    all_to_all x1, starting transfers between devices: 3.86 us -> 8.61 us  [body(): sums = lax.all_to_all(sums, 'gz', 0, 0)]
    all_to_all x1, waiting for transfers between devices: 7.69 us -> 3.15 us  [body(): sums = lax.all_to_all(sums, 'gz', 0, 0)]
where the time goes in v13:
time: 86.5 us; the launch traced here: 86.2 us
  blocking collectives  54.2 us (63%)
  Pallas kernels  11.6 us (13%)
  starting transfers between devices  11.5 us (13%)
  waiting for transfers between devices  7.12 us (8%)
  local copies, waits for them, and re-layouts  0.97 us (1%)
    all_to_all x1, blocking collectives, body(): parts = lax.all_to_all(sent, GROUP, 0, 0)  23.5 us
    all_to_all x1, blocking collectives, body(): parts = lax.all_to_all(leaving, GROUP, 0, 0)  17.8 us
    all_to_all x1, blocking collectives, body(): every = lax.all_to_all(every, GROUP, 0, 0).reshape(512, 128)  12.9 us
    pallas_call x7, Pallas kernels, call(): pl.pallas_call(kernel, out_shape=tuple((jax.ShapeDtypeStruct(shape, dtype...  9.73 us
    all_to_all x1, starting transfers between devices, body(): sums = lax.all_to_all(sums, 'gz', 0, 0)  8.61 us
    ppermute x1, waiting for transfers between devices, body(): second = lax.ppermute(second, AXES, swapped(1))  3.25 us
    all_to_all x1, waiting for transfers between devices, body(): sums = lax.all_to_all(sums, 'gz', 0, 0)  3.15 us
    ppermute x1, starting transfers between devices, body(): second = lax.ppermute(second, AXES, swapped(1))  2.74 us
  transfers between devices with their start and end apart: 3, of which 3 were waited for; matrix products, arithmetic and copies ran while one was open for 0% of the time, Pallas kernels for 3%

profile of v13, /device:TPU:1, one launch (start us, length us, event | category | flops | bytes accessed | tf_op | source)
XLA Modules:
  0.0 86.2 jit_solution(214830428474397426)
XLA Ops:
  0.6 0.0 copy-start.2
  0.6 0.9 %copy-done.2 = bf16[32,2,16,128]{3,2,1,0:T(8,128)(2,1)S(1)} copy-done((bf16[32,2,16,128]{3,2,1,0:T(8,128)(2,1)S(1)}, bf16[32,2,16,128]{3,2,1,0:T(8,128)(2,1)}, u32[]{:S(2)}) %copy-start.2) | copy-done | bytes 262168
  1.6 0.9 pack.1
  2.4 0.0 copy-start.1
  2.5 0.0 copy-start.3
  2.5 0.0 copy-start.4
  2.5 23.5 %all_to_all.20.parts_ref = bf16[32,32,128]{2,1,0:T(8,128)(2,1)S(1)} all-to-all(bf16[32,32,128]{2,1,0:T(8,128)(2,1)S(1)} %pack.1), channel_id=1, replica_groups=mesh['gx'=4,'gy'=8,'gz'=8] {'gx','gy'}, dimensions={0} | all-to-all | bytes 524288 | tf_op jit(solution)/shard_map/all_to_all | solution.py:378
  25.9 0.0 copy-start
  25.9 0.6 arrange.1
  26.5 0.1 collective-permute-start
  26.6 2.7 %collective-permute-start.1 = (bf16[3,256,128]{2,1,0:T(8,128)(2,1)S(1)}, bf16[3,256,128]{2,1,0:T(8,128)(2,1)S(1)}, u32[]{:S(2)}, u32[]{:S(2)}) collective-permute-start(bf16[3,256,128]{2,1,0:T(8,128)(2,1)S(1)} %get-tuple-element.26), channel_id=1, source_target_pairs={{16,24},{88,80},{72,136},{144,152},{216,208},{200,40},{48,56},{120... | collective-permute-start | bytes 589832 | tf_op jit(solution)/shard_map/ppermute | solution.py:411
  29.4 0.0 copy-done.1
  29.4 0.0 copy-done.3
  29.4 0.0 copy-done.4
  29.4 0.0 copy-done
  29.4 0.9 %filters.1 = (bf16[288,288]{1,0:T(8,128)(2,1)S(1)}, bf16[96,576]{1,0:T(8,128)(2,1)S(1)}, bf16[2,288,192]{2,1,0:T(8,128)(2,1)S(1)}, bf16[2,96,384]{2,1,0:T(8,128)(2,1)S(1)}) custom-call(bf16[27,32,32]{2,1,0:T(8,128)(2,1)S(1)} %bitcast.14, bf16[27,32,32]{2,1,0:T(8,128)(2,1)S(1)} %bitcast.11, bf16[27,32,32]{2,1,0:T(8,128)(2,1)S(1)} %bitcast.15, ...), custom_call_target="tpu_custom_call" | custom-call | flops 200000000 | bytes 1048576 | tf_op jit(solution)/shard_map/filters/pallas_call | solution.py:355
  30.3 0.1 convert_multiply_fusion
  30.4 0.7 collective-permute-done.refs_1_
  31.1 3.2 %collective-permute-done.1.refs_2_ = bf16[3,256,128]{2,1,0:T(8,128)(2,1)S(1)} collective-permute-done((bf16[3,256,128]{2,1,0:T(8,128)(2,1)S(1)}, bf16[3,256,128]{2,1,0:T(8,128)(2,1)S(1)}, u32[]{:S(2)}, u32[]{:S(2)}) %collective-permute-start.1) | collective-permute-done | bytes 196640 | tf_op jit(solution)/shard_map/ppermute | solution.py:411
  34.4 5.1 %layers.1 = bf16[32,48,128]{2,1,0:T(8,128)(2,1)S(1)} custom-call(bf16[4,256,128]{2,1,0:T(8,128)(2,1)S(1)} %get-tuple-element.24.refs_0_, bf16[3,256,128]{2,1,0:T(8,128)(2,1)S(1)} %collective-permute-done.refs_1_, bf16[3,256,128]{2,1,0:T(8,128)(2,1)S(1)} %collective-permute-done.1.refs_2_, bf16[288,288]{1,0:T(8,128)(2,1)S(1)} %get-tuple-element.33.refs_3_, ...), custom_call_target="tpu_custom_call" | custom-call | flops 8000000000 | bytes 1048576 | tf_op jit(solution)/shard_map/layers/pallas_call | solution.py:355
  39.4 17.8 %all_to_all.21.parts_ref = bf16[32,48,128]{2,1,0:T(8,128)(2,1)S(1)} all-to-all(bf16[32,48,128]{2,1,0:T(8,128)(2,1)S(1)} %layers.1), channel_id=1, replica_groups=mesh['gx'=4,'gy'=8,'gz'=8] {'gx','gy'}, dimensions={0} | all-to-all | bytes 786432 | tf_op jit(solution)/shard_map/all_to_all | solution.py:431
  57.3 0.7 gather_sums.1
  57.9 8.6 %all-to-all-start.2 = ((f32[8,16,128]{2,1,0:T(8,128)}), f32[8,16,128]{2,1,0:T(8,128)S(1)}, u32[]{:S(2)}, u32[]{:S(2)}) async-start(f32[8,16,128]{2,1,0:T(8,128)} %gather_sums.1), calls=%async_computation.2 | async-start | bytes 131072 | tf_op jit(solution)/shard_map/all_to_all | solution.py:433
  66.5 1.7 %unpack.1 = bf16[32,2,16,128]{3,2,1,0:T(8,128)(2,1)} custom-call(bf16[32,48,128]{2,1,0:T(8,128)(2,1)S(1)} %all_to_all.21.parts_ref), custom_call_target="tpu_custom_call" | custom-call | flops 1000000000 | bytes 1048576 | tf_op jit(solution)/shard_map/unpack/pallas_call | solution.py:355
  68.2 3.2 %all-to-all-done.2.parts_ref = f32[8,16,128]{2,1,0:T(8,128)S(1)} async-done(((f32[8,16,128]{2,1,0:T(8,128)}), f32[8,16,128]{2,1,0:T(8,128)S(1)}, u32[]{:S(2)}, u32[]{:S(2)}) %all-to-all-start.2) | async-done | bytes 65568 | tf_op jit(solution)/shard_map/all_to_all | solution.py:433
  71.4 12.9 %all_to_all.22 = bf16[32,16,128]{2,1,0:T(8,128)(2,1)S(1)} all-to-all(bf16[32,16,128]{2,1,0:T(8,128)(2,1)S(1)} %combine.1), channel_id=1, replica_groups=mesh['gx'=4,'gy'=8,'gz'=8] {'gx','gy'}, dimensions={0} | all-to-all | bytes 262144 | tf_op jit(solution)/shard_map/all_to_all | solution.py:445
  84.3 1.9 %finish.1 = (f32[27,32,32]{2,1,0:T(8,128)}, f32[27,32,32]{2,1,0:T(8,128)}) custom-call(bf16[512,128]{1,0:T(8,128)(2,1)S(1)} %bitcast.13, f32[27,32,32]{2,1,0:T(8,128)S(1)} %bitcast.10, f32[27,32,32]{2,1,0:T(8,128)S(1)} %bitcast.9), custom_call_target="tpu_custom_call" | custom-call | tf_op jit(solution)/shard_map/finish/pallas_call | solution.py:447
  (1 shorter events, 0.0 us)
Async XLA Ops:
  0.6 1.0 %copy-start.2 = (bf16[32,2,16,128]{3,2,1,0:T(8,128)(2,1)S(1)}, bf16[32,2,16,128]{3,2,1,0:T(8,128)(2,1)}, u32[]{:S(2)}) copy-start(bf16[32,2,16,128]{3,2,1,0:T(8,128)(2,1)} %cells_ref.1) | copy-start | bytes 786436
  2.4 26.9 %copy-start.1 = (bf16[3,3,3,32,32]{4,3,2,1,0:T(8,128)(2,1)S(1)}, bf16[3,3,3,32,32]{4,3,2,1,0:T(8,128)(2,1)}, u32[]{:S(2)}) copy-start(bf16[3,3,3,32,32]{4,3,2,1,0:T(8,128)(2,1)} %param.9) | copy-start | bytes 165892
  2.5 26.9 %copy-start.3 = (bf16[3,3,3,32,32]{4,3,2,1,0:T(8,128)(2,1)S(1)}, bf16[3,3,3,32,32]{4,3,2,1,0:T(8,128)(2,1)}, u32[]{:S(2)}) copy-start(bf16[3,3,3,32,32]{4,3,2,1,0:T(8,128)(2,1)} %param.6) | copy-start | bytes 165892
  2.5 26.9 %copy-start.4 = (bf16[3,3,3,32,32]{4,3,2,1,0:T(8,128)(2,1)S(1)}, bf16[3,3,3,32,32]{4,3,2,1,0:T(8,128)(2,1)}, u32[]{:S(2)}) copy-start(bf16[3,3,3,32,32]{4,3,2,1,0:T(8,128)(2,1)} %param.7) | copy-start | bytes 165892
  25.9 3.4 %copy-start = (bf16[3,3,3,32,32]{4,3,2,1,0:T(8,128)(2,1)S(1)}, bf16[3,3,3,32,32]{4,3,2,1,0:T(8,128)(2,1)}, u32[]{:S(2)}) copy-start(bf16[3,3,3,32,32]{4,3,2,1,0:T(8,128)(2,1)} %param.8) | copy-start | bytes 165892
  26.5 4.6 %collective-permute-start = (bf16[3,256,128]{2,1,0:T(8,128)(2,1)S(1)}, bf16[3,256,128]{2,1,0:T(8,128)(2,1)S(1)}, u32[]{:S(2)}, u32[]{:S(2)}) collective-permute-start(bf16[3,256,128]{2,1,0:T(8,128)(2,1)S(1)} %get-tuple-element.25), channel_id=1, source_target_pairs={{8,16},{24,88},{80,72},{136,144},{152,216},{208,200},{40,48},{56,1... | collective-permute-start | bytes 589832 | tf_op jit(solution)/shard_map/ppermute | solution.py:410
  26.6 7.8 %collective-permute-start.1 = (bf16[3,256,128]{2,1,0:T(8,128)(2,1)S(1)}, bf16[3,256,128]{2,1,0:T(8,128)(2,1)S(1)}, u32[]{:S(2)}, u32[]{:S(2)}) collective-permute-start(bf16[3,256,128]{2,1,0:T(8,128)(2,1)S(1)} %get-tuple-element.26), channel_id=1, source_target_pairs={{16,24},{88,80},{72,136},{144,152},{216,208},{200,40},{48,56},{120... | collective-permute-start | bytes 589832 | tf_op jit(solution)/shard_map/ppermute | solution.py:411
  57.9 13.5 %all-to-all-start.2 = ((f32[8,16,128]{2,1,0:T(8,128)}), f32[8,16,128]{2,1,0:T(8,128)S(1)}, u32[]{:S(2)}, u32[]{:S(2)}) async-start(f32[8,16,128]{2,1,0:T(8,128)} %gather_sums.1), calls=%async_computation.2 | async-start | bytes 131072 | tf_op jit(solution)/shard_map/all_to_all | solution.py:433

commit v14 on v12

--- a/solution.py
+++ b/solution.py
@@ -133,7 +133,7 @@
     return before(product[0:32]) + product[32:64] + after(product[64:96])
 
 
-def near(groups, z, x, whole=False):
+def near(groups, pair, x, whole=False):
     def block(column):
         ref, at = column
         rows = ref[at, max(32 * x - 32, 0) : min(32 * x + 64, 256)]
@@ -145,8 +145,8 @@
         return [rows]
 
     columns = []
-    for at in range(2):
-        rows = sum((block(group[z + at + offset]) for group in groups for offset in range(3)), [])
+    for z in pair:
+        rows = sum((block(group[z + offset]) for group in groups for offset in range(3)), [])
         columns.append(jnp.concatenate(rows, axis=0))
     return jnp.concatenate(columns, axis=1)
 
@@ -156,13 +156,44 @@
 
 
 def correlate(group, z, targets):
-    rows = jnp.concatenate([near((group,), z, x, True) for x in range(PLANES)], axis=1)
+    rows = jnp.concatenate([near((group,), (z, z + 1), x, True) for x in range(PLANES)], axis=1)
     return lax.dot_general(
         rows,
         jnp.concatenate(targets, axis=1),
         (((1,), (1,)), ((), ())),
         preferred_element_type=F32,
     )
+
+
+def weights(ref, edge, rows, x):
+    if x == 0:
+        return edge[0, rows]
+    if x == PLANES - 1:
+        return edge[1, rows]
+    return ref[rows]
+
+
+def first_layer(weight_ref, edge_ref, volume, pair, x):
+    product = jnp.dot(
+        weights(weight_ref, edge_ref, slice(0, 192), x),
+        near((volume,), pair, x),
+        preferred_element_type=F32,
+    )
+    for at in range(2):
+        part = product[:, 128 * at : 128 * at + 128]
+        hidden, slope = gelu_pair(fold(part[0:96]))
+        yield hidden, slope * fold(part[96:192]), slope
+
+
+def inner(own_ref, weight_ref, edge_ref, hidden_ref, tangent_ref, slope_ref):
+    volume = [(own_ref, at) for at in range(OWN)]
+    for x in range(PLANES):
+        for at, (hidden, tangent, slope) in enumerate(
+            first_layer(weight_ref, edge_ref, volume, (0, 1), x)
+        ):
+            hidden_ref[at, tile_of(x)] = hidden.astype(BF16)
+            tangent_ref[at, tile_of(x)] = tangent.astype(BF16)
+            slope_ref[at, x] = slope
 
 
 def layers(
@@ -174,6 +205,9 @@
     joint_ref,
     edge_ref,
     edge_joint_ref,
+    hidden_ref,
+    tangent_ref,
+    slope_ref,
     out_ref,
     p_halo,
     p_hid,
@@ -197,37 +231,27 @@
     volume += [(p_halo, 3 + at) for at in range(3)]
     hidden_columns = [(p_hid, at) for at in range(8)]
     tangent_columns = [(p_tan, at) for at in range(8)]
+    for at in range(2):
+        hidden_columns[3 + at] = (hidden_ref, at)
+        tangent_columns[3 + at] = (tangent_ref, at)
     jv_columns = [(p_jv, at) for at in range(6)]
 
-    def weights(ref, edge, rows, x):
-        if x == 0:
-            return edge[0, rows]
-        if x == PLANES - 1:
-            return edge[1, rows]
-        return ref[rows]
-
-    for z in range(0, 8, 2):
+    for pair in ((1, 2), (5, 6), (0, 7)):
         for x in range(PLANES):
-            product = jnp.dot(
-                weights(weight_ref, edge_ref, slice(0, 192), x),
-                near((volume,), z, x),
-                preferred_element_type=F32,
-            )
-            for at in range(2):
-                part = product[:, 128 * at : 128 * at + 128]
-                here = inside(z + at - 2)
-                hidden, slope = gelu_pair(fold(part[0:96]))
-                tangent = slope * fold(part[96:192])
-                p_hid[z + at, tile_of(x)] = jnp.where(here, hidden, 0.0).astype(BF16)
-                p_tan[z + at, tile_of(x)] = jnp.where(here, tangent, 0.0).astype(BF16)
-                if 2 <= z + at < 6:
-                    slopes[z + at - 2, x] = slope
+            for z, (hidden, tangent, slope) in zip(
+                pair, first_layer(weight_ref, edge_ref, volume, pair, x)
+            ):
+                here = inside(z - 2)
+                p_hid[z, tile_of(x)] = jnp.where(here, hidden, 0.0).astype(BF16)
+                p_tan[z, tile_of(x)] = jnp.where(here, tangent, 0.0).astype(BF16)
+                if z in (2, 5):
+                    slopes[z - 2, x] = slope
 
     for z in range(0, 6, 2):
         for x in range(PLANES):
             product = jnp.dot(
                 weights(joint_ref, edge_joint_ref, slice(0, 96), x),
-                near((tangent_columns, hidden_columns), z, x),
+                near((tangent_columns, hidden_columns), (z, z + 1), x),
                 preferred_element_type=F32,
             )
             for at in range(2):
@@ -259,12 +283,13 @@
         for x in range(PLANES):
             product = jnp.dot(
                 weights(weight_ref, edge_ref, slice(192, 288), x),
-                near((jv_columns,), z, x),
+                near((jv_columns,), (z, z + 1), x),
                 preferred_element_type=F32,
             )
             tiles = []
             for at in range(2):
-                back = slopes[z + at, x] * fold(product[:, 128 * at : 128 * at + 128])
+                slope = slope_ref[z + at - 1, x] if z + at in (1, 2) else slopes[z + at, x]
+                back = slope * fold(product[:, 128 * at : 128 * at + 128])
                 tiles.append(back.astype(BF16).astype(F32))
             targets.append(spread(tiles))
         sums_first = sums_first + correlate(volume, z + 2, targets)
@@ -407,12 +432,22 @@
         pairs = [(device(i), device(i + 1)) for i in range(start, members * n_gz - 1, 2)]
         return pairs + [(b, a) for a, b in pairs]
 
+    middle = ((2, 256, 128), BF16)
+    ready = call(
+        inner,
+        (own, weights[0], weights[2]),
+        [middle, middle, ((2, PLANES) + small, F32)],
+        [],
+        "inner",
+        8,
+        10**9,
+    )
     first = lax.ppermute(first, AXES, swapped(0))
     second = lax.ppermute(second, AXES, swapped(1))
 
     (leaving,) = call(
         lambda *refs: layers(width * n_gz, *refs),
-        (own, first, second, *weights),
+        (own, first, second, *weights, *ready),
         [((members, 48, 128), BF16)],
         [
             ((6, 256, 128), BF16),

time: 86.8 us -> 86.6 us (level)
    pallas_call x7 -> x8, Pallas kernels: 9.76 us -> 10.1 us  [call(): pl.pallas_call(kernel, out_shape=tuple((jax.ShapeDtypeStruct(shape, dtype...]
  transfers between devices with their start and end apart: 3 -> 3, of which waited for: 3 -> 3; matrix products, arithmetic and copies ran while one was open for 0% -> 0% of each run, Pallas kernels for 3% -> 4%
where the time goes in v14:
time: 86.6 us; the launch traced here: 86.2 us
  blocking collectives  54.6 us (63%)
  Pallas kernels  12 us (14%)
  waiting for transfers between devices  11.2 us (13%)
  starting transfers between devices  6.7 us (8%)
  local copies, waits for them, and re-layouts  0.97 us (1%)
    all_to_all x1, blocking collectives, body(): parts = lax.all_to_all(sent, GROUP, 0, 0)  23.5 us
    all_to_all x1, blocking collectives, body(): parts = lax.all_to_all(leaving, GROUP, 0, 0)  17.8 us
    all_to_all x1, blocking collectives, body(): sums = lax.all_to_all(sums, 'gz', 0, 0)  13.3 us
    pallas_call x8, Pallas kernels, call(): pl.pallas_call(kernel, out_shape=tuple((jax.ShapeDtypeStruct(shape, dtype...  10.1 us
    all_to_all x1, waiting for transfers between devices, body(): every = lax.all_to_all(every, GROUP, 0, 0).reshape(512, 128)  7.69 us
    all_to_all x1, starting transfers between devices, body(): every = lax.all_to_all(every, GROUP, 0, 0).reshape(512, 128)  3.86 us
    ppermute x1, waiting for transfers between devices, body(): second = lax.ppermute(second, AXES, swapped(1))  3.25 us
    ppermute x1, starting transfers between devices, body(): second = lax.ppermute(second, AXES, swapped(1))  2.74 us
  transfers between devices with their start and end apart: 3, of which 3 were waited for; matrix products, arithmetic and copies ran while one was open for 0% of the time, Pallas kernels for 4%

profile of v14, /device:TPU:1, one launch (start us, length us, event | category | flops | bytes accessed | tf_op | source)
XLA Modules:
  0.0 86.2 jit_solution(6532768752673244419)
XLA Ops:
  0.6 0.0 copy-start.2
  0.6 0.9 %copy-done.2 = bf16[32,2,16,128]{3,2,1,0:T(8,128)(2,1)S(1)} copy-done((bf16[32,2,16,128]{3,2,1,0:T(8,128)(2,1)S(1)}, bf16[32,2,16,128]{3,2,1,0:T(8,128)(2,1)}, u32[]{:S(2)}) %copy-start.2) | copy-done | bytes 262168
  1.6 0.9 pack.1
  2.4 0.0 copy-start.1
  2.5 0.0 copy-start.3
  2.5 0.0 copy-start.4
  2.5 23.5 %all_to_all.20.parts_ref = bf16[32,32,128]{2,1,0:T(8,128)(2,1)S(1)} all-to-all(bf16[32,32,128]{2,1,0:T(8,128)(2,1)S(1)} %pack.1), channel_id=1, replica_groups=mesh['gx'=4,'gy'=8,'gz'=8] {'gx','gy'}, dimensions={0} | all-to-all | bytes 524288 | tf_op jit(solution)/shard_map/all_to_all | solution.py:403
  25.9 0.0 copy-start
  25.9 0.6 arrange.1
  26.5 0.1 collective-permute-start
  26.6 2.7 %collective-permute-start.1 = (bf16[3,256,128]{2,1,0:T(8,128)(2,1)S(1)}, bf16[3,256,128]{2,1,0:T(8,128)(2,1)S(1)}, u32[]{:S(2)}, u32[]{:S(2)}) collective-permute-start(bf16[3,256,128]{2,1,0:T(8,128)(2,1)S(1)} %get-tuple-element.23), channel_id=1, source_target_pairs={{16,24},{88,80},{72,136},{144,152},{216,208},{200,40},{48,56},{120... | collective-permute-start | bytes 589832 | tf_op jit(solution)/shard_map/ppermute | solution.py:446
  29.4 0.0 copy-done.1
  29.4 0.0 copy-done.3
  29.4 0.0 copy-done.4
  29.4 0.0 copy-done
  29.4 0.9 %filters.1 = (bf16[288,288]{1,0:T(8,128)(2,1)S(1)}, bf16[96,576]{1,0:T(8,128)(2,1)S(1)}, bf16[2,288,192]{2,1,0:T(8,128)(2,1)S(1)}, bf16[2,96,384]{2,1,0:T(8,128)(2,1)S(1)}) custom-call(bf16[27,32,32]{2,1,0:T(8,128)(2,1)S(1)} %bitcast.14, bf16[27,32,32]{2,1,0:T(8,128)(2,1)S(1)} %bitcast.11, bf16[27,32,32]{2,1,0:T(8,128)(2,1)S(1)} %bitcast.15, ...), custom_call_target="tpu_custom_call" | custom-call | flops 200000000 | bytes 1048576 | tf_op jit(solution)/shard_map/filters/pallas_call | solution.py:380
  30.3 0.6 inner.1
  30.9 0.2 collective-permute-done.refs_1_
  31.1 3.2 %collective-permute-done.1.refs_2_ = bf16[3,256,128]{2,1,0:T(8,128)(2,1)S(1)} collective-permute-done((bf16[3,256,128]{2,1,0:T(8,128)(2,1)S(1)}, bf16[3,256,128]{2,1,0:T(8,128)(2,1)S(1)}, u32[]{:S(2)}, u32[]{:S(2)}) %collective-permute-start.1) | collective-permute-done | bytes 196640 | tf_op jit(solution)/shard_map/ppermute | solution.py:446
  34.4 4.8 %layers.1 = bf16[32,48,128]{2,1,0:T(8,128)(2,1)S(1)} custom-call(bf16[4,256,128]{2,1,0:T(8,128)(2,1)S(1)} %get-tuple-element.21.own_ref.refs_0_, bf16[3,256,128]{2,1,0:T(8,128)(2,1)S(1)} %collective-permute-done.refs_1_, bf16[3,256,128]{2,1,0:T(8,128)(2,1)S(1)} %collective-permute-done.1.refs_2_, bf16[288,288]{1,0:T(8,128)(2,1)S(1)} %get-tuple-element.28.weight_ref.refs_3_, ...), custom_call_target="tpu_custom_call" | custom-call | flops 8000000000 | bytes 1048576 | tf_op jit(solution)/shard_map/layers/pallas_call | solution.py:380
  39.2 17.8 %all_to_all.21.parts_ref = bf16[32,48,128]{2,1,0:T(8,128)(2,1)S(1)} all-to-all(bf16[32,48,128]{2,1,0:T(8,128)(2,1)S(1)} %layers.1), channel_id=1, replica_groups=mesh['gx'=4,'gy'=8,'gz'=8] {'gx','gy'}, dimensions={0} | all-to-all | bytes 786432 | tf_op jit(solution)/shard_map/all_to_all | solution.py:465
  57.1 13.3 %all_to_all.22.parts_ref = f32[8,16,128]{2,1,0:T(8,128)S(1)} all-to-all(f32[8,16,128]{2,1,0:T(8,128)S(1)} %gather_sums.1), channel_id=1, replica_groups=mesh['gx'=4,'gy'=8,'gz'=8] {'gz'}, dimensions={0} | all-to-all | bytes 131072 | tf_op jit(solution)/shard_map/all_to_all | solution.py:467
  70.3 0.7 combine.1
  71.0 3.9 %all-to-all-start.3 = ((bf16[32,16,128]{2,1,0:T(8,128)(2,1)}), bf16[32,16,128]{2,1,0:T(8,128)(2,1)S(1)}, u32[]{:S(2)}, u32[]{:S(2)}) async-start(bf16[32,16,128]{2,1,0:T(8,128)(2,1)} %combine.1), calls=%async_computation.3 | async-start | bytes 262144 | tf_op jit(solution)/shard_map/all_to_all | solution.py:469
  74.9 0.1 convert_multiply_fusion
  75.0 1.7 %unpack.1 = bf16[32,2,16,128]{3,2,1,0:T(8,128)(2,1)} custom-call(bf16[32,48,128]{2,1,0:T(8,128)(2,1)S(1)} %all_to_all.21.parts_ref), custom_call_target="tpu_custom_call" | custom-call | flops 1000000000 | bytes 1048576 | tf_op jit(solution)/shard_map/unpack/pallas_call | solution.py:380
  76.7 7.7 %all-to-all-done.3 = bf16[32,16,128]{2,1,0:T(8,128)(2,1)S(1)} async-done(((bf16[32,16,128]{2,1,0:T(8,128)(2,1)}), bf16[32,16,128]{2,1,0:T(8,128)(2,1)S(1)}, u32[]{:S(2)}, u32[]{:S(2)}) %all-to-all-start.3) | async-done | bytes 131104 | tf_op jit(solution)/shard_map/all_to_all | solution.py:469
  84.4 1.9 %finish.1 = (f32[27,32,32]{2,1,0:T(8,128)}, f32[27,32,32]{2,1,0:T(8,128)}) custom-call(bf16[512,128]{1,0:T(8,128)(2,1)S(1)} %bitcast.13, f32[27,32,32]{2,1,0:T(8,128)S(1)} %bitcast.10, f32[27,32,32]{2,1,0:T(8,128)S(1)} %bitcast.9), custom_call_target="tpu_custom_call" | custom-call | tf_op jit(solution)/shard_map/finish/pallas_call | solution.py:480
  (1 shorter events, 0.0 us)
Async XLA Ops:
  0.6 1.0 %copy-start.2 = (bf16[32,2,16,128]{3,2,1,0:T(8,128)(2,1)S(1)}, bf16[32,2,16,128]{3,2,1,0:T(8,128)(2,1)}, u32[]{:S(2)}) copy-start(bf16[32,2,16,128]{3,2,1,0:T(8,128)(2,1)} %cells_ref.1) | copy-start | bytes 786436
  2.4 26.9 %copy-start.1 = (bf16[3,3,3,32,32]{4,3,2,1,0:T(8,128)(2,1)S(1)}, bf16[3,3,3,32,32]{4,3,2,1,0:T(8,128)(2,1)}, u32[]{:S(2)}) copy-start(bf16[3,3,3,32,32]{4,3,2,1,0:T(8,128)(2,1)} %param.9) | copy-start | bytes 165892
  2.5 26.9 %copy-start.3 = (bf16[3,3,3,32,32]{4,3,2,1,0:T(8,128)(2,1)S(1)}, bf16[3,3,3,32,32]{4,3,2,1,0:T(8,128)(2,1)}, u32[]{:S(2)}) copy-start(bf16[3,3,3,32,32]{4,3,2,1,0:T(8,128)(2,1)} %param.6) | copy-start | bytes 165892
  2.5 26.9 %copy-start.4 = (bf16[3,3,3,32,32]{4,3,2,1,0:T(8,128)(2,1)S(1)}, bf16[3,3,3,32,32]{4,3,2,1,0:T(8,128)(2,1)}, u32[]{:S(2)}) copy-start(bf16[3,3,3,32,32]{4,3,2,1,0:T(8,128)(2,1)} %param.7) | copy-start | bytes 165892
  25.9 3.4 %copy-start = (bf16[3,3,3,32,32]{4,3,2,1,0:T(8,128)(2,1)S(1)}, bf16[3,3,3,32,32]{4,3,2,1,0:T(8,128)(2,1)}, u32[]{:S(2)}) copy-start(bf16[3,3,3,32,32]{4,3,2,1,0:T(8,128)(2,1)} %param.8) | copy-start | bytes 165892
  26.5 4.6 %collective-permute-start = (bf16[3,256,128]{2,1,0:T(8,128)(2,1)S(1)}, bf16[3,256,128]{2,1,0:T(8,128)(2,1)S(1)}, u32[]{:S(2)}, u32[]{:S(2)}) collective-permute-start(bf16[3,256,128]{2,1,0:T(8,128)(2,1)S(1)} %get-tuple-element.22), channel_id=1, source_target_pairs={{8,16},{24,88},{80,72},{136,144},{152,216},{208,200},{40,48},{56,1... | collective-permute-start | bytes 589832 | tf_op jit(solution)/shard_map/ppermute | solution.py:445
  26.6 7.8 %collective-permute-start.1 = (bf16[3,256,128]{2,1,0:T(8,128)(2,1)S(1)}, bf16[3,256,128]{2,1,0:T(8,128)(2,1)S(1)}, u32[]{:S(2)}, u32[]{:S(2)}) collective-permute-start(bf16[3,256,128]{2,1,0:T(8,128)(2,1)S(1)} %get-tuple-element.23), channel_id=1, source_target_pairs={{16,24},{88,80},{72,136},{144,152},{216,208},{200,40},{48,56},{120... | collective-permute-start | bytes 589832 | tf_op jit(solution)/shard_map/ppermute | solution.py:446
  71.0 13.4 %all-to-all-start.3 = ((bf16[32,16,128]{2,1,0:T(8,128)(2,1)}), bf16[32,16,128]{2,1,0:T(8,128)(2,1)S(1)}, u32[]{:S(2)}, u32[]{:S(2)}) async-start(bf16[32,16,128]{2,1,0:T(8,128)(2,1)} %combine.1), calls=%async_computation.3 | async-start | bytes 262144 | tf_op jit(solution)/shard_map/all_to_all | solution.py:469
